TPU v7x, 128 devices: a whole 4x4x4 slice. The times are simulated.
128 devices in a mesh: section: 2 (over z_lo), dev: 64 (over z_hi, x, y, core).
Axes of the slice: x: 4, y: 4, z: 4 (z_hi: 2, z_lo: 2; z = z_hi * 2 + z_lo), core: 2. Of those that a mesh axis runs over, the one named last changes fastest.
Arguments:
- frames: bfloat16 [2048, 32, 1024], P(('section', 'dev')), may hold values from -6 to 6
- window_counts: int32 [2, 64], replicated, may hold values from 1 to 20, 1024 in all within a row
- learned_queries: bfloat16 [32, 1024], replicated, may hold values from -6 to 6
- frame_kv: bfloat16 [1024, 2048], replicated, may hold values from -0.1875 to 0.1875
- query_out: bfloat16 [1024, 1024], replicated, may hold values from -0.1875 to 0.1875
- query_gain: float32 [1024], replicated, may hold values from 0.25 to 1.75
- captions: bfloat16 [2, 64, 128, 2048], P('section', 'dev'), may hold values from -6 to 6
- caption_lengths: int32 [2, 64], P('section', 'dev'), may hold values from 1 to 128
- caption_gain: float32 [2048], replicated, may hold values from 0.25 to 1.75
- w_query: bfloat16 [2048, 1024], replicated, may hold values from -0.125 to 0.125
- memory_kv: bfloat16 [1024, 2048], replicated, may hold values from -0.1875 to 0.1875
- w_output: bfloat16 [1024, 2048], replicated, may hold values from -0.1875 to 0.1875
- upstream: bfloat16 [2, 64, 128, 2048], P('section', 'dev'), may hold values from -6 to 6
Outputs:
- decoded: bfloat16 [2, 64, 128, 2048], P('section', 'dev')
- caption_grad: bfloat16 [2, 64, 128, 2048], P('section', 'dev')
- memory_grad: bfloat16 [2048, 32, 1024], P(('section', 'dev'))
- kv_grad: float32 [1024, 2048], P(('section', 'dev'))
Inputs may be any that keep to these rules, and one draw needn't show every extreme that they name: `window_counts`: each row sums to 1024; in each row some video has exactly 20.
All inputs are finite; a program needn't handle non-finite values.
Results may differ from a plain program's by a relative error of at most 0.023.
Values may be sent and summed in bfloat16 or wider, within the bound.
No kernel may reach another device: no remote copies, remote signals or barrier semaphores. Data moves between devices by JAX's collectives and lax.ppermute only.
A program may use at most 192 MiB of HBM per device.

v0:
```python
import jax
import jax.numpy as jnp
from jax import lax
from jax.sharding import Mesh
from jax.sharding import PartitionSpec as P

HEADS = 16
HEAD_DIM = 64
INNER = 1024
QDIM = 1024
QHEADS = 16
QUERIES = 32
FRAMES = 32
WIN_DEV = 16
MOST_WIN = 20
CAPLEN = 128
DEV = ("dev_0", "dev_1", "dev_2", "dev_3")
SECTION_DEV = ("section", "dev_0", "dev_1", "dev_2", "dev_3")


EPSILON = 1e-06


def cut_along(array, dim, peers):
    dims = array.shape
    blocks = array.reshape(*dims[:dim], peers, dims[dim] // peers, *dims[dim + 1 :])
    return jnp.moveaxis(blocks, dim, 0)


def summed_rows(array, chips, core, dim):
    sizes = (lax.axis_size(chips), lax.axis_size(core))
    blocks = cut_along(array, dim, sizes[0] * sizes[1])
    inside = blocks.shape[1:]
    blocks = blocks.reshape(*sizes, *inside).swapaxes(0, 1).reshape(-1, *inside)
    blocks = lax.psum_scatter(blocks, core, scatter_dimension=0, tiled=True)
    return lax.psum_scatter(blocks, chips, scatter_dimension=0, tiled=True)[0]


def cut_rows(length, count):
    hop = length // count
    if hop >= 8:
        hop -= hop % 8
    return [hop * k for k in range(1, count)]


def laid_out(blocks, dim):
    dims = list(blocks.shape[1:])
    dims[dim] *= blocks.shape[0]
    return jnp.moveaxis(blocks, 0, dim).reshape(dims)


def exchange_in_pieces(array, axis, pieces, split_dim, concat_dim):
    blocks = cut_along(array, split_dim, lax.axis_size(axis))
    split_at = max(range(1, max(2, blocks.ndim - 1)), key=lambda d: blocks.shape[d])
    finished = []
    for share in jnp.split(blocks, cut_rows(blocks.shape[split_at], pieces), axis=split_at):
        if share.size:
            finished.append(lax.all_to_all(share, axis, split_axis=0, concat_axis=0, tiled=True))
    return laid_out(jnp.concatenate(finished, axis=split_at), concat_dim)


def rms_scale(values, gain):
    return values * lax.rsqrt(jnp.mean(values * values, axis=-1, keepdims=True) + EPSILON) * gain


def compress_block(frames_block, learned_queries, frame_kv, query_out, query_gain):
    blocks = frames_block.shape[0]
    flat_frames = frames_block.reshape(blocks * FRAMES, QDIM)
    key_value = jnp.dot(flat_frames, frame_kv, preferred_element_type=jnp.float32).astype(
        jnp.bfloat16
    )
    key_heads = key_value[:, :QDIM].reshape(blocks, FRAMES, QHEADS, HEAD_DIM)
    value_heads = key_value[:, QDIM:].reshape(blocks, FRAMES, QHEADS, HEAD_DIM)
    query_heads = learned_queries.reshape(QUERIES, QHEADS, HEAD_DIM)
    scores = jnp.einsum(
        "qhe,nfhe->nhqf", query_heads, key_heads, preferred_element_type=jnp.float32
    ) * HEAD_DIM ** (-0.5)
    attention = jax.nn.softmax(scores, axis=-1).astype(jnp.bfloat16)
    context = jnp.einsum(
        "nhqf,nfhe->nqhe", attention, value_heads, preferred_element_type=jnp.float32
    ).astype(jnp.bfloat16)
    projected = jnp.dot(
        context.reshape(blocks * QUERIES, QDIM), query_out, preferred_element_type=jnp.float32
    )
    hidden = learned_queries.astype(jnp.float32)[None] + projected.reshape(blocks, QUERIES, QDIM)
    return rms_scale(hidden, query_gain).astype(jnp.bfloat16)


def attend(
    tokens, length, upstream, key_heads, value_heads, key_live, caption_gain, w_query, w_output
):
    source = tokens.astype(jnp.float32)
    inv_rms = lax.rsqrt(jnp.mean(source * source, axis=-1, keepdims=True) + EPSILON)
    normed = (source * inv_rms * caption_gain).astype(jnp.bfloat16)
    query_heads = (
        jnp.dot(normed, w_query, preferred_element_type=jnp.float32)
        .astype(jnp.bfloat16)
        .reshape(CAPLEN, HEADS, HEAD_DIM)
    )
    scores = jnp.einsum(
        "lhe,mhe->hlm", query_heads, key_heads, preferred_element_type=jnp.float32
    ) * HEAD_DIM ** (-0.5)
    scores = jnp.where(key_live[None, None, :], scores, jnp.float32(-1e30))
    attention = jax.nn.softmax(scores, axis=-1)
    weights = attention.astype(jnp.bfloat16)
    context = (
        jnp.einsum("hlm,mhe->lhe", weights, value_heads, preferred_element_type=jnp.float32)
        .astype(jnp.bfloat16)
        .reshape(CAPLEN, INNER)
    )
    decoded = (source + jnp.dot(context, w_output, preferred_element_type=jnp.float32)).astype(
        jnp.bfloat16
    )
    row_live = jnp.arange(CAPLEN, dtype=jnp.int32) < length
    grad_out = jnp.where(row_live[:, None], upstream, jnp.zeros_like(upstream))
    d_context = (
        jnp.dot(grad_out, w_output.T, preferred_element_type=jnp.float32)
        .astype(jnp.bfloat16)
        .reshape(CAPLEN, HEADS, HEAD_DIM)
    )
    d_probs = jnp.einsum("lhe,mhe->hlm", d_context, value_heads, preferred_element_type=jnp.float32)
    d_scores = (
        attention
        * (d_probs - jnp.sum(d_probs * attention, axis=-1, keepdims=True))
        * HEAD_DIM ** (-0.5)
    ).astype(jnp.bfloat16)
    d_query = (
        jnp.einsum("hlm,mhe->lhe", d_scores, key_heads, preferred_element_type=jnp.float32)
        .astype(jnp.bfloat16)
        .reshape(CAPLEN, INNER)
    )
    d_keys = jnp.einsum("hlm,lhe->mhe", d_scores, query_heads, preferred_element_type=jnp.float32)
    d_values = jnp.einsum("hlm,lhe->mhe", weights, d_context, preferred_element_type=jnp.float32)
    rows_total = key_heads.shape[0]
    d_pair = jnp.concatenate(
        [d_keys.reshape(rows_total, INNER), d_values.reshape(rows_total, INNER)], axis=1
    ).astype(jnp.bfloat16)
    d_scaled = jnp.dot(d_query, w_query.T, preferred_element_type=jnp.float32) * caption_gain
    caption_grad = grad_out.astype(jnp.float32) + inv_rms * (
        d_scaled - source * inv_rms * inv_rms * jnp.mean(d_scaled * source, axis=-1, keepdims=True)
    )
    return (decoded, caption_grad.astype(jnp.bfloat16), d_pair)


def local(
    frames,
    window_counts,
    learned_queries,
    frame_kv,
    query_out,
    query_gain,
    captions,
    caption_lengths,
    caption_gain,
    w_query,
    memory_kv,
    w_output,
    upstream,
):
    videos = lax.axis_size(DEV)
    per_slot = (MOST_WIN + videos - 2) // (videos - 1)
    section_id = lax.axis_index("section")
    video_id = lax.axis_index(DEV)
    counts_row = lax.dynamic_index_in_dim(window_counts, section_id, 0, keepdims=False)
    run_ends = jnp.cumsum(counts_row)
    starts = run_ends - counts_row
    local_index = jnp.arange(WIN_DEV, dtype=jnp.int32)
    ranked = (
        local_index // per_slot * (per_slot * videos) + video_id * per_slot + local_index % per_slot
    )
    owner_video = jnp.sum((run_ends[None, :] <= ranked[:, None]).astype(jnp.int32), axis=1)
    target = owner_video * per_slot + local_index % per_slot
    slot_index = jnp.arange(videos * per_slot, dtype=jnp.int32)
    send_map = (slot_index[:, None] == target[None, :]).astype(jnp.bfloat16)
    count_here = lax.dynamic_index_in_dim(counts_row, video_id, 0, keepdims=False)
    start_here = lax.dynamic_index_in_dim(starts, video_id, 0, keepdims=False)
    position = jnp.arange(MOST_WIN, dtype=jnp.int32)
    incoming = start_here + position
    source_slot = incoming // per_slot % videos * per_slot + incoming % per_slot
    present = position < count_here
    take_map = ((slot_index[None, :] == source_slot[:, None]) & present[:, None]).astype(
        jnp.bfloat16
    )
    packed = jnp.dot(
        send_map, frames.reshape(WIN_DEV, FRAMES * QDIM), preferred_element_type=jnp.float32
    ).astype(jnp.bfloat16)
    arrived = lax.all_to_all(
        packed.reshape(videos, per_slot, FRAMES, QDIM), DEV, split_axis=0, concat_axis=0, tiled=True
    )
    frames_here = jnp.dot(
        take_map,
        arrived.reshape(videos * per_slot, FRAMES * QDIM),
        preferred_element_type=jnp.float32,
    ).astype(jnp.bfloat16)
    compressed = compress_block(
        frames_here.reshape(MOST_WIN, FRAMES, QDIM),
        learned_queries,
        frame_kv,
        query_out,
        query_gain,
    )
    memory_half = jnp.where(present[:, None, None], compressed, jnp.zeros_like(compressed)).reshape(
        MOST_WIN * QUERIES, QDIM
    )
    key_value = jnp.dot(
        lax.all_gather(memory_half, "section", axis=0, tiled=True),
        memory_kv,
        preferred_element_type=jnp.float32,
    ).astype(jnp.bfloat16)
    key_heads = key_value[:, :INNER].reshape(-1, HEADS, HEAD_DIM)
    value_heads = key_value[:, INNER:].reshape(-1, HEADS, HEAD_DIM)
    counts_col = lax.dynamic_index_in_dim(window_counts, video_id, 1, keepdims=False)
    token_pos = jnp.arange(MOST_WIN * QUERIES, dtype=jnp.int32) // QUERIES
    key_live = (token_pos[None, :] < counts_col[:, None]).reshape(-1)
    decoded, caption_grad, d_pair = attend(
        captions[0, 0],
        caption_lengths[0, 0],
        upstream[0, 0],
        key_heads,
        value_heads,
        key_live,
        caption_gain,
        w_query,
        w_output,
    )
    d_sum = (
        lax.psum_scatter(d_pair, "section", scatter_dimension=0, tiled=True)
        .astype(jnp.float32)
        .astype(jnp.bfloat16)
    )
    d_memory = jnp.dot(d_sum, memory_kv.T, preferred_element_type=jnp.float32).astype(jnp.bfloat16)
    kv_grad = summed_rows(
        jnp.dot(memory_half.T, d_sum, preferred_element_type=jnp.float32).astype(jnp.bfloat16),
        ("section", "dev_0", "dev_1", "dev_2"),
        "dev_3",
        0,
    ).astype(jnp.float32)
    grad_slots = jnp.dot(
        take_map.T, d_memory.reshape(MOST_WIN, QUERIES * QDIM), preferred_element_type=jnp.float32
    ).astype(jnp.bfloat16)
    returned = exchange_in_pieces(grad_slots.reshape(videos, per_slot, QUERIES, QDIM), DEV, 2, 0, 0)
    memory_grad = jnp.dot(
        send_map.T,
        returned.reshape(videos * per_slot, QUERIES * QDIM),
        preferred_element_type=jnp.float32,
    ).astype(jnp.bfloat16)
    return (
        decoded[None, None],
        caption_grad[None, None],
        memory_grad.reshape(WIN_DEV, QUERIES, QDIM),
        kv_grad,
    )


def solution(mesh):
    finer = Mesh(
        mesh.devices.reshape(mesh.shape["section"], 2, 4, 4, 2),
        ("section", "dev_0", "dev_1", "dev_2", "dev_3"),
    )
    placed = (
        P(SECTION_DEV, None, None),
        P(),
        P(),
        P(),
        P(),
        P(),
        P("section", DEV, None, None),
        P("section", DEV),
        P(),
        P(),
        P(),
        P(),
        P("section", DEV, None, None),
    )
    return jax.shard_map(
        local,
        mesh=finer,
        in_specs=placed,
        out_specs=(
            P("section", DEV, None, None),
            P("section", DEV, None, None),
            P(SECTION_DEV, None, None),
            P(SECTION_DEV, None),
        ),
        check_vma=False,
    )
```

profile of v0, /device:TPU:64, one launch (start us, length us, event | category | flops | bytes accessed | tf_op | source)
XLA Modules:
  0.0 741.8 jit_solution(17250548522140290213)
XLA Ops:
  11.6 4.4 copy.78
  16.0 10.9 %all-to-all-start = ((bf16[64,1,32,1024]{3,2,1,0:T(8,128)(2,1)}), bf16[64,1,32,1024]{3,2,1,0:T(8,128)(2,1)}, u32[]{:S(2)}, u32[]{:S(2)}) async-start(bf16[64,1,32,1024]{3,2,1,0:T(8,128)(2,1)} %bitcast.123), calls=%async_computation | async-start | bytes 8388608 | tf_op jit(solution)/shard_map/all_to_all | solution.py:187
  30.3 49.5 %all-to-all-done = bf16[64,1,32,1024]{3,2,1,0:T(8,128)(2,1)} async-done(((bf16[64,1,32,1024]{3,2,1,0:T(8,128)(2,1)}), bf16[64,1,32,1024]{3,2,1,0:T(8,128)(2,1)}, u32[]{:S(2)}, u32[]{:S(2)}) %all-to-all-start) | async-done | bytes 4194336 | tf_op jit(solution)/shard_map/all_to_all | solution.py:187
  79.8 4.6 copy.79
  86.4 3.2 reshape_reshape.12
  89.6 5.3 convolution_convert_fusion.7
  96.2 4.4 reshape.194
  105.9 11.8 %fusion.91 = (f32[20,16,32]{2,0,1:T(8,128)S(1)}, f32[20,16,32,32]{2,3,0,1:T(8,128)S(1)}) fusion(f32[16,20,32,32]{3,2,1,0:T(8,128)S(1)} %fusion.27), kind=kOutput, calls=%fused_computation.120 | output fusion | flops 1310751 | bytes 2662400 | tf_op jit(solution)/shard_map/sub | solution.py:78
  121.9 3.7 dot_general.70
  130.0 2.9 convolution_convert_fusion.10
  133.1 3.7 convolution_convert_fusion.9
  137.0 36.9 %all-gather.2.cloned.1.call-done = bf16[1280,1024]{1,0:T(8,128)(2,1)} async-done(((bf16[640,1024]{1,0:T(8,128)(2,1)}), bf16[1280,1024]{1,0:T(8,128)(2,1)}) %all-gather.2.cloned.1.call-update) | async-done | bytes 2621456 | tf_op jit(solution)/shard_map/all_gather | solution.py:206
  174.0 8.5 %convolution_convert_fusion.4 = bf16[1280,2048]{1,0:T(8,128)(2,1)S(1)} fusion(bf16[1280,1024]{1,0:T(8,128)(2,1)} %all-gather.2.cloned.1.call-done, bf16[1024,2048]{1,0:T(8,128)(2,1)} %param.23), kind=kOutput, calls=%fused_computation.13 | convolution fusion | flops 5371330560 | bytes 12058624 | tf_op jit(solution)/shard_map/dot_general | solution.py:205
  185.4 4.4 copy.65
  189.9 4.4 copy.63
  194.2 7.2 fusion.93
  201.5 8.8 %fusion.92 = (f32[16,128]{1,0:T(8,128)S(1)}, f32[16,128,1280]{2,1,0:T(8,128)}) fusion(pred[1280]{0:T(1024)(128)(4,1)S(1)} %lt.80, bf16[128,16,64]{0,2,1:T(8,128)(2,1)S(1)} %bitcast.148, bf16[1280,16,64]{0,2,1:T(8,128)(2,1)} %bitcast.140), kind=kOutput, calls=%fused_computation.121 | convolution fusion | flops 346031360 | bytes 13378816 | tf_op jit(solution)/shard_map/sub | solution.py:104
  210.3 6.4 convolution_convert_fusion.6
  216.7 25.8 %fusion.19 = bf16[16,64,1280]{2,1,0:T(8,128)(2,1)} fusion(bf16[128,16,64]{0,2,1:T(8,128)(2,1)S(1)} %bitcast.149, f32[16,128,1280]{2,1,0:T(8,128)} %fusion.93, f32[16,128,1280]{2,1,0:T(8,128)} %get-tuple-element.15, f32[16,128]{1,0:T(8,128)S(1)} %get-tuple-element.14), kind=kOutput, calls=%fused_computation.28 | convolution fusion | flops 355208448 | bytes 23863296 | tf_op jit(solution)/shard_map/hlm,lhe->mhe/dot_general | solution.py:132
  242.5 5.2 pad_maximum_fusion
  247.8 8.0 %copy.75 = bf16[1280,2048]{1,0:T(8,128)(2,1)} copy(bf16[1280,2048]{0,1:T(8,128)(2,1)} %pad_maximum_fusion) | data formatting | bytes 10485760
  255.8 69.4 %reduce-scatter.10.cloned.1.call-done = bf16[640,2048]{1,0:T(8,128)(2,1)} async-done(((bf16[1280,2048]{1,0:T(8,128)(2,1)}), bf16[640,2048]{1,0:T(8,128)(2,1)}) %reduce-scatter.10.cloned.1.call-update) | async-done | bytes 2621456
  325.2 5.6 convolution_convert_fusion.5
  333.2 7.0 convolution_convert_fusion.8
  348.9 10.5 %all-to-all-start.1 = ((bf16[64,1,1,16,1024]{4,3,2,1,0:T(8,128)(2,1)}), bf16[64,1,1,16,1024]{4,3,2,1,0:T(8,128)(2,1)}, u32[]{:S(2)}, u32[]{:S(2)}) async-start(bf16[64,1,1,16,1024]{4,3,2,1,0:T(8,128)(2,1)} %get-tuple-element.6), calls=%async_computation.1 | async-start | bytes 4194304 | tf_op jit(solution)/shard_map/all_to_all | solution.py:58
  360.0 25.0 %fusion.49 = bf16[16,64,128]{2,1,0:T(8,128)(2,1)S(1)} fusion(bf16[1280,16,64]{0,2,1:T(8,128)(2,1)} %bitcast.141, f32[16,128,1280]{2,1,0:T(8,128)} %fusion.93, f32[16,128,1280]{2,1,0:T(8,128)} %get-tuple-element.15, f32[16,128]{1,0:T(8,128)S(1)} %get-tuple-element.14), kind=kOutput, calls=%fused_computation.59 | convolution fusion | flops 354028800 | bytes 23863296 | tf_op jit(solution)/shard_map/hlm,mhe->lhe/dot_general | solution.py:128
  385.0 3.8 fusion.59
  388.9 10.6 %all-to-all-start.2 = ((bf16[64,1,1,16,1024]{4,3,2,1,0:T(8,128)(2,1)}), bf16[64,1,1,16,1024]{4,3,2,1,0:T(8,128)(2,1)}, u32[]{:S(2)}, u32[]{:S(2)}) async-start(bf16[64,1,1,16,1024]{4,3,2,1,0:T(8,128)(2,1)} %get-tuple-element.7), calls=%async_computation.2 | async-start | bytes 4194304 | tf_op jit(solution)/shard_map/all_to_all | solution.py:58
  399.5 6.9 fusion.46
  409.2 19.0 %all-to-all-done.2 = bf16[64,1,1,16,1024]{4,3,2,1,0:T(8,128)(2,1)} async-done(((bf16[64,1,1,16,1024]{4,3,2,1,0:T(8,128)(2,1)}), bf16[64,1,1,16,1024]{4,3,2,1,0:T(8,128)(2,1)}, u32[]{:S(2)}, u32[]{:S(2)}) %all-to-all-start.2) | async-done | bytes 2097184 | tf_op jit(solution)/shard_map/all_to_all | solution.py:58
  428.1 3.0 pad_maximum_fusion.1
  435.9 297.4 %reduce-scatter.8.cloned.1.call-done = bf16[1,8,2048]{2,1,0:T(8,128)(2,1)} async-done(((bf16[64,8,2048]{2,1,0:T(8,128)(2,1)}), bf16[1,8,2048]{2,1,0:T(8,128)(2,1)}) %reduce-scatter.8.cloned.1.call-update) | async-done | bytes 32784 | tf_op jit(solution)/shard_map/reduce_scatter | solution.py:36
  (84 shorter events, 47.9 us)
Async XLA Ops:
  7.2 118.4 %copy-start = (bf16[1024,1024]{1,0:T(8,128)(2,1)S(1)}, bf16[1024,1024]{1,0:T(8,128)(2,1)}, u32[]{:S(2)}) copy-start(bf16[1024,1024]{1,0:T(8,128)(2,1)} %param.17) | copy-start | bytes 6291460
  10.3 1.2 copy-start.12
  16.0 10.9 %copy-start.8 = (bf16[32,1024]{1,0:T(8,128)(2,1)S(1)}, bf16[32,1024]{1,0:T(8,128)(2,1)}, u32[]{:S(2)}) copy-start(bf16[32,1024]{1,0:T(8,128)(2,1)} %param.15) | copy-start | bytes 196612
  16.0 11.8 %copy-start.10 = (s32[2,64]{1,0:T(2,128)S(1)}, s32[2,64]{1,0:T(2,128)}, u32[]{:S(2)}) copy-start(s32[2,64]{1,0:T(2,128)} %param.14) | copy-start | bytes 1540
  16.0 63.8 %all-to-all-start = ((bf16[64,1,32,1024]{3,2,1,0:T(8,128)(2,1)}), bf16[64,1,32,1024]{3,2,1,0:T(8,128)(2,1)}, u32[]{:S(2)}, u32[]{:S(2)}) async-start(bf16[64,1,32,1024]{3,2,1,0:T(8,128)(2,1)} %bitcast.123), calls=%async_computation | async-start | bytes 8388608 | tf_op jit(solution)/shard_map/all_to_all | solution.py:187
  26.9 147.1 %all-gather.2.cloned.1.call-start = ((), (), s32[]{:S(2)}) async-start(), calls=%async_computation.6 | async-start | bytes 3932160 | tf_op jit(solution)/shard_map/all_gather | solution.py:206
  105.9 11.8 %copy-start.5 = (bf16[20,32,16,64]{3,2,1,0:T(8,128)(2,1)S(1)}, bf16[20,32,16,64]{3,2,1,0:T(8,128)(2,1)}, u32[]{:S(2)}) copy-start(bf16[20,32,16,64]{3,2,1,0:T(8,128)(2,1)} %reshape.194) | copy-start | bytes 3932164
  119.2 6.4 copy-start.7
  125.6 1.7 copy-start.11
  127.2 2.6 copy-start.3
  127.2 2.8 copy-start.9
  128.8 4.4 copy-start.6
  128.8 196.5 %reduce-scatter.10.cloned.1.call-start = ((), (), s32[]{:S(2)}) async-start(), calls=%async_computation.9 | async-start | bytes 7864320
  255.7 69.5 %copy-start.4 = (bf16[20,32,1024]{2,1,0:T(8,128)(2,1)S(1)}, bf16[20,32,1024]{2,1,0:T(8,128)(2,1)}, u32[]{:S(2)}) copy-start(bf16[20,32,1024]{2,1,0:T(8,128)(2,1)} %fusion.43) | copy-start | bytes 3932164
  255.8 103.7 %reduce-scatter.6.cloned.1.call-start = ((), (), s32[]{:S(2)}) async-start(), calls=%async_computation.7 | async-start | bytes 6291456 | tf_op jit(solution)/shard_map/reduce_scatter | solution.py:35
  348.9 39.9 %all-to-all-start.1 = ((bf16[64,1,1,16,1024]{4,3,2,1,0:T(8,128)(2,1)}), bf16[64,1,1,16,1024]{4,3,2,1,0:T(8,128)(2,1)}, u32[]{:S(2)}, u32[]{:S(2)}) async-start(bf16[64,1,1,16,1024]{4,3,2,1,0:T(8,128)(2,1)} %get-tuple-element.6), calls=%async_computation.1 | async-start | bytes 4194304 | tf_op jit(solution)/shard_map/all_to_all | solution.py:58
  359.4 374.0 %reduce-scatter.8.cloned.1.call-start = ((), (), s32[]{:S(2)}) async-start(), calls=%async_computation.8 | async-start | bytes 2129920 | tf_op jit(solution)/shard_map/reduce_scatter | solution.py:36
  388.9 39.3 %all-to-all-start.2 = ((bf16[64,1,1,16,1024]{4,3,2,1,0:T(8,128)(2,1)}), bf16[64,1,1,16,1024]{4,3,2,1,0:T(8,128)(2,1)}, u32[]{:S(2)}, u32[]{:S(2)}) async-start(bf16[64,1,1,16,1024]{4,3,2,1,0:T(8,128)(2,1)} %get-tuple-element.7), calls=%async_computation.2 | async-start | bytes 4194304 | tf_op jit(solution)/shard_map/all_to_all | solution.py:58
  399.5 7.0 copy-start.2
  431.2 2.5 copy-start.13
  431.2 303.6 %copy-start.1 = (bf16[1024,1024]{1,0:T(8,128)(2,1)S(1)}, bf16[1024,1024]{1,0:T(8,128)(2,1)}, u32[]{:S(2)}) copy-start(bf16[1024,1024]{1,0:T(8,128)(2,1)} %param.17) | copy-start | bytes 6291460
Sparse Core Ops, SparseCore 0:
  128.9 45.0 all-gather.1
  255.9 69.3 reduce-scatter.9
  333.3 16.1 reduce-scatter.5
  362.3 371.0 reduce-scatter.7
where the time goes:
time: 750 us; the launch traced here: 742 us
  waiting for transfers between devices  473 us (63%)
  matrix products  130 us (17%)
  local copies, waits for them, and re-layouts  65.1 us (9%)
  starting transfers between devices  32.2 us (4%)
  other arithmetic  26.8 us (4%)
  between operations  15.3 us (2%)
    reduce_scatter x1, waiting for transfers between devices, summed_rows(): return lax.psum_scatter(blocks, chips, scatter_dimension=0, tiled=True)[0]  297 us
    unnamed x5, waiting for transfers between devices  70 us
    all_to_all x1, waiting for transfers between devices, local(): lax.all_to_all(packed.reshape(videos, per_slot, FRAMES, QDIM), DEV, split...  49.5 us
    all_gather x1, waiting for transfers between devices, local(): lax.all_gather(memory_half, 'section', axis=0, tiled=True)  36.9 us
    dot_general x1, matrix products, attend(): jnp.einsum('hlm,lhe->mhe', d_scores, query_heads, preferred_element_type=...  25.8 us
    unnamed x35, local copies, waits for them, and re-layouts  25.4 us
    dot_general x1, matrix products, attend(): jnp.einsum('hlm,mhe->lhe', d_scores, key_heads, preferred_element_type=jn...  25 us
    all_to_all x2, starting transfers between devices, exchange_in_pieces(): lax.all_to_all(share, axis, split_axis=0, concat_axis=0, tiled=True)  21.1 us
  transfers between devices with their start and end apart: 7, of which 5 were waited for; matrix products, arithmetic and copies ran while one was open for 10% of the time, Pallas kernels for 0%

commit v1 on v0

v1 whole, which is shorter than its diff:
```python
import jax
import jax.numpy as jnp
from jax import lax
from jax.experimental import pallas as pl
from jax.experimental.pallas import tpu as pltpu
from jax.sharding import Mesh
from jax.sharding import PartitionSpec as P

HEADS = 16
HEAD_DIM = 64
INNER = 1024
QDIM = 1024
QHEADS = 16
QUERIES = 32
FRAMES = 32
WIN_DEV = 16
MOST_WIN = 20
CAPLEN = 128
PAIRS = HEADS // 2
ROWS = MOST_WIN * QUERIES
DEV = ("dev_0", "dev_1", "dev_2", "dev_3")
CHIP = ("dev_0", "dev_1", "dev_2")
CORE = "dev_3"
SECTION_DEV = ("section", "dev_0", "dev_1", "dev_2", "dev_3")
SWAP = [(0, 1), (1, 0)]

EPSILON = 1e-06
DEAD = -1e30


def rms_scale(values, gain):
    return values * lax.rsqrt(jnp.mean(values * values, axis=-1, keepdims=True) + EPSILON) * gain


def compress_block(frames_block, learned_queries, frame_kv, query_out, query_gain):
    blocks = frames_block.shape[0]
    flat_frames = frames_block.reshape(blocks * FRAMES, QDIM)
    key_value = jnp.dot(flat_frames, frame_kv, preferred_element_type=jnp.float32).astype(
        jnp.bfloat16
    )
    key_heads = key_value[:, :QDIM].reshape(blocks, FRAMES, QHEADS, HEAD_DIM)
    value_heads = key_value[:, QDIM:].reshape(blocks, FRAMES, QHEADS, HEAD_DIM)
    query_heads = learned_queries.reshape(QUERIES, QHEADS, HEAD_DIM)
    scores = jnp.einsum(
        "qhe,nfhe->nhqf", query_heads, key_heads, preferred_element_type=jnp.float32
    ) * HEAD_DIM ** (-0.5)
    attention = jax.nn.softmax(scores, axis=-1).astype(jnp.bfloat16)
    context = jnp.einsum(
        "nhqf,nfhe->nqhe", attention, value_heads, preferred_element_type=jnp.float32
    ).astype(jnp.bfloat16)
    projected = jnp.dot(
        context.reshape(blocks * QUERIES, QDIM), query_out, preferred_element_type=jnp.float32
    )
    hidden = learned_queries.astype(jnp.float32)[None] + projected.reshape(blocks, QUERIES, QDIM)
    return rms_scale(hidden, query_gain).astype(jnp.bfloat16)


def gather_windows(index, sources, zero_fill):
    count = index.shape[0]
    limits = []
    for source in sources:
        limits.append((limits[-1] if limits else 0) + source.shape[0])

    def kernel(index_ref, *refs):
        source_refs, out_ref, sems = refs[: len(sources)], refs[-2], refs[-1]

        def each(i, act):
            which = index_ref[i]
            low = 0
            for source_ref, high in zip(source_refs, limits):

                @pl.when((which >= low) & (which < high))
                def _():
                    act(pltpu.make_async_copy(source_ref.at[which - low], out_ref.at[i], sems.at[i]))

                low = high

        @pl.loop(0, count)
        def _(i):
            each(i, lambda copy: copy.start())
            if zero_fill:

                @pl.when(index_ref[i] < 0)
                def _():
                    out_ref[i] = jnp.zeros(out_ref.shape[1:], out_ref.dtype)

        @pl.loop(0, count)
        def _(i):
            each(i, lambda copy: copy.wait())

    inner = sources[0].shape[1:]
    size = count * inner[0] * inner[1] * 2
    return pl.pallas_call(
        kernel,
        out_shape=jax.ShapeDtypeStruct((count, *inner), sources[0].dtype),
        in_specs=[pl.BlockSpec(memory_space=pltpu.SMEM)]
        + [pl.BlockSpec(memory_space=pl.ANY)] * len(sources),
        out_specs=pl.BlockSpec(memory_space=pltpu.VMEM),
        scratch_shapes=[pltpu.SemaphoreType.DMA((count,))],
        cost_estimate=pl.CostEstimate(flops=2 * 10**9, bytes_accessed=2 * size, transcendentals=0),
        name="gather_windows",
    )(index, *sources)


NT = (((1,), (1,)), ((), ()))
TN = (((0,), (0,)), ((), ()))
NN = (((1,), (0,)), ((), ()))


def stacked(own_ref, other_ref):
    both = jnp.concatenate([own_ref[...], other_ref[...]], axis=0)
    lane = lax.broadcasted_iota(jnp.int32, both.shape, 1)
    zero = jnp.zeros_like(both)
    return jnp.concatenate(
        [jnp.where(lane < HEAD_DIM, both, zero), jnp.where(lane < HEAD_DIM, zero, both)], axis=0
    )


def dot(a, b, dims):
    return lax.dot_general(a, b, dims, preferred_element_type=jnp.float32)


def masked_scores(keys, queries, live):
    scores = dot(keys, queries, NT)
    row = lax.broadcasted_iota(jnp.int32, scores.shape, 0)
    return jnp.where(row < live, scores, DEAD)


def stats_kernel(live_ref, q_own, q_other, dc_own, dc_other, kv_ref, stats_ref):
    pair = pl.program_id(0)
    keys, values = kv_ref[:, :128], kv_ref[:, 128:]
    scores = masked_scores(keys, stacked(q_own, q_other), live_ref[0])
    top = jnp.max(scores, axis=0, keepdims=True)
    grown = jnp.exp(scores - top)
    d_probs = dot(values, stacked(dc_own, dc_other), NT)
    stats_ref[0, pl.ds(pair, 1), :] = top
    stats_ref[1, pl.ds(pair, 1), :] = jnp.sum(grown, axis=0, keepdims=True)
    stats_ref[2, pl.ds(pair, 1), :] = jnp.sum(grown * d_probs, axis=0, keepdims=True)


def heads_apart(product):
    both = 2 * CAPLEN
    rows = jnp.concatenate([product[:HEAD_DIM, :both], product[HEAD_DIM:, both:]], axis=0)
    return rows.T


def grads_kernel(
    live_ref,
    q_own,
    q_other,
    dc_own,
    dc_other,
    kv_ref,
    stats_ref,
    peer_ref,
    context_own,
    context_other,
    dq_own,
    dq_other,
    dkv_ref,
):
    pair = pl.program_id(0)
    keys, values = kv_ref[:, :128], kv_ref[:, 128:]

    def mine(which):
        return stats_ref[which, pl.ds(pair, 1), :]

    def theirs(which):
        line = peer_ref[which, pl.ds(pair, 1), :]
        parts = [line[:, 128 * k : 128 * (k + 1)] for k in (1, 0, 3, 2)]
        return jnp.concatenate(parts, axis=1)

    top_mine, top_theirs = mine(0), theirs(0)
    top = jnp.maximum(top_mine, top_theirs)
    grow_mine, grow_theirs = jnp.exp(top_mine - top), jnp.exp(top_theirs - top)
    inverse = 1.0 / (mine(1) * grow_mine + theirs(1) * grow_theirs)
    delta = (mine(2) * grow_mine + theirs(2) * grow_theirs) * inverse

    queries, d_context = stacked(q_own, q_other), stacked(dc_own, dc_other)
    scores = masked_scores(keys, queries, live_ref[0])
    probs = jnp.exp(scores - top) * inverse
    weights = probs.astype(jnp.bfloat16)
    d_probs = dot(values, d_context, NT)
    d_scores = (probs * (d_probs - delta)).astype(jnp.bfloat16)
    dkv_ref[:, :128] = dot(d_scores, queries, NN).astype(jnp.bfloat16)
    dkv_ref[:, 128:] = dot(weights, d_context, NN).astype(jnp.bfloat16)
    context = heads_apart(dot(values, weights, TN))
    context_own[...] = context[:CAPLEN]
    context_other[...] = context[CAPLEN:].astype(jnp.bfloat16)
    d_query = heads_apart(dot(keys, d_scores, TN)) * HEAD_DIM ** (-0.5)
    dq_own[...] = d_query[:CAPLEN]
    dq_other[...] = d_query[CAPLEN:].astype(jnp.bfloat16)


def attention_specs():
    tokens = pl.BlockSpec((CAPLEN, 128), lambda i: (0, i))
    return tokens, [
        pl.BlockSpec(memory_space=pltpu.SMEM),
        tokens,
        tokens,
        tokens,
        tokens,
        pl.BlockSpec((ROWS, 256), lambda i: (0, i)),
    ]


def attention_stats(live, q_own, q_other, dc_own, dc_other, key_value):
    _, in_specs = attention_specs()
    return pl.pallas_call(
        stats_kernel,
        grid=(PAIRS,),
        out_shape=jax.ShapeDtypeStruct((3, PAIRS, 4 * CAPLEN), jnp.float32),
        in_specs=in_specs,
        out_specs=pl.BlockSpec((3, PAIRS, 4 * CAPLEN), lambda i: (0, 0, 0)),
        cost_estimate=pl.CostEstimate(
            flops=5 * 10**9, bytes_accessed=4 * 10**6, transcendentals=3 * 10**6
        ),
        name="attention_stats",
    )(live, q_own, q_other, dc_own, dc_other, key_value)


def attention_grads(live, q_own, q_other, dc_own, dc_other, key_value, stats, peer):
    tokens, in_specs = attention_specs()
    whole = pl.BlockSpec((3, PAIRS, 4 * CAPLEN), lambda i: (0, 0, 0))
    wide = jax.ShapeDtypeStruct((CAPLEN, INNER), jnp.float32)
    narrow = jax.ShapeDtypeStruct((CAPLEN, INNER), jnp.bfloat16)
    return pl.pallas_call(
        grads_kernel,
        grid=(PAIRS,),
        out_shape=(
            wide,
            narrow,
            wide,
            narrow,
            jax.ShapeDtypeStruct((ROWS, 2 * INNER), jnp.bfloat16),
        ),
        in_specs=in_specs + [whole, whole],
        out_specs=(tokens, tokens, tokens, tokens, pl.BlockSpec((ROWS, 256), lambda i: (0, i))),
        cost_estimate=pl.CostEstimate(
            flops=12 * 10**9, bytes_accessed=10**7, transcendentals=3 * 10**6
        ),
        name="attention_grads",
    )(live, q_own, q_other, dc_own, dc_other, key_value, stats, peer)


def local(
    frames,
    window_counts,
    learned_queries,
    frame_kv,
    query_out,
    query_gain,
    captions,
    caption_lengths,
    caption_gain,
    w_query,
    memory_kv,
    w_output,
    upstream,
):
    videos = lax.axis_size(DEV)
    chips = videos // 2
    section_id = lax.axis_index("section")
    video_id = lax.axis_index(DEV)
    core = lax.axis_index(CORE)
    sibling = video_id + 1 - 2 * core
    counts = lax.dynamic_index_in_dim(window_counts, section_id, 0, keepdims=False)
    video = jnp.arange(videos, dtype=jnp.int32)
    ends = jnp.sum(jnp.where(video[None, :] <= video[:, None], counts[None, :], 0), axis=1)
    ranked = jnp.arange(WIN_DEV, dtype=jnp.int32) * videos + video_id
    owner_chip = jnp.sum((ends[None, :] <= ranked[:, None]).astype(jnp.int32), axis=1) // 2
    chip_slot = jnp.arange(chips, dtype=jnp.int32)
    hit = chip_slot[:, None] == owner_chip[None, :]
    window = jnp.arange(WIN_DEV, dtype=jnp.int32)
    send_index = jnp.sum(jnp.where(hit, window[None, :] + 1, 0), axis=1) - 1

    def span(which):
        count = jnp.sum(jnp.where(video == which, counts, 0))
        return count, jnp.sum(jnp.where(video < which, counts, 0))

    count_here, start_here = span(video_id)
    count_near, start_near = span(sibling)
    position = jnp.arange(MOST_WIN, dtype=jnp.int32)
    rank = start_here + position
    take_index = jnp.where(
        position < count_here, rank % videos // 2 + jnp.where(rank % 2 == core, 0, chips), -1
    )
    sender = 2 * chip_slot + core
    place_here = (sender - start_here + 16 * videos) % videos
    place_near = (sender - start_near + 16 * videos) % videos
    back_index = jnp.where(
        place_here < count_here,
        place_here,
        jnp.where(place_near < count_near, MOST_WIN + place_near, -1),
    )
    live = (count_here * QUERIES)[None]

    source = captions[0, 0].astype(jnp.float32)
    inv_rms = lax.rsqrt(jnp.mean(source * source, axis=-1, keepdims=True) + EPSILON)
    normed = (source * inv_rms * caption_gain).astype(jnp.bfloat16)
    query = jnp.dot(normed, w_query, preferred_element_type=jnp.float32).astype(jnp.bfloat16)
    query = query * jnp.bfloat16(HEAD_DIM ** (-0.5))
    row_live = jnp.arange(CAPLEN, dtype=jnp.int32) < caption_lengths[0, 0]
    grad_out = jnp.where(row_live[:, None], upstream[0, 0], jnp.zeros_like(upstream[0, 0]))
    d_context = jnp.dot(grad_out, w_output.T, preferred_element_type=jnp.float32).astype(
        jnp.bfloat16
    )
    query_other = lax.ppermute(query, "section", SWAP)
    d_context_other = lax.ppermute(d_context, "section", SWAP)
    paired_kv = (
        memory_kv.reshape(QDIM, 2, PAIRS, 128).transpose(0, 2, 1, 3).reshape(QDIM, 2 * INNER)
    )

    memory = compress_block(frames, learned_queries, frame_kv, query_out, query_gain)
    packed = gather_windows(send_index, [memory], False)
    arrived = lax.all_to_all(packed, CHIP, split_axis=0, concat_axis=0, tiled=True)
    beside = lax.ppermute(arrived, CORE, SWAP)
    half = gather_windows(take_index, [arrived, beside], True).reshape(ROWS, QDIM)
    key_value = jnp.dot(half, paired_kv, preferred_element_type=jnp.float32).astype(jnp.bfloat16)

    tokens = (live, query, query_other, d_context, d_context_other, key_value)
    stats = attention_stats(*tokens)
    peer = lax.ppermute(stats, "section", SWAP)
    context_own, context_other, dq_own, dq_other, d_sum = attention_grads(*tokens, stats, peer)

    d_memory = lax.dot_general(d_sum, paired_kv, NT, preferred_element_type=jnp.float32).astype(
        jnp.bfloat16
    )
    d_memory = d_memory.reshape(MOST_WIN, QUERIES, QDIM)
    d_beside = lax.ppermute(d_memory, CORE, SWAP)
    d_packed = gather_windows(back_index, [d_memory, d_beside], False)
    returned = lax.all_to_all(d_packed, CHIP, split_axis=0, concat_axis=0, tiled=True)
    memory_grad = gather_windows(owner_chip, [returned], False)

    term = jnp.dot(half.T, d_sum, preferred_element_type=jnp.float32).astype(jnp.bfloat16)
    term = term.reshape(2 * chips, 2, QDIM // (4 * chips), 2 * INNER)
    kept = lax.dynamic_index_in_dim(term, core, 1, keepdims=False)
    given = lax.dynamic_index_in_dim(term, 1 - core, 1, keepdims=False)
    got = lax.ppermute(given, CORE, SWAP)
    chip_term = (kept.astype(jnp.float32) + got.astype(jnp.float32)).astype(jnp.bfloat16)
    terms = lax.all_to_all(chip_term, ("section", *CHIP), split_axis=0, concat_axis=0, tiled=True)
    kv_grad = jnp.sum(terms.astype(jnp.float32), axis=0)
    kv_grad = kv_grad.reshape(-1, PAIRS, 2, 128).transpose(0, 2, 1, 3).reshape(-1, 2 * INNER)

    context = (context_own + lax.ppermute(context_other, "section", SWAP)).astype(jnp.bfloat16)
    decoded = (source + jnp.dot(context, w_output, preferred_element_type=jnp.float32)).astype(
        jnp.bfloat16
    )
    d_query = (dq_own + lax.ppermute(dq_other, "section", SWAP)).astype(jnp.bfloat16)
    d_scaled = jnp.dot(d_query, w_query.T, preferred_element_type=jnp.float32) * caption_gain
    caption_grad = grad_out.astype(jnp.float32) + inv_rms * (
        d_scaled - source * inv_rms * inv_rms * jnp.mean(d_scaled * source, axis=-1, keepdims=True)
    )
    return (
        decoded[None, None],
        caption_grad.astype(jnp.bfloat16)[None, None],
        memory_grad,
        kv_grad,
    )


def solution(mesh):
    finer = Mesh(
        mesh.devices.reshape(mesh.shape["section"], 2, 4, 4, 2),
        ("section", "dev_0", "dev_1", "dev_2", "dev_3"),
    )
    placed = (
        P(SECTION_DEV, None, None),
        P(),
        P(),
        P(),
        P(),
        P(),
        P("section", DEV, None, None),
        P("section", DEV),
        P(),
        P(),
        P(),
        P(),
        P("section", DEV, None, None),
    )
    return jax.shard_map(
        local,
        mesh=finer,
        in_specs=placed,
        out_specs=(
            P("section", DEV, None, None),
            P("section", DEV, None, None),
            P(SECTION_DEV, None, None),
            P(SECTION_DEV, None),
        ),
        check_vma=False,
    )
```

time: 750 us -> 246 us (0.33)
  waiting for transfers between devices: 473 us -> 54.5 us
  matrix products: 130 us -> 34.2 us
  blocking collectives: 0 us -> 37.9 us
  local copies, waits for them, and re-layouts: 65.1 us -> 30.8 us
  Pallas kernels: 0 us -> 33.9 us
  between operations: 15.3 us -> 2.45 us
  starting transfers between devices: 32.2 us -> 21.6 us
    reduce_scatter x2 -> x0, waiting for transfers between devices: 297 us -> none  [the longest x1 297 us: summed_rows(): return lax.psum_scatter(blocks, chips, scatter_dimension=0, tiled=True)[0]]
    dot_general x16 -> x7, matrix products: 110 us -> 24.6 us  [the longest x1 7.04 us: local(): jnp.dot(half, paired_kv, preferred_element_type=jnp.float32)]
    unnamed x5 -> x0, waiting for transfers between devices: 70 us -> none
    all_to_all x3 -> x2, waiting for transfers between devices: 68.5 us -> 23.6 us  [the longest x1 23.6 us: local(): lax.all_to_all(d_packed, CHIP, split_axis=0, concat_axis=0, tiled=True)]
    all_to_all x0 -> x1, blocking collectives: none -> 37.9 us  [local(): lax.all_to_all(packed, CHIP, split_axis=0, concat_axis=0, tiled=True)]
    all_gather x1 -> x0, waiting for transfers between devices: 36.9 us -> none  [local(): lax.all_gather(memory_half, 'section', axis=0, tiled=True)]
    pallas_call x0 -> x6, Pallas kernels: none -> 33.9 us  [the longest x4 13.8 us: gather_windows(): pl.pallas_call(kernel, out_shape=jax.ShapeDtypeStruct((count, *inner), so...]
    ppermute x0 -> x8, waiting for transfers between devices: none -> 30.9 us  [the longest x1 28 us: local(): lax.ppermute(dq_other, 'section', SWAP)]
  transfers between devices with their start and end apart: 7 -> 10, of which waited for: 5 -> 4; matrix products, arithmetic and copies ran while one was open for 10% -> 17% of each run, Pallas kernels for 0% -> 4%
where the time goes in v1:
time: 246 us; the launch traced here: 242 us
  waiting for transfers between devices  54.5 us (22%)
  blocking collectives  37.9 us (15%)
  matrix products  34.2 us (14%)
  Pallas kernels  33.9 us (14%)
  local copies, waits for them, and re-layouts  30.8 us (13%)
  other arithmetic  26.8 us (11%)
  starting transfers between devices  21.6 us (9%)
    all_to_all x1, blocking collectives, local(): lax.all_to_all(packed, CHIP, split_axis=0, concat_axis=0, tiled=True)  37.9 us
    ppermute x1, waiting for transfers between devices, local(): lax.ppermute(dq_other, 'section', SWAP)  28 us
    all_to_all x1, waiting for transfers between devices, local(): lax.all_to_all(d_packed, CHIP, split_axis=0, concat_axis=0, tiled=True)  23.6 us
    pallas_call x4, Pallas kernels, gather_windows(): pl.pallas_call(kernel, out_shape=jax.ShapeDtypeStruct((count, *inner), so...  13.8 us
    pallas_call x1, Pallas kernels, attention_grads(): pl.pallas_call(grads_kernel, grid=(PAIRS,), out_shape=(wide, narrow, wide...  11.5 us
    unnamed x50, local copies, waits for them, and re-layouts  10.5 us
    sub x1, other arithmetic, compress_block(): attention = jax.nn.softmax(scores, axis=-1).astype(jnp.bfloat16)  9.46 us
    pallas_call x1, Pallas kernels, attention_stats(): pl.pallas_call(stats_kernel, grid=(PAIRS,), out_shape=jax.ShapeDtypeStruc...  8.51 us
  transfers between devices with their start and end apart: 10, of which 4 were waited for; matrix products, arithmetic and copies ran while one was open for 17% of the time, Pallas kernels for 4%

profile of v1, /device:TPU:64, one launch (start us, length us, event | category | flops | bytes accessed | tf_op | source)
XLA Modules:
  0.0 242.3 jit_solution(12545409794165625036)
XLA Ops:
  5.1 4.8 %convolution_convert_fusion.2 = bf16[512,2048]{1,0:T(8,128)(2,1)S(1)} fusion(bf16[512,1024]{1,0:T(8,128)(2,1)} %bitcast.91, bf16[1024,2048]{1,0:T(8,128)(2,1)} %param.16), kind=kOutput, calls=%fused_computation.12 | convolution fusion | flops 2148532224 | bytes 7340032 | tf_op jit(solution)/shard_map/dot_general | solution.py:38
  11.1 4.0 %reshape.107 = bf16[16,32,16,64]{3,2,1,0:T(8,128)(2,1)} reshape(bf16[512,1024]{1,0:T(8,128)(2,1)} %get-tuple-element.19) | data formatting | bytes 2097152 | tf_op jit(solution)/shard_map/reshape | solution.py:42
  15.1 2.3 reshape.108
  17.4 2.3 fusion.14
  19.7 9.5 %fusion.50 = (f32[16,16,32]{2,0,1:T(8,128)S(1)}, f32[16,16,32,32]{2,3,0,1:T(8,128)S(1)}) fusion(f32[16,16,32,32]{3,2,1,0:T(8,128)S(1)} %fusion.14), kind=kOutput, calls=%fused_computation.107 | output fusion | flops 1048607 | bytes 2129920 | tf_op jit(solution)/shard_map/sub | solution.py:47
  30.4 2.2 copy.38
  32.6 3.2 %dot_general.40 = bf16[16,32,1024]{2,1,0:T(8,128)(2,1)S(1)} reshape(bf16[16,32,16,64]{3,2,1,0:T(8,128)(2,1)} %copy.38) | data formatting | bytes 2097152 | tf_op jit(solution)/shard_map/dot_general | solution.py:51
  38.5 3.7 %gather_windows.4 = bf16[32,32,1024]{2,1,0:T(8,128)(2,1)} custom-call(s32[32]{0:T(128)} %broadcast_add_fusion.index_ref, bf16[16,32,1024]{2,1,0:T(8,128)(2,1)} %multiply_convert_fusion.refs_0_), custom_call_target="tpu_custom_call" | custom-call | flops 2000000000 | bytes 4194304 | tf_op jit(solution)/shard_map/gather_windows/pallas_call | solution.py:93
  42.2 37.9 %all_to_all.15.refs_0_ = bf16[32,32,1024]{2,1,0:T(8,128)(2,1)} all-to-all(bf16[32,32,1024]{2,1,0:T(8,128)(2,1)} %gather_windows.4), channel_id=1, replica_groups=mesh['section'=2,'dev_0'=2,'dev_1'=4,'dev_2'=4,'dev_3'=2] {'dev_0','dev_..., dimensions={0} | all-to-all | bytes 4194304 | tf_op jit(solution)/shard_map/all_to_all | solution.py:316
  82.5 1.9 collective-permute-start.1
  86.5 6.4 %copy.39 = bf16[1024,2048]{0,1:T(8,128)(2,1)} copy(bf16[1024,2048]{1,0:T(8,128)(2,1)} %param.23) | data formatting | bytes 8388608 | tf_op args[10]
  93.0 4.7 %copy.40 = bf16[1024,8,2,128]{0,3,2,1:T(8,128)(2,1)} copy(bf16[1024,8,2,128]{0,3,1,2:T(8,128)(2,1)} %bitcast.80) | data formatting | bytes 8388608 | tf_op jit(solution)/shard_map/transpose | solution.py:311
  97.7 1.8 compare_select_fusion.10.index_ref
  99.5 3.3 %gather_windows.5 = bf16[20,32,1024]{2,1,0:T(8,128)(2,1)} custom-call(s32[20]{0:T(128)} %compare_select_fusion.10.index_ref, bf16[32,32,1024]{2,1,0:T(8,128)(2,1)} %all_to_all.15.refs_0_, bf16[32,32,1024]{2,1,0:T(8,128)(2,1)} %collective-permute-done.2.refs_1_), custom_call_target="tpu_custom_call" | custom-call | flops 2000000000 | bytes 2621440 | tf_op jit(solution)/shard_map/gather_windows/pallas_call | solution.py:93
  102.9 7.0 %convolution_convert_fusion.1.kv_ref = bf16[640,2048]{1,0:T(8,128)(2,1)} fusion(bf16[640,1024]{1,0:T(8,128)(2,1)} %bitcast.92, bf16[1024,2048]{0,1:T(8,128)(2,1)} %bitcast.83), kind=kOutput, calls=%fused_computation.11 | convolution fusion | flops 2685665280 | bytes 8126464 | tf_op jit(solution)/shard_map/dot_general | solution.py:319
  110.7 8.5 %attention_stats.1.stats_ref = f32[3,8,512]{2,1,0:T(8,128)} custom-call(s32[1]{0:T(128)} %bitcast.2.live_ref, bf16[128,1024]{1,0:T(8,128)(2,1)} %copy-done.12, bf16[128,1024]{1,0:T(8,128)(2,1)} %copy-done.19, bf16[128,1024]{1,0:T(8,128)(2,1)} %copy-done.11, bf16[128,1024]{1,0:T(8,128)(2,1)} %copy-done.18, bf16[640,2048]{1,0:T(8,128)(2,1)} %convolution_convert_fusion.1.kv_ref), custom_call_target="tpu_custom_call" | custom-call | flops 5000000000 | bytes 4000000 | tf_op jit(solution)/shard_map/attention_stats/pallas_call | solution.py:209
  120.7 2.8 %collective-permute-done.3.peer_ref = f32[3,8,512]{2,1,0:T(8,128)S(1)} collective-permute-done((f32[3,8,512]{2,1,0:T(8,128)}, f32[3,8,512]{2,1,0:T(8,128)S(1)}, u32[]{:S(2)}, u32[]{:S(2)}) %collective-permute-start.3) | collective-permute-done | bytes 49184 | tf_op jit(solution)/shard_map/ppermute | solution.py:323
  124.1 11.5 %attention_grads.1 = (f32[128,1024]{1,0:T(8,128)}, bf16[128,1024]{1,0:T(8,128)(2,1)}, f32[128,1024]{1,0:T(8,128)}, bf16[128,1024]{1,0:T(8,128)(2,1)}, bf16[640,2048]{1,0:T(8,128)(2,1)}) custom-call(s32[1]{0:T(128)} %bitcast.2.live_ref, bf16[128,1024]{1,0:T(8,128)(2,1)} %copy-done.12, bf16[128,1024]{1,0:T(8,128)(2,1)} %copy-done.19, ...), custom_call_target="tpu_custom_call" | custom-call | flops 12000000000 | bytes 10000000 | tf_op jit(solution)/shard_map/attention_grads/pallas_call | solution.py:227
  135.7 6.0 %convolution_convert_fusion.3 = bf16[640,1024]{1,0:T(8,128)(2,1)S(1)} fusion(bf16[640,2048]{1,0:T(8,128)(2,1)} %get-tuple-element.13, bf16[1024,2048]{0,1:T(8,128)(2,1)} %bitcast.84), kind=kOutput, calls=%fused_computation.32 | convolution fusion | flops 2685009920 | bytes 8126464 | tf_op jit(solution)/shard_map/dot_general | solution.py:326
  141.8 3.7 %convolution_convert_fusion = bf16[1024,2048]{1,0:T(8,128)(2,1)S(1)} fusion(bf16[640,1024]{1,0:T(8,128)(2,1)S(1)} %bitcast.93, bf16[640,2048]{1,0:T(8,128)(2,1)S(1)} %copy-done.23), kind=kOutput, calls=%fused_computation.9 | convolution fusion | flops 2686451712 | bytes 8126464 | tf_op jit(solution)/shard_map/dot_general | solution.py:335
  145.5 1.9 copy-done.6
  147.5 1.6 dynamic-slice_bitcast_fusion
  149.5 3.1 %compare_select_fusion.index_ref = s32[32]{0:T(128)} fusion(s32[]{:T(128)} %get-tuple-element.15, s32[]{:T(128)} %get-tuple-element.14, s32[]{:T(128)} %get-tuple-element.17, s32[]{:T(128)} %get-tuple-element.16, s32[]{:T(128)S(6)} %axis_index.56), kind=kLoop, calls=%fused_computation.62 | loop fusion | flops 1056 | bytes 148 | tf_op jit(solution)/shard_map/jit(_where)/select_n | solution.py:291
  152.6 3.7 %gather_windows.6 = bf16[32,32,1024]{2,1,0:T(8,128)(2,1)} custom-call(s32[32]{0:T(128)} %compare_select_fusion.index_ref, bf16[20,32,1024]{2,1,0:T(8,128)(2,1)} %bitcast.90, bf16[20,32,1024]{2,1,0:T(8,128)(2,1)} %collective-permute-done.6.refs_1_), custom_call_target="tpu_custom_call" | custom-call | flops 2000000000 | bytes 4194304 | tf_op jit(solution)/shard_map/gather_windows/pallas_call | solution.py:93
  156.3 6.7 %all-to-all-start.1 = ((bf16[32,32,1024]{2,1,0:T(8,128)(2,1)}), bf16[32,32,1024]{2,1,0:T(8,128)(2,1)}, u32[]{:S(2)}, u32[]{:S(2)}) async-start(bf16[32,32,1024]{2,1,0:T(8,128)(2,1)} %gather_windows.6), calls=%async_computation.1 | async-start | bytes 4194304 | tf_op jit(solution)/shard_map/all_to_all | solution.py:332
  163.0 4.5 %fusion.1 = bf16[64,8,2048]{2,1,0:T(8,128)(2,1)} fusion(bf16[64,8,2048]{2,1,0:T(8,128)(2,1)} %collective-permute-done.7, bf16[64,2,8,2048]{3,2,1,0:T(8,128)(2,1)} %bitcast.82, s32[]{:T(128)S(6)} %select_n.101), kind=kLoop, calls=%fused_computation.2 | loop fusion | flops 4194304 | bytes 6291460 | tf_op jit(solution)/shard_map/convert_element_type | solution.py:340
  167.5 23.6 %all-to-all-done.1.refs_0_ = bf16[32,32,1024]{2,1,0:T(8,128)(2,1)} async-done(((bf16[32,32,1024]{2,1,0:T(8,128)(2,1)}), bf16[32,32,1024]{2,1,0:T(8,128)(2,1)}, u32[]{:S(2)}, u32[]{:S(2)}) %all-to-all-start.1) | async-done | bytes 2097184 | tf_op jit(solution)/shard_map/all_to_all | solution.py:332
  191.1 8.5 %all-to-all-start.2 = ((bf16[64,8,2048]{2,1,0:T(8,128)(2,1)}), bf16[64,8,2048]{2,1,0:T(8,128)(2,1)}, u32[]{:S(2)}, u32[]{:S(2)}) async-start(bf16[64,8,2048]{2,1,0:T(8,128)(2,1)} %fusion.1), calls=%async_computation.2 | async-start | bytes 4194304 | tf_op jit(solution)/shard_map/all_to_all | solution.py:341
  201.7 28.0 %collective-permute-done.5 = bf16[128,1024]{1,0:T(8,128)(2,1)S(1)} collective-permute-done((bf16[128,1024]{1,0:T(8,128)(2,1)S(1)}, bf16[128,1024]{1,0:T(8,128)(2,1)S(1)}, u32[]{:S(2)}, u32[]{:S(2)}) %collective-permute-start.5) | collective-permute-done | bytes 262176 | tf_op jit(solution)/shard_map/ppermute | solution.py:349
  229.7 3.9 %fusion.31 = (f32[128]{0:T(128)S(1)}, f32[128,2048]{1,0:T(8,128)S(1)}) fusion(bf16[1,1,128,2048]{3,2,1,0:T(8,128)(2,1)S(1)} %copy-done.5, f32[2048]{0:T(1024)S(1)} %copy-done.13, bf16[2048,1024]{1,0:T(8,128)(2,1)} %param.22, f32[128,1024]{1,0:T(8,128)S(1)} %copy-done.10, bf16[128,1024]{1,0:T(8,128)(2,1)S(1)} %collective-permute-done.5), kind=kOutput, calls=%fused_computation.45 | convolution fusion | flops 538312576 | bytes 6562304 | tf_op jit(solution)/shard_map/dot_general | solution.py:350
  236.5 3.2 %gather_windows.7 = bf16[16,32,1024]{2,1,0:T(8,128)(2,1)} custom-call(s32[16]{0:T(128)} %copy-done.22, bf16[32,32,1024]{2,1,0:T(8,128)(2,1)} %all-to-all-done.1.refs_0_), custom_call_target="tpu_custom_call" | custom-call | flops 2000000000 | bytes 2097152 | tf_op jit(solution)/shard_map/gather_windows/pallas_call | solution.py:93
  239.7 1.9 convert_reduce_fusion
  (87 shorter events, 21.5 us)
Async XLA Ops:
  0.6 35.2 %copy-start = (bf16[1024,1024]{1,0:T(8,128)(2,1)S(1)}, bf16[1024,1024]{1,0:T(8,128)(2,1)}, u32[]{:S(2)}) copy-start(bf16[1024,1024]{1,0:T(8,128)(2,1)} %param.17) | copy-start | bytes 6291460
  4.5 5.5 %copy-start.22 = (s32[16]{0:T(128)}, s32[16]{0:T(128)S(1)}, u32[]{:S(2)}) copy-start(s32[16]{0:T(128)S(1)} %and_select_fusion.2.index_ref) | copy-start | bytes 196
  19.7 9.5 %copy-start.7 = (bf16[16,32,16,64]{3,2,1,0:T(8,128)(2,1)S(1)}, bf16[16,32,16,64]{3,2,1,0:T(8,128)(2,1)}, u32[]{:S(2)}) copy-start(bf16[16,32,16,64]{3,2,1,0:T(8,128)(2,1)} %reshape.107) | copy-start | bytes 3145732
  35.8 1.4 copy-start.14
  38.5 42.4 %copy-start.8 = (bf16[1,1,128,2048]{3,2,1,0:T(8,128)(2,1)S(1)}, bf16[1,1,128,2048]{3,2,1,0:T(8,128)(2,1)}, u32[]{:S(2)}) copy-start(bf16[1,1,128,2048]{3,2,1,0:T(8,128)(2,1)} %param.25) | copy-start | bytes 1572868
  42.2 38.7 %copy-start.3 = (bf16[1024,2048]{1,0:T(8,128)(2,1)S(1)}, bf16[1024,2048]{1,0:T(8,128)(2,1)}, u32[]{:S(2)}) copy-start(bf16[1024,2048]{1,0:T(8,128)(2,1)} %param.24) | copy-start | bytes 12582916
  80.1 4.2 %copy-start.5 = (bf16[1,1,128,2048]{3,2,1,0:T(8,128)(2,1)S(1)}, bf16[1,1,128,2048]{3,2,1,0:T(8,128)(2,1)}, u32[]{:S(2)}) copy-start(bf16[1,1,128,2048]{3,2,1,0:T(8,128)(2,1)} %param.19) | copy-start | bytes 1572868
  80.1 19.4 %collective-permute-start.2 = (bf16[32,32,1024]{2,1,0:T(8,128)(2,1)}, bf16[32,32,1024]{2,1,0:T(8,128)(2,1)}, u32[]{:S(2)}, u32[]{:S(2)}) collective-permute-start(bf16[32,32,1024]{2,1,0:T(8,128)(2,1)} %all_to_all.15.refs_0_), channel_id=1, source_target_pairs={{0,1},{1,0},{2,3},{3,2},{4,5},{5,4},{6,7},{7,6},{8,9},{9,8},{10,11... | collective-permute-start | bytes 6291464 | tf_op jit(solution)/shard_map/ppermute | solution.py:317
  80.9 3.6 %copy-start.2 = (bf16[2048,1024]{1,0:T(8,128)(2,1)S(1)}, bf16[2048,1024]{1,0:T(8,128)(2,1)}, u32[]{:S(2)}) copy-start(bf16[2048,1024]{1,0:T(8,128)(2,1)} %param.22) | copy-start | bytes 12582916
  80.9 3.6 %copy-start.13 = (f32[2048]{0:T(1024)S(1)}, f32[2048]{0:T(1024)}, u32[]{:S(2)}) copy-start(f32[2048]{0:T(1024)} %param.21) | copy-start | bytes 24580
  82.5 2.9 %copy-start.11 = (bf16[128,1024]{1,0:T(8,128)(2,1)}, bf16[128,1024]{1,0:T(8,128)(2,1)S(1)}, u32[]{:S(2)}) copy-start(bf16[128,1024]{1,0:T(8,128)(2,1)S(1)} %convolution_convert_fusion.4.dc_own) | copy-start | bytes 786436
  82.5 27.4 %collective-permute-start.1 = (bf16[128,1024]{1,0:T(8,128)(2,1)S(1)}, bf16[128,1024]{1,0:T(8,128)(2,1)S(1)}, u32[]{:S(2)}, u32[]{:S(2)}) collective-permute-start(bf16[128,1024]{1,0:T(8,128)(2,1)S(1)} %convolution_convert_fusion.4.dc_own), channel_id=1, source_target_pairs={{0,64},{64,0},{1,65},{65,1},{2,66},{66,2},{3,67},{67,3},{4,68},{68... | collective-permute-start | bytes 786440 | tf_op jit(solution)/shard_map/ppermute | solution.py:309
  85.4 7.6 %copy-start.12 = (bf16[128,1024]{1,0:T(8,128)(2,1)}, bf16[128,1024]{1,0:T(8,128)(2,1)S(1)}, u32[]{:S(2)}) copy-start(bf16[128,1024]{1,0:T(8,128)(2,1)S(1)} %fusion.23.q_own) | copy-start | bytes 786436
  85.4 24.5 %collective-permute-start = (bf16[128,1024]{1,0:T(8,128)(2,1)S(1)}, bf16[128,1024]{1,0:T(8,128)(2,1)S(1)}, u32[]{:S(2)}, u32[]{:S(2)}) collective-permute-start(bf16[128,1024]{1,0:T(8,128)(2,1)S(1)} %fusion.23.q_own), channel_id=1, source_target_pairs={{0,64},{64,0},{1,65},{65,1},{2,66},{66,2},{3,67},{67,3},{4,68},{68... | collective-permute-start | bytes 786440 | tf_op jit(solution)/shard_map/ppermute | solution.py:308
  109.9 0.8 copy-start.19
  119.2 4.3 %collective-permute-start.3 = (f32[3,8,512]{2,1,0:T(8,128)}, f32[3,8,512]{2,1,0:T(8,128)S(1)}, u32[]{:S(2)}, u32[]{:S(2)}) collective-permute-start(f32[3,8,512]{2,1,0:T(8,128)} %attention_stats.1.stats_ref), channel_id=1, source_target_pairs={{0,64},{64,0},{1,65},{65,1},{2,66},{66,2},{3,67},{67,3},{4,68},{68... | collective-permute-start | bytes 147464 | tf_op jit(solution)/shard_map/ppermute | solution.py:323
  135.7 6.1 %copy-start.21 = (bf16[20,32,1024]{2,1,0:T(8,128)(2,1)S(1)}, bf16[20,32,1024]{2,1,0:T(8,128)(2,1)}, u32[]{:S(2)}) copy-start(bf16[20,32,1024]{2,1,0:T(8,128)(2,1)} %gather_windows.5) | copy-start | bytes 3932164
  135.7 6.1 %copy-start.23 = (bf16[640,2048]{1,0:T(8,128)(2,1)S(1)}, bf16[640,2048]{1,0:T(8,128)(2,1)}, u32[]{:S(2)}) copy-start(bf16[640,2048]{1,0:T(8,128)(2,1)} %get-tuple-element.13) | copy-start | bytes 7864324
  141.7 3.8 %copy-start.15 = (bf16[640,1024]{1,0:T(8,128)(2,1)}, bf16[640,1024]{1,0:T(8,128)(2,1)S(1)}, u32[]{:S(2)}) copy-start(bf16[640,1024]{1,0:T(8,128)(2,1)S(1)} %convolution_convert_fusion.3) | copy-start | bytes 3932164
  141.7 10.9 %collective-permute-start.6 = (bf16[20,32,1024]{2,1,0:T(8,128)(2,1)S(1)}, bf16[20,32,1024]{2,1,0:T(8,128)(2,1)}, u32[]{:S(2)}, u32[]{:S(2)}) collective-permute-start(bf16[20,32,1024]{2,1,0:T(8,128)(2,1)S(1)} %bitcast.89), channel_id=1, source_target_pairs={{0,1},{1,0},{2,3},{3,2},{4,5},{5,4},{6,7},{7,6},{8,9},{9,8},{10,11... | collective-permute-start | bytes 3932168 | tf_op jit(solution)/shard_map/ppermute | solution.py:330
  145.5 1.9 copy-start.6
  149.1 13.9 %collective-permute-start.7 = (bf16[64,8,2048]{2,1,0:T(8,128)(2,1)}, bf16[64,8,2048]{2,1,0:T(8,128)(2,1)}, u32[]{:S(2)}, u32[]{:S(2)}) collective-permute-start(bf16[64,8,2048]{2,1,0:T(8,128)(2,1)} %dynamic-slice_bitcast_fusion), channel_id=1, source_target_pairs={{0,1},{1,0},{2,3},{3,2},{4,5},{5,4},{6,7},{7,6},{8,9},{9,8},{10,11... | collective-permute-start | bytes 6291464 | tf_op jit(solution)/shard_map/ppermute | solution.py:339
  156.3 34.8 %all-to-all-start.1 = ((bf16[32,32,1024]{2,1,0:T(8,128)(2,1)}), bf16[32,32,1024]{2,1,0:T(8,128)(2,1)}, u32[]{:S(2)}, u32[]{:S(2)}) async-start(bf16[32,32,1024]{2,1,0:T(8,128)(2,1)} %gather_windows.6), calls=%async_computation.1 | async-start | bytes 4194304 | tf_op jit(solution)/shard_map/all_to_all | solution.py:332
  167.5 32.1 %copy-start.17 = (bf16[128,1024]{1,0:T(8,128)(2,1)S(1)}, bf16[128,1024]{1,0:T(8,128)(2,1)}, u32[]{:S(2)}) copy-start(bf16[128,1024]{1,0:T(8,128)(2,1)} %get-tuple-element.12) | copy-start | bytes 786436
  167.5 33.6 %copy-start.16 = (bf16[128,1024]{1,0:T(8,128)(2,1)S(1)}, bf16[128,1024]{1,0:T(8,128)(2,1)}, u32[]{:S(2)}) copy-start(bf16[128,1024]{1,0:T(8,128)(2,1)} %get-tuple-element.10) | copy-start | bytes 786436
  167.5 62.2 %copy-start.10 = (f32[128,1024]{1,0:T(8,128)S(1)}, f32[128,1024]{1,0:T(8,128)}, u32[]{:S(2)}) copy-start(f32[128,1024]{1,0:T(8,128)} %get-tuple-element.11) | copy-start | bytes 1572868
  191.1 48.5 %all-to-all-start.2 = ((bf16[64,8,2048]{2,1,0:T(8,128)(2,1)}), bf16[64,8,2048]{2,1,0:T(8,128)(2,1)}, u32[]{:S(2)}, u32[]{:S(2)}) async-start(bf16[64,8,2048]{2,1,0:T(8,128)(2,1)} %fusion.1), calls=%async_computation.2 | async-start | bytes 4194304 | tf_op jit(solution)/shard_map/all_to_all | solution.py:341
  199.6 30.1 %collective-permute-start.5 = (bf16[128,1024]{1,0:T(8,128)(2,1)S(1)}, bf16[128,1024]{1,0:T(8,128)(2,1)S(1)}, u32[]{:S(2)}, u32[]{:S(2)}) collective-permute-start(bf16[128,1024]{1,0:T(8,128)(2,1)S(1)} %copy-done.17), channel_id=1, source_target_pairs={{0,64},{64,0},{1,65},{65,1},{2,66},{66,2},{3,67},{67,3},{4,68},{68... | collective-permute-start | bytes 786440 | tf_op jit(solution)/shard_map/ppermute | solution.py:349
  201.1 32.7 %collective-permute-start.4 = (bf16[128,1024]{1,0:T(8,128)(2,1)S(1)}, bf16[128,1024]{1,0:T(8,128)(2,1)S(1)}, u32[]{:S(2)}, u32[]{:S(2)}) collective-permute-start(bf16[128,1024]{1,0:T(8,128)(2,1)S(1)} %copy-done.16), channel_id=1, source_target_pairs={{0,64},{64,0},{1,65},{65,1},{2,66},{66,2},{3,67},{67,3},{4,68},{68... | collective-permute-start | bytes 786440 | tf_op jit(solution)/shard_map/ppermute | solution.py:345
  229.7 4.0 %copy-start.4 = (bf16[1024,2048]{1,0:T(8,128)(2,1)S(1)}, bf16[1024,2048]{1,0:T(8,128)(2,1)}, u32[]{:S(2)}) copy-start(bf16[1024,2048]{1,0:T(8,128)(2,1)} %param.24) | copy-start | bytes 12582916
  229.7 4.0 %copy-start.9 = (f32[128,1024]{1,0:T(8,128)S(1)}, f32[128,1024]{1,0:T(8,128)}, u32[]{:S(2)}) copy-start(f32[128,1024]{1,0:T(8,128)} %get-tuple-element.9) | copy-start | bytes 1572868
  236.5 5.8 %copy-start.1 = (bf16[1024,1024]{1,0:T(8,128)(2,1)S(1)}, bf16[1024,1024]{1,0:T(8,128)(2,1)}, u32[]{:S(2)}) copy-start(bf16[1024,1024]{1,0:T(8,128)(2,1)} %param.17) | copy-start | bytes 6291460
  (2 other events, 1.3 us)

commit v2 on v1

v2 whole, which is shorter than its diff:
```python
import functools

import jax
import jax.numpy as jnp
from jax import lax
from jax.experimental import pallas as pl
from jax.experimental.pallas import tpu as pltpu
from jax.sharding import Mesh
from jax.sharding import PartitionSpec as P


HEADS = 16
HEAD_DIM = 64
INNER = 1024
QDIM = 1024
QUERIES = 32
FRAMES = 32
WIN_DEV = 16
MOST_WIN = 20
CAPLEN = 128
PAIRS = HEADS // 2
ROWS = MOST_WIN * QUERIES
DEV = ("dev_0", "dev_1", "dev_2", "dev_3")
CHIP = ("dev_0", "dev_1", "dev_2")
CORE = "dev_3"
SECTION_DEV = ("section", "dev_0", "dev_1", "dev_2", "dev_3")
SWAP = [(0, 1), (1, 0)]

EPSILON = 1e-06
DEAD = -1e30


NT = (((1,), (1,)), ((), ()))
TN = (((0,), (0,)), ((), ()))
NN = (((1,), (0,)), ((), ()))


def dot(a, b, dims=NN):
    return lax.dot_general(a, b, dims, preferred_element_type=jnp.float32)


def smem():
    return pl.BlockSpec(memory_space=pltpu.SMEM)


def anywhere():
    return pl.BlockSpec(memory_space=pl.ANY)


def run_start(counts_ref, section, video):
    step = lambda v, total: total + jnp.where(v < video, counts_ref[section, v], 0)
    return lax.fori_loop(0, counts_ref.shape[1], step, jnp.int32(0))


def vmem():
    return pl.BlockSpec(memory_space=pltpu.VMEM)


def limit(mib):
    return pltpu.CompilerParams(vmem_limit_bytes=mib << 20)


def columns(pair, base=0):
    return pl.ds(pl.multiple_of(base + pair * 128, 128), 128)


CUTS = [pl.ds(512 * c, 512) for c in range(4)]


def compress_kernel(
    place_ref,
    counts_ref,
    queries_ref,
    gain_ref,
    frames_hbm,
    weight_hbm,
    out_hbm,
    sent_hbm,
    frames_ref,
    weight_ref,
    pairs_ref,
    context_ref,
    out_ref,
    memory_ref,
    slots_ref,
    fetch_sems,
    sems,
):
    copies = 4
    rows = copies * FRAMES
    wide = 2 * QUERIES * copies
    frames_fetch = pltpu.make_async_copy(frames_hbm, frames_ref, fetch_sems.at[4])
    out_fetch = pltpu.make_async_copy(out_hbm, out_ref, fetch_sems.at[5])
    fetches = [
        pltpu.make_async_copy(weight_hbm.at[:, cut], weight_ref.at[:, cut], fetch_sems.at[c])
        for c, cut in enumerate(CUTS)
    ]
    frames_fetch.start()
    for fetch in fetches:
        fetch.start()
    out_fetch.start()
    section, video_id = place_ref[0], place_ref[1]
    videos = counts_ref.shape[1]

    def owned(v, start):
        end = start + counts_ref[section, v]
        window = (start - video_id + 2 * videos - 1) // videos - 1

        @pl.when(window * videos + video_id < end)
        def _():
            slots_ref[window] = v // 2

        return end

    lax.fori_loop(0, videos, owned, jnp.int32(0))
    frames_fetch.wait()
    for fetch, cut in zip(fetches, CUTS):
        fetch.wait()
        pairs_ref[:, cut] = dot(frames_ref[...], weight_ref[:, cut]).astype(jnp.bfloat16)

    row = lax.broadcasted_iota(jnp.int32, (rows, wide), 0)
    column = lax.broadcasted_iota(jnp.int32, (rows, wide), 1)
    same = row // FRAMES == column // (2 * QUERIES)
    low = lax.broadcasted_iota(jnp.int32, (QUERIES, 128), 1) < HEAD_DIM

    @pl.loop(0, PAIRS, unroll=2)
    def _(pair):
        at = columns(pair)
        queries = queries_ref[:, at]
        zero = jnp.zeros_like(queries)
        apart = [jnp.where(low, queries, zero), jnp.where(low, zero, queries)]
        apart = jnp.concatenate(apart * copies, axis=0)
        for group in range(WIN_DEV // copies):
            inside = pl.ds(group * rows, rows)
            keys, values = pairs_ref[inside, at], pairs_ref[inside, columns(pair, QDIM)]
            scores = (dot(keys, apart, NT) * HEAD_DIM ** (-0.5)).reshape(copies, FRAMES, wide)
            grown = jnp.exp(scores - jnp.max(scores, axis=1, keepdims=True))
            attention = grown * (1.0 / jnp.sum(grown, axis=1, keepdims=True))
            attention = jnp.where(same, attention.reshape(rows, wide), 0.0).astype(jnp.bfloat16)
            product = dot(attention, values, TN)
            for c in range(copies):
                start = c * 2 * QUERIES
                mixed = jnp.where(
                    low,
                    product[start : start + QUERIES],
                    product[start + QUERIES : start + 2 * QUERIES],
                )
                window = group * copies + c
                context_ref[pl.ds(window * QUERIES, QUERIES), at] = mixed.astype(jnp.bfloat16)

    out_fetch.wait()
    base = queries_ref[...].astype(jnp.float32)
    gain = gain_ref[...]
    for group in range(WIN_DEV // copies):
        projected = dot(context_ref[pl.ds(group * rows, rows), :], out_ref[...])
        hidden = projected.reshape(copies, QUERIES, QDIM) + base[None]
        scale = lax.rsqrt(jnp.mean(hidden * hidden, axis=-1, keepdims=True) + EPSILON)
        memory_ref[pl.ds(group * copies, copies)] = (hidden * scale * gain[None]).astype(
            jnp.bfloat16
        )
        for window in range(group * copies, (group + 1) * copies):
            pltpu.make_async_copy(
                memory_ref.at[window], sent_hbm.at[slots_ref[window]], sems.at[window]
            ).start()
    for window in range(WIN_DEV):
        pltpu.make_async_copy(memory_ref.at[window], sent_hbm.at[0], sems.at[window]).wait()


def compress_windows(place, counts, frames, queries, frame_kv, query_out, gain):
    chips = counts.shape[1] // 2
    tall = WIN_DEV * FRAMES
    return pl.pallas_call(
        compress_kernel,
        out_shape=jax.ShapeDtypeStruct((chips, QUERIES, QDIM), jnp.bfloat16),
        in_specs=[smem(), smem(), vmem(), vmem(), anywhere(), anywhere(), anywhere()],
        out_specs=anywhere(),
        scratch_shapes=[
            pltpu.VMEM((tall, QDIM), jnp.bfloat16),
            pltpu.VMEM((QDIM, 2 * QDIM), jnp.bfloat16),
            pltpu.VMEM((tall, 2 * QDIM), jnp.bfloat16),
            pltpu.VMEM((tall, QDIM), jnp.bfloat16),
            pltpu.VMEM((QDIM, QDIM), jnp.bfloat16),
            pltpu.VMEM((WIN_DEV, QUERIES, QDIM), jnp.bfloat16),
            pltpu.SMEM((WIN_DEV,), jnp.int32),
            pltpu.SemaphoreType.DMA((6,)),
            pltpu.SemaphoreType.DMA((WIN_DEV,)),
        ],
        cost_estimate=pl.CostEstimate(
            flops=6 * 10**9, bytes_accessed=9 * 10**6, transcendentals=10**6
        ),
        name="compress_windows",
    )(place, counts, queries, gain[None], frames.reshape(tall, QDIM), frame_kv, query_out)


def stacked(own_ref, other_ref, at):
    both = jnp.concatenate([own_ref[:, at], other_ref[:, at]], axis=0)
    lane = lax.broadcasted_iota(jnp.int32, both.shape, 1)
    zero = jnp.zeros_like(both)
    return jnp.concatenate(
        [jnp.where(lane < HEAD_DIM, both, zero), jnp.where(lane < HEAD_DIM, zero, both)], axis=0
    )


def masked_scores(keys, queries, live):
    scores = dot(keys, queries, NT)
    row = lax.broadcasted_iota(jnp.int32, scores.shape, 0)
    return jnp.where(row < live, scores, DEAD)


def touch_kernel(place_ref, weight_ref, out_ref):
    for k in range(place_ref.shape[0]):
        out_ref[k] = place_ref[k]


def touched(place, memory_kv):
    return pl.pallas_call(
        touch_kernel,
        out_shape=jax.ShapeDtypeStruct(place.shape, place.dtype),
        in_specs=[smem(), vmem()],
        out_specs=smem(),
        compiler_params=limit(16),
        cost_estimate=pl.CostEstimate(flops=10**9, bytes_accessed=4 * 10**6, transcendentals=0),
        name="touched",
    )(place, memory_kv)


def project_kernel(
    place_ref, counts_ref, arrived_ref, beside_ref, weight_ref, half_ref, kv_ref, sems
):
    section, video_id = place_ref[0], place_ref[1]
    videos = counts_ref.shape[1]
    core = video_id % 2
    count = counts_ref[section, video_id]
    start = run_start(counts_ref, section, video_id)

    def block(p):
        return half_ref.at[pl.ds(pl.multiple_of(p * QUERIES, QUERIES), QUERIES)]

    @pl.loop(0, MOST_WIN)
    def _(p):
        rank = start + p
        slot = rank % videos // 2
        near = rank % 2 == core

        @pl.when((p < count) & near)
        def _():
            pltpu.make_async_copy(arrived_ref.at[slot], block(p), sems.at[p]).start()

        @pl.when((p < count) & jnp.logical_not(near))
        def _():
            pltpu.make_async_copy(beside_ref.at[slot], block(p), sems.at[p]).start()

        @pl.when(p >= count)
        def _():
            half_ref[pl.ds(pl.multiple_of(p * QUERIES, QUERIES), QUERIES), :] = jnp.zeros(
                (QUERIES, QDIM), jnp.bfloat16
            )

    @pl.loop(0, MOST_WIN)
    def _(p):
        @pl.when(p < count)
        def _():
            pltpu.make_async_copy(arrived_ref.at[0], block(p), sems.at[p]).wait()

    for cut in CUTS:
        kv_ref[:, cut] = dot(half_ref[...], weight_ref[:, cut]).astype(jnp.bfloat16)


def project_memory(place, counts, arrived, beside, memory_kv):
    return pl.pallas_call(
        project_kernel,
        out_shape=(
            jax.ShapeDtypeStruct((ROWS, QDIM), jnp.bfloat16),
            jax.ShapeDtypeStruct((ROWS, 2 * INNER), jnp.bfloat16),
        ),
        in_specs=[smem(), smem(), anywhere(), anywhere(), vmem()],
        out_specs=(vmem(), vmem()),
        scratch_shapes=[pltpu.SemaphoreType.DMA((MOST_WIN,))],
        compiler_params=limit(16),
        cost_estimate=pl.CostEstimate(
            flops=5 * 10**9, bytes_accessed=10**7, transcendentals=0
        ),
        name="project_memory",
    )(place, counts, arrived, beside, memory_kv)


def stats_kernel(
    place_ref, counts_ref, q_own, q_other, dc_own, dc_other, kv_ref, stats_ref
):
    live = counts_ref[place_ref[0], place_ref[1]] * QUERIES

    @pl.loop(0, PAIRS, unroll=2)
    def _(pair):
        at = columns(pair)
        keys, values = kv_ref[:, at], kv_ref[:, columns(pair, INNER)]
        scores = masked_scores(keys, stacked(q_own, q_other, at), live)
        top = jnp.max(scores, axis=0, keepdims=True)
        grown = jnp.exp(scores - top)
        d_probs = dot(values, stacked(dc_own, dc_other, at), NT)
        stats_ref[0, pl.ds(pair, 1), :] = top
        stats_ref[1, pl.ds(pair, 1), :] = jnp.sum(grown, axis=0, keepdims=True)
        stats_ref[2, pl.ds(pair, 1), :] = jnp.sum(grown * d_probs, axis=0, keepdims=True)


def attention_stats(place, counts, tokens, key_value):
    return pl.pallas_call(
        stats_kernel,
        out_shape=jax.ShapeDtypeStruct((3, PAIRS, 4 * CAPLEN), jnp.float32),
        in_specs=[smem(), smem()] + [vmem()] * 5,
        out_specs=vmem(),
        compiler_params=limit(16),
        cost_estimate=pl.CostEstimate(
            flops=5 * 10**9, bytes_accessed=4 * 10**6, transcendentals=3 * 10**6
        ),
        name="attention_stats",
    )(place, counts, *tokens, key_value)


def pack_kernel(place_ref, counts_ref, own_hbm, near_hbm, out_ref, sems):
    section, video_id = place_ref[0], place_ref[1]
    videos = counts_ref.shape[1]
    core = video_id % 2
    sibling = video_id + 1 - 2 * core
    count, count_near = counts_ref[section, video_id], counts_ref[section, sibling]
    start = run_start(counts_ref, section, video_id)
    start_near = jnp.where(core == 0, start + count, start - count_near)
    for act in ("start", "wait"):
        for source, first, size in ((own_hbm, start, count), (near_hbm, start_near, count_near)):
            odd = (core - first) % 2

            @pl.loop(0, MOST_WIN // 2)
            def _(i):
                p = odd + 2 * i
                slot = (first + p) % videos // 2

                @pl.when(p < size)
                def _():
                    copy = pltpu.make_async_copy(source.at[p], out_ref.at[slot], sems.at[slot])
                    copy.start() if act == "start" else copy.wait()


def pack_gradients(place, counts, own, near):
    chips = counts.shape[1] // 2
    return pl.pallas_call(
        pack_kernel,
        out_shape=jax.ShapeDtypeStruct((chips, QUERIES, QDIM), jnp.bfloat16),
        in_specs=[smem(), smem(), anywhere(), anywhere()],
        out_specs=pl.BlockSpec(memory_space=pltpu.VMEM),
        scratch_shapes=[pltpu.SemaphoreType.DMA((chips,))],
        cost_estimate=pl.CostEstimate(
            flops=2 * 10**9, bytes_accessed=4 * 10**6, transcendentals=0
        ),
        name="pack_gradients",
    )(place, counts, own, near)


def unpack_kernel(place_ref, counts_ref, returned_hbm, out_ref, sems):
    section, video_id = place_ref[0], place_ref[1]
    videos = counts_ref.shape[1]

    def take(v, start):
        end = start + counts_ref[section, v]
        window = (start - video_id + 2 * videos - 1) // videos - 1

        @pl.when(window * videos + video_id < end)
        def _():
            pltpu.make_async_copy(
                returned_hbm.at[v // 2], out_ref.at[window], sems.at[window]
            ).start()

        return end

    lax.fori_loop(0, videos, take, jnp.int32(0))
    for window in range(WIN_DEV):
        pltpu.make_async_copy(returned_hbm.at[0], out_ref.at[window], sems.at[window]).wait()


def unpack_gradients(place, counts, returned):
    return pl.pallas_call(
        unpack_kernel,
        out_shape=jax.ShapeDtypeStruct((WIN_DEV, QUERIES, QDIM), jnp.bfloat16),
        in_specs=[smem(), smem(), anywhere()],
        out_specs=pl.BlockSpec(memory_space=pltpu.VMEM),
        scratch_shapes=[pltpu.SemaphoreType.DMA((WIN_DEV,))],
        cost_estimate=pl.CostEstimate(
            flops=2 * 10**9, bytes_accessed=2 * 10**6, transcendentals=0
        ),
        name="unpack_gradients",
    )(place, counts, returned)


RINGS = 4
PART = QDIM // RINGS


def turn_kernel(place_ref, half_ref, kept_ref, given_ref, turned):
    core = place_ref[1] % 2
    turned[...] = half_ref[...].T
    for flip, out_ref in ((core, kept_ref), (1 - core, given_ref)):

        @pl.loop(0, RINGS)
        def _(first):
            for second in range(RINGS):
                for third in range(RINGS):
                    first_at = (place_ref[2 + flip] + first) % RINGS
                    second_at = (place_ref[3 - flip] + second) % RINGS
                    x = jnp.where(flip == 0, first_at, second_at)
                    y = jnp.where(flip == 0, second_at, first_at)
                    z = (place_ref[4] + third) % RINGS
                    chip = ((z % 2 * 2 + z // 2) * RINGS + x) * RINGS + y
                    to = (first * RINGS + second) * RINGS + third
                    out_ref[pl.ds(pl.multiple_of(to * 16, 16), 16), :] = turned[
                        pl.ds(pl.multiple_of(chip * 16, 16), 16), :
                    ]


def turned_memory(place, half):
    out = jax.ShapeDtypeStruct((QDIM, ROWS), jnp.bfloat16)
    return pl.pallas_call(
        turn_kernel,
        out_shape=(out, out),
        in_specs=[smem(), vmem()],
        out_specs=(vmem(), vmem()),
        scratch_shapes=[pltpu.VMEM((QDIM, ROWS), jnp.bfloat16)],
        compiler_params=limit(16),
        cost_estimate=pl.CostEstimate(
            flops=2 * 10**9, bytes_accessed=4 * 10**6, transcendentals=0
        ),
        name="turned_memory",
    )(place, half)


def term_kernel(sibling, place_ref, turned_ref, sum_ref, out_ref):
    core = place_ref[1] % 2
    which = 1 - core if sibling else core
    for step in range(RINGS):
        rows = pl.ds(step * PART, PART)
        out_ref[step] = dot(turned_ref[rows, :], sum_ref[which]).astype(jnp.bfloat16)


def gradient_term(place, turned, d_sum, sibling):
    return pl.pallas_call(
        functools.partial(term_kernel, sibling),
        out_shape=jax.ShapeDtypeStruct((RINGS, PART, INNER), jnp.bfloat16),
        in_specs=[smem(), vmem(), vmem()],
        out_specs=vmem(),
        compiler_params=limit(16),
        cost_estimate=pl.CostEstimate(
            flops=3 * 10**9, bytes_accessed=5 * 10**6, transcendentals=0
        ),
        name="given_term" if sibling else "kept_term",
    )(place, turned, d_sum)


def moved(shifts):
    pairs = []
    for device in range(128):
        core, y, x, z = device % 2, device // 2 % 4, device // 8 % 4, device // 64 + device // 32 % 2 * 2
        first, second, third = shifts
        along = (second, first) if core else (first, second)
        x, y, z = (x + along[0]) % RINGS, (y + along[1]) % RINGS, (z + third) % RINGS
        pairs.append((device, ((z % 2 * 2 + z // 2) * 16 + x * 4 + y) * 2 + core))
    return pairs


def shifted(value, *shifts):
    return lax.ppermute(value.astype(jnp.bfloat16), SECTION_DEV, moved(shifts))


def wider(value):
    return value.astype(jnp.float32)


def summed_terms(kept, got):
    total = [wider(kept[r]) + wider(got[r]) for r in range(RINGS)]
    half = PART // 2
    ahead = shifted(total[2][:half], 1, 0, 0)
    behind = shifted(total[2][half:], RINGS - 1, 0, 0)
    nearer = jnp.concatenate([total[1][:half] + wider(ahead), total[1][half:]], axis=0)
    farther = jnp.concatenate([total[3][:half], total[3][half:] + wider(behind)], axis=0)
    whole = (
        total[0]
        + wider(shifted(nearer, 1, 0, 0))
        + wider(shifted(farther, RINGS - 1, 0, 0))
    )
    total = whole.reshape(RINGS, -1, INNER)
    sent = [wider(shifted(total[r], 0, r, 0)) for r in range(1, RINGS)]
    total = (total[0] + sent[0] + sent[1] + sent[2]).reshape(RINGS, -1, INNER)
    return [total[0]] + [shifted(total[r], 0, 0, r) for r in range(1, RINGS)]


def heads_apart(product):
    both = 2 * CAPLEN
    rows = jnp.concatenate([product[:HEAD_DIM, :both], product[HEAD_DIM:, both:]], axis=0)
    return rows.T


def grads_kernel(
    place_ref,
    counts_ref,
    weight_ref,
    q_own,
    q_other,
    dc_own,
    dc_other,
    kv_ref,
    stats_ref,
    peer_ref,
    context_own,
    context_other,
    dq_own,
    dq_other,
    sum_ref,
    memory_ref,
):
    live = counts_ref[place_ref[0], place_ref[1]] * QUERIES

    @pl.loop(0, PAIRS)
    def _(pair):
        at = columns(pair)
        keys, values = kv_ref[:, at], kv_ref[:, columns(pair, INNER)]

        def mine(which):
            return stats_ref[which, pl.ds(pair, 1), :]

        def theirs(which):
            line = peer_ref[which, pl.ds(pair, 1), :]
            parts = [line[:, 128 * k : 128 * (k + 1)] for k in (1, 0, 3, 2)]
            return jnp.concatenate(parts, axis=1)

        top_mine, top_theirs = mine(0), theirs(0)
        top = jnp.maximum(top_mine, top_theirs)
        grow_mine, grow_theirs = jnp.exp(top_mine - top), jnp.exp(top_theirs - top)
        inverse = 1.0 / (mine(1) * grow_mine + theirs(1) * grow_theirs)
        delta = (mine(2) * grow_mine + theirs(2) * grow_theirs) * inverse

        queries, d_context = stacked(q_own, q_other, at), stacked(dc_own, dc_other, at)
        scores = masked_scores(keys, queries, live)
        probs = jnp.exp(scores - top) * inverse
        weights = probs.astype(jnp.bfloat16)
        d_probs = dot(values, d_context, NT)
        d_scores = (probs * (d_probs - delta)).astype(jnp.bfloat16)
        sum_ref[0, :, at] = dot(d_scores, queries).astype(jnp.bfloat16)
        sum_ref[1, :, at] = dot(weights, d_context).astype(jnp.bfloat16)
        context = heads_apart(dot(values, weights, TN))
        context_own[:, at] = context[:CAPLEN]
        context_other[:, at] = context[CAPLEN:].astype(jnp.bfloat16)
        d_query = heads_apart(dot(keys, d_scores, TN)) * HEAD_DIM ** (-0.5)
        dq_own[:, at] = d_query[:CAPLEN]
        dq_other[:, at] = d_query[CAPLEN:].astype(jnp.bfloat16)

    for c in range(4):
        cut = pl.ds(256 * c, 256)
        product = dot(sum_ref[0], weight_ref[cut, :INNER], NT)
        product += dot(sum_ref[1], weight_ref[cut, INNER:], NT)
        memory_ref[:, cut] = product.astype(jnp.bfloat16)


def attention_grads(place, counts, memory_kv, tokens, key_value, stats, peer):
    wide = jax.ShapeDtypeStruct((CAPLEN, INNER), jnp.float32)
    narrow = jax.ShapeDtypeStruct((CAPLEN, INNER), jnp.bfloat16)
    return pl.pallas_call(
        grads_kernel,
        out_shape=(
            wide,
            narrow,
            wide,
            narrow,
            jax.ShapeDtypeStruct((2, ROWS, INNER), jnp.bfloat16),
            jax.ShapeDtypeStruct((ROWS, QDIM), jnp.bfloat16),
        ),
        in_specs=[smem(), smem()] + [vmem()] * 8,
        out_specs=(vmem(),) * 6,
        compiler_params=limit(24),
        cost_estimate=pl.CostEstimate(
            flops=12 * 10**9, bytes_accessed=10**7, transcendentals=3 * 10**6
        ),
        name="attention_grads",
    )(place, counts, memory_kv, *tokens, key_value, stats, peer)


def local(
    frames,
    window_counts,
    learned_queries,
    frame_kv,
    query_out,
    query_gain,
    captions,
    caption_lengths,
    caption_gain,
    w_query,
    memory_kv,
    w_output,
    upstream,
):
    section = lax.axis_index("section")
    video_id = lax.axis_index(DEV)
    core = lax.axis_index(CORE)
    facts = (
        section,
        video_id,
        lax.axis_index("dev_1"),
        lax.axis_index("dev_2"),
        2 * lax.axis_index("dev_0") + section,
    )
    at = jnp.arange(8, dtype=jnp.int32)
    place = sum(jnp.where(at == k, fact, 0) for k, fact in enumerate(facts))

    sent = compress_windows(
        place, window_counts, frames, learned_queries, frame_kv, query_out, query_gain
    )
    arrived = lax.all_to_all(sent, CHIP, split_axis=0, concat_axis=0, tiled=True)
    captions, upstream, sent = lax.optimization_barrier((captions, upstream, sent))

    source = captions[0, 0].astype(jnp.float32)
    inv_rms = lax.rsqrt(jnp.mean(source * source, axis=-1, keepdims=True) + EPSILON)
    normed = (source * inv_rms * caption_gain).astype(jnp.bfloat16)
    query = jnp.dot(normed, w_query, preferred_element_type=jnp.float32).astype(jnp.bfloat16)
    query = query * jnp.bfloat16(HEAD_DIM ** (-0.5))
    row_live = jnp.arange(CAPLEN, dtype=jnp.int32) < caption_lengths[0, 0]
    grad_out = jnp.where(row_live[:, None], upstream[0, 0], jnp.zeros_like(upstream[0, 0]))
    d_context = jnp.dot(grad_out, w_output.T, preferred_element_type=jnp.float32).astype(
        jnp.bfloat16
    )
    query_other = lax.ppermute(query, "section", SWAP)
    d_context_other = lax.ppermute(d_context, "section", SWAP)

    arrived, query, d_context = lax.optimization_barrier((arrived, query, d_context))
    place = touched(place, memory_kv)
    beside = lax.ppermute(arrived, CORE, SWAP)
    tokens = (query, query_other, d_context, d_context_other)
    half, key_value = project_memory(place, window_counts, arrived, beside, memory_kv)
    stats = attention_stats(place, window_counts, tokens, key_value)
    peer = lax.ppermute(stats, "section", SWAP)
    half, stats = lax.optimization_barrier((half, stats))
    turned_kept, turned_given = turned_memory(place, half)
    peer, turned_kept, turned_given = lax.optimization_barrier((peer, turned_kept, turned_given))
    context_own, context_other, dq_own, dq_other, d_sum, d_memory = attention_grads(
        place, window_counts, memory_kv, tokens, key_value, stats, peer
    )

    d_memory = d_memory.reshape(MOST_WIN, QUERIES, QDIM)
    d_beside = lax.ppermute(d_memory, CORE, SWAP)
    given = gradient_term(place, turned_given, d_sum, True)
    got = lax.ppermute(given, CORE, SWAP)
    d_sum, given = lax.optimization_barrier((d_sum, given))
    kept = gradient_term(place, turned_kept, d_sum, False)
    d_beside, kept = lax.optimization_barrier((d_beside, kept))
    packed = pack_gradients(place, window_counts, d_memory, d_beside)
    packed, context_other, dq_other = lax.optimization_barrier((packed, context_other, dq_other))
    returned = lax.all_to_all(packed, CHIP, split_axis=0, concat_axis=0, tiled=True)
    memory_grad = unpack_gradients(place, window_counts, returned)

    context = (context_own + lax.ppermute(context_other, "section", SWAP)).astype(jnp.bfloat16)
    decoded = (source + jnp.dot(context, w_output, preferred_element_type=jnp.float32)).astype(
        jnp.bfloat16
    )
    d_query = (dq_own + lax.ppermute(dq_other, "section", SWAP)).astype(jnp.bfloat16)
    d_scaled = jnp.dot(d_query, w_query.T, preferred_element_type=jnp.float32) * caption_gain
    caption_grad = grad_out.astype(jnp.float32) + inv_rms * (
        d_scaled - source * inv_rms * inv_rms * jnp.mean(d_scaled * source, axis=-1, keepdims=True)
    )
    caption_grad = caption_grad.astype(jnp.bfloat16)

    own, *sent = summed_terms(kept, got)
    total = (own + wider(sent[0]) + wider(sent[1]) + wider(sent[2])).reshape(2, -1, INNER)
    stays = lax.dynamic_index_in_dim(total, core, 0, keepdims=False)
    leaves = lax.dynamic_index_in_dim(total, 1 - core, 0, keepdims=False)
    comes = lax.ppermute(leaves, CORE, SWAP)
    kv_grad = jnp.where(
        core == 0,
        jnp.concatenate([stays, comes], axis=1),
        jnp.concatenate([comes, stays], axis=1),
    )

    return (
        decoded[None, None],
        caption_grad[None, None],
        memory_grad,
        kv_grad,
    )


def solution(mesh):
    finer = Mesh(
        mesh.devices.reshape(mesh.shape["section"], 2, 4, 4, 2),
        ("section", "dev_0", "dev_1", "dev_2", "dev_3"),
    )
    placed = (
        P(SECTION_DEV, None, None),
        P(),
        P(),
        P(),
        P(),
        P(),
        P("section", DEV, None, None),
        P("section", DEV),
        P(),
        P(),
        P(),
        P(),
        P("section", DEV, None, None),
    )
    return jax.shard_map(
        local,
        mesh=finer,
        in_specs=placed,
        out_specs=(
            P("section", DEV, None, None),
            P("section", DEV, None, None),
            P(SECTION_DEV, None, None),
            P(SECTION_DEV, None),
        ),
        check_vma=False,
    )
```

time: 246 us -> 171 us (0.70)
  the two profiles are of different devices: /device:TPU:64 before, /device:TPU:1 now
where the time goes in v2:
time: 171 us; the launch traced here: 170 us
  Pallas kernels  54.4 us (32%)
  waiting for transfers between devices  50.8 us (30%)
  starting transfers between devices  41.3 us (24%)
  matrix products  10.2 us (6%)
  other arithmetic  8.24 us (5%)
  local copies, waits for them, and re-layouts  3.43 us (2%)
  between operations  1.89 us (1%)
    ppermute x10, waiting for transfers between devices, shifted(): return lax.ppermute(value.astype(jnp.bfloat16), SECTION_DEV, moved(shifts))  23.5 us
    all_to_all x1, waiting for transfers between devices, local(): lax.all_to_all(sent, CHIP, split_axis=0, concat_axis=0, tiled=True)  22.5 us
    ppermute x10, starting transfers between devices, shifted(): return lax.ppermute(value.astype(jnp.bfloat16), SECTION_DEV, moved(shifts))  15.2 us
    pallas_call x1, Pallas kernels, attention_grads(): pl.pallas_call(grads_kernel, out_shape=(wide, narrow, wide, narrow, jax.S...  13.1 us
    pallas_call x1, Pallas kernels, compress_windows(): pl.pallas_call(compress_kernel, out_shape=jax.ShapeDtypeStruct((chips, QU...  11.5 us
    all_to_all x1, starting transfers between devices, local(): lax.all_to_all(sent, CHIP, split_axis=0, concat_axis=0, tiled=True)  11.3 us
    pallas_call x1, Pallas kernels, project_memory(): pl.pallas_call(project_kernel, out_shape=(jax.ShapeDtypeStruct((ROWS, QDI...  6.41 us
    pallas_call x2, Pallas kernels, gradient_term(): pl.pallas_call(functools.partial(term_kernel, sibling), out_shape=jax.Sha...  6.06 us
  transfers between devices with their start and end apart: 21, of which 7 were waited for; matrix products, arithmetic and copies ran while one was open for 11% of the time, Pallas kernels for 10%

profile of v2, /device:TPU:1, one launch (start us, length us, event | category | flops | bytes accessed | tf_op | source)
XLA Modules:
  0.0 170.3 jit_solution(14347116914421714257)
XLA Ops:
  1.2 11.5 %compress_windows.1 = bf16[32,32,1024]{2,1,0:T(8,128)(2,1)} custom-call(s32[8]{0:T(128)} %fusion.33.place_ref, s32[2,64]{1,0:T(2,128)} %counts_ref.11, bf16[32,1024]{1,0:T(8,128)(2,1)} %queries_ref.1, f32[1,1024]{1,0:T(1,128)} %bitcast.62, bf16[512,1024]{1,0:T(8,128)(2,1)} %bitcast.61, bf16[1024,2048]{1,0:T(8,128)(2,1)} %weight_hbm.1, bf16[1024,1024]{1,0:T(8,128)(2,1)} %out_hbm.1), custom_call_target="tpu_custom_call" | custom-call | flops 6000000000 | bytes 9000000 | tf_op jit(solution)/shard_map/compress_windows/pallas_call | solution.py:172
  12.7 11.3 %all-to-all-start = ((bf16[32,32,1024]{2,1,0:T(8,128)(2,1)}), bf16[32,32,1024]{2,1,0:T(8,128)(2,1)S(1)}, u32[]{:S(2)}, u32[]{:S(2)}) async-start(bf16[32,32,1024]{2,1,0:T(8,128)(2,1)} %compress_windows.1), calls=%async_computation | async-start | bytes 4194304 | tf_op jit(solution)/shard_map/all_to_all | solution.py:613
  24.9 3.9 %convolution_convert_fusion.dc_own = bf16[128,1024]{1,0:T(8,128)(2,1)S(1)} fusion(bf16[1024,2048]{1,0:T(8,128)(2,1)} %param.24, bf16[1,1,128,2048]{3,2,1,0:T(8,128)(2,1)S(1)} %copy-done.14, pred[128]{0:T(512)(128)(4,1)S(1)} %iota_compare_fusion), kind=kOutput, calls=%fused_computation.9 | convolution fusion | flops 537264128 | bytes 4980864 | tf_op jit(solution)/shard_map/dot_general | solution.py:623
  29.6 22.5 %all-to-all-done.arrived_ref = bf16[32,32,1024]{2,1,0:T(8,128)(2,1)S(1)} async-done(((bf16[32,32,1024]{2,1,0:T(8,128)(2,1)}), bf16[32,32,1024]{2,1,0:T(8,128)(2,1)S(1)}, u32[]{:S(2)}, u32[]{:S(2)}) %all-to-all-start) | async-done | bytes 2097184 | tf_op jit(solution)/shard_map/all_to_all | solution.py:613
  52.1 1.8 %collective-permute-start.2 = (bf16[32,32,1024]{2,1,0:T(8,128)(2,1)S(1)}, bf16[32,32,1024]{2,1,0:T(8,128)(2,1)S(1)}, u32[]{:S(2)}, u32[]{:S(2)}) collective-permute-start(bf16[32,32,1024]{2,1,0:T(8,128)(2,1)S(1)} %all-to-all-done.arrived_ref), channel_id=1, source_target_pairs={{0,1},{1,0},{2,3},{3,2},{4,5},{5,4},{6,7},{7,6},{8,9},{9,8},{10,11... | collective-permute-start | bytes 6291464 | tf_op jit(solution)/shard_map/ppermute | solution.py:631
  55.4 2.2 %copy-done = bf16[1024,2048]{1,0:T(8,128)(2,1)S(1)} copy-done((bf16[1024,2048]{1,0:T(8,128)(2,1)S(1)}, bf16[1024,2048]{1,0:T(8,128)(2,1)}, u32[]{:S(2)}) %copy-start) | copy-done | bytes 4194328
  59.8 6.4 %project_memory.1 = (bf16[640,1024]{1,0:T(8,128)(2,1)S(1)}, bf16[640,2048]{1,0:T(8,128)(2,1)S(1)}) custom-call(s32[8]{0:T(128)S(1)} %touched.1.place_ref, s32[2,64]{1,0:T(2,128)S(1)} %copy-done.9, bf16[32,32,1024]{2,1,0:T(8,128)(2,1)S(1)} %all-to-all-done.arrived_ref, bf16[32,32,1024]{2,1,0:T(8,128)(2,1)S(1)} %collective-permute-done.2.beside_ref, ...), custom_call_target="tpu_custom_call" | custom-call | flops 5000000000 | bytes 10000000 | tf_op jit(solution)/shard_map/project_memory/pallas_call | solution.py:270
  66.2 1.2 collective-permute-done.1.dc_other
  67.5 5.1 %attention_stats.1.stats_ref = f32[3,8,512]{2,1,0:T(8,128)S(1)} custom-call(s32[8]{0:T(128)S(1)} %touched.1.place_ref, s32[2,64]{1,0:T(2,128)S(1)} %copy-done.9, bf16[128,1024]{1,0:T(8,128)(2,1)S(1)} %fusion.4.q_own, bf16[128,1024]{1,0:T(8,128)(2,1)S(1)} %collective-permute-done.q_other, bf16[128,1024]{1,0:T(8,128)(2,1)S(1)} %convolution_convert_fusion.dc_own, ...), custom_call_target="tpu_custom_call" | custom-call | flops 5000000000 | bytes 4000000 | tf_op jit(solution)/shard_map/attention_stats/pallas_call | solution.py:306
  73.5 3.1 %turned_memory.1 = (bf16[1024,640]{1,0:T(8,128)(2,1)S(1)}, bf16[1024,640]{1,0:T(8,128)(2,1)S(1)}) custom-call(s32[8]{0:T(128)S(1)} %touched.1.place_ref, bf16[640,1024]{1,0:T(8,128)(2,1)S(1)} %get-tuple-element.38.half_ref), custom_call_target="tpu_custom_call" | custom-call | flops 2000000000 | bytes 4000000 | tf_op jit(solution)/shard_map/turned_memory/pallas_call | solution.py:419
  76.7 13.1 %attention_grads.1 = (f32[128,1024]{1,0:T(8,128)S(1)}, bf16[128,1024]{1,0:T(8,128)(2,1)S(1)}, f32[128,1024]{1,0:T(8,128)S(1)}, bf16[128,1024]{1,0:T(8,128)(2,1)}...) custom-call(s32[8]{0:T(128)S(1)} %touched.1.place_ref, s32[2,64]{1,0:T(2,128)S(1)} %copy-done.9, ...), custom_call_target="tpu_custom_call" | custom-call | flops 12000000000 | bytes 10000000 | tf_op jit(solution)/shard_map/attention_grads/pallas_call | solution.py:562
  89.8 3.7 %given_term.1 = bf16[4,256,1024]{2,1,0:T(8,128)(2,1)} custom-call(s32[8]{0:T(128)S(1)} %touched.1.place_ref, bf16[1024,640]{1,0:T(8,128)(2,1)S(1)} %get-tuple-element.46.turned_ref, bf16[2,640,1024]{2,1,0:T(8,128)(2,1)S(1)} %get-tuple-element.47.sum_ref), custom_call_target="tpu_custom_call" | custom-call | flops 3000000000 | bytes 5000000 | tf_op jit(solution)/shard_map/given_term/pallas_call | solution.py:442
  94.7 2.3 %kept_term.1 = bf16[4,256,1024]{2,1,0:T(8,128)(2,1)S(1)} custom-call(s32[8]{0:T(128)S(1)} %touched.1.place_ref, bf16[1024,640]{1,0:T(8,128)(2,1)S(1)} %get-tuple-element.44.turned_ref, bf16[2,640,1024]{2,1,0:T(8,128)(2,1)S(1)} %get-tuple-element.47.sum_ref), custom_call_target="tpu_custom_call" | custom-call | flops 3000000000 | bytes 5000000 | tf_op jit(solution)/shard_map/kept_term/pallas_call | solution.py:442
  97.1 3.6 %collective-permute-done.4.near_hbm = bf16[20,32,1024]{2,1,0:T(8,128)(2,1)} collective-permute-done((bf16[20,32,1024]{2,1,0:T(8,128)(2,1)S(1)}, bf16[20,32,1024]{2,1,0:T(8,128)(2,1)}, u32[]{:S(2)}, u32[]{:S(2)}) %collective-permute-start.4) | collective-permute-done | bytes 1310752 | tf_op jit(solution)/shard_map/ppermute | solution.py:644
  100.7 4.1 %pack_gradients.1 = bf16[32,32,1024]{2,1,0:T(8,128)(2,1)} custom-call(s32[8]{0:T(128)} %copy-done.5, s32[2,64]{1,0:T(2,128)} %counts_ref.11, bf16[20,32,1024]{2,1,0:T(8,128)(2,1)} %bitcast.60, bf16[20,32,1024]{2,1,0:T(8,128)(2,1)} %collective-permute-done.4.near_hbm), custom_call_target="tpu_custom_call" | custom-call | flops 2000000000 | bytes 4000000 | tf_op jit(solution)/shard_map/pack_gradients/pallas_call | solution.py:344
  105.7 2.0 %convert_add_fusion.1 = (f32[1,256,1024]{2,1,0:T(8,128)S(1)}, f32[1,256,1024]{2,1,0:T(8,128)S(1)}, bf16[1,256,1024]{2,1,0:T(8,128)(2,1)S(1)}) fusion(bf16[4,256,1024]{2,1,0:T(8,128)(2,1)} %collective-permute-done.7, bf16[4,256,1024]{2,1,0:T(8,128)(2,1)S(1)} %kept_term.1), kind=kLoop, calls=%fused_computation.24 | loop fusion | flops 2621440 | bytes 5767168 | tf_op jit(solution)/shard_map/add | solution.py:475
  108.9 1.6 collective-permute-start.10
  110.6 3.9 %collective-permute-done.8 = bf16[128,1024]{1,0:T(8,128)(2,1)S(1)} collective-permute-done((bf16[128,1024]{1,0:T(8,128)(2,1)S(1)}, bf16[128,1024]{1,0:T(8,128)(2,1)S(1)}, u32[]{:S(2)}, u32[]{:S(2)}) %collective-permute-start.8) | collective-permute-done | bytes 262176 | tf_op jit(solution)/shard_map/ppermute | solution.py:467
  116.3 2.7 %collective-permute-start.11 = (bf16[256,1024]{1,0:T(8,128)(2,1)}, bf16[256,1024]{1,0:T(8,128)(2,1)}, u32[]{:S(2)}, u32[]{:S(2)}) collective-permute-start(bf16[256,1024]{1,0:T(8,128)(2,1)} %pad_maximum_fusion.1), channel_id=1, source_target_pairs={{0,24},{1,7},{2,26},{3,1},{4,28},{5,3},{6,30},{7,5},{8,0},{9,15},{... | collective-permute-start | bytes 1572872 | tf_op jit(solution)/shard_map/ppermute | solution.py:467
  119.0 5.7 %all-to-all-start.1 = ((bf16[32,32,1024]{2,1,0:T(8,128)(2,1)}), bf16[32,32,1024]{2,1,0:T(8,128)(2,1)}, u32[]{:S(2)}, u32[]{:S(2)}) async-start(bf16[32,32,1024]{2,1,0:T(8,128)(2,1)} %pack_gradients.1), calls=%async_computation.1 | async-start | bytes 4194304 | tf_op jit(solution)/shard_map/all_to_all | solution.py:652
  125.2 4.0 %fusion.12 = (f32[128]{0:T(128)S(1)}, f32[128,2048]{1,0:T(8,128)S(1)}) fusion(bf16[1,1,128,2048]{3,2,1,0:T(8,128)(2,1)} %param.19, f32[2048]{0:T(1024)S(1)} %copy-done.16, bf16[2048,1024]{1,0:T(8,128)(2,1)} %param.22, f32[128,1024]{1,0:T(8,128)S(1)} %get-tuple-element.52, bf16[128,1024]{1,0:T(8,128)(2,1)} %collective-permute-done.6), kind=kOutput, calls=%fused_computation.19 | convolution fusion | flops 538312576 | bytes 6562304 | tf_op jit(solution)/shard_map/dot_general | solution.py:660
  129.2 1.8 %fusion.37 = (bf16[256,1024]{1,0:T(8,128)(2,1)S(1)}, f32[256,1024]{1,0:T(8,128)S(1)}) fusion(bf16[256,1024]{1,0:T(8,128)(2,1)} %collective-permute-done.11, bf16[256,1024]{1,0:T(8,128)(2,1)} %collective-permute-done.9, bf16[4,256,1024]{2,1,0:T(8,128)(2,1)} %collective-permute-done.7, bf16[4,256,1024]{2,1,0:T(8,128)(2,1)S(1)} %kept_term.1), kind=kLoop, calls=%fused_computation.70 | loop fusion | flops 2097152 | bytes 3670016 | tf_op jit(solution)/shard_map/convert.6
  131.1 1.2 collective-permute-start.12
  132.3 2.4 %collective-permute-start.13 = (bf16[64,1024]{1,0:T(8,128)(2,1)S(1)}, bf16[64,1024]{1,0:T(8,128)(2,1)S(1)}, u32[]{:S(2)}, u32[]{:S(2)}) collective-permute-start(bf16[64,1024]{1,0:T(8,128)(2,1)S(1)} %get-tuple-element.65), channel_id=1, source_target_pairs={{0,4},{1,17},{2,6},{3,19},{4,0},{5,21},{6,2},{7,23},{8,12},{9,25},... | collective-permute-start | bytes 393224 | tf_op jit(solution)/shard_map/ppermute | solution.py:467
  134.7 1.2 collective-permute-start.14
  135.9 16.4 %collective-permute-done.12 = bf16[64,1024]{1,0:T(8,128)(2,1)S(1)} collective-permute-done((bf16[64,1024]{1,0:T(8,128)(2,1)S(1)}, bf16[64,1024]{1,0:T(8,128)(2,1)S(1)}, u32[]{:S(2)}, u32[]{:S(2)}) %collective-permute-start.12) | collective-permute-done | bytes 131104 | tf_op jit(solution)/shard_map/ppermute | solution.py:467
  152.3 2.1 %collective-permute-done.13 = bf16[64,1024]{1,0:T(8,128)(2,1)S(1)} collective-permute-done((bf16[64,1024]{1,0:T(8,128)(2,1)S(1)}, bf16[64,1024]{1,0:T(8,128)(2,1)S(1)}, u32[]{:S(2)}, u32[]{:S(2)}) %collective-permute-start.13) | collective-permute-done | bytes 131104 | tf_op jit(solution)/shard_map/ppermute | solution.py:467
  154.9 3.7 %collective-permute-start.16 = (bf16[16,1024]{1,0:T(8,128)(2,1)S(1)}, bf16[16,1024]{1,0:T(8,128)(2,1)S(1)}, u32[]{:S(2)}, u32[]{:S(2)}) collective-permute-start(bf16[16,1024]{1,0:T(8,128)(2,1)S(1)} %get-tuple-element.70), channel_id=1, source_target_pairs={{0,32},{1,33},{2,34},{3,35},{4,36},{5,37},{6,38},{7,39},{8,40},{9,... | collective-permute-start | bytes 98312 | tf_op jit(solution)/shard_map/ppermute | solution.py:467
  159.4 1.2 fusion.14
  161.8 2.2 %collective-permute-start.18 = (f32[8,1024]{1,0:T(8,128)S(1)}, f32[8,1024]{1,0:T(8,128)S(1)}, u32[]{:S(2)}, u32[]{:S(2)}) collective-permute-start(f32[8,1024]{1,0:T(8,128)S(1)} %get-tuple-element.72), channel_id=1, source_target_pairs={{0,1},{1,0},{2,3},{3,2},{4,5},{5,4},{6,7},{7,6},{8,9},{9,8},{10,11... | collective-permute-start | bytes 98312 | tf_op jit(solution)/shard_map/ppermute | solution.py:670
  164.0 1.6 fusion.1
  166.3 3.9 %unpack_gradients.1 = bf16[16,32,1024]{2,1,0:T(8,128)(2,1)} custom-call(s32[8]{0:T(128)} %copy-done.5, s32[2,64]{1,0:T(2,128)} %counts_ref.11, bf16[32,32,1024]{2,1,0:T(8,128)(2,1)} %all-to-all-done.1.returned_hbm), custom_call_target="tpu_custom_call" | custom-call | flops 2000000000 | bytes 2000000 | tf_op jit(solution)/shard_map/unpack_gradients/pallas_call | solution.py:379
  (79 shorter events, 15.1 us)
Async XLA Ops:
  12.7 12.0 %copy-start.12 = (bf16[1,1,128,2048]{3,2,1,0:T(8,128)(2,1)S(1)}, bf16[1,1,128,2048]{3,2,1,0:T(8,128)(2,1)}, u32[]{:S(2)}) copy-start(bf16[1,1,128,2048]{3,2,1,0:T(8,128)(2,1)} %param.19) | copy-start | bytes 1572868
  12.7 12.2 %copy-start.14 = (bf16[1,1,128,2048]{3,2,1,0:T(8,128)(2,1)S(1)}, bf16[1,1,128,2048]{3,2,1,0:T(8,128)(2,1)}, u32[]{:S(2)}) copy-start(bf16[1,1,128,2048]{3,2,1,0:T(8,128)(2,1)} %param.25) | copy-start | bytes 1572868
  12.7 39.5 %all-to-all-start = ((bf16[32,32,1024]{2,1,0:T(8,128)(2,1)}), bf16[32,32,1024]{2,1,0:T(8,128)(2,1)S(1)}, u32[]{:S(2)}, u32[]{:S(2)}) async-start(bf16[32,32,1024]{2,1,0:T(8,128)(2,1)} %compress_windows.1), calls=%async_computation | async-start | bytes 4194304 | tf_op jit(solution)/shard_map/all_to_all | solution.py:613
  28.8 26.6 %copy-start.4 = (s32[8]{0:T(128)S(1)}, s32[8]{0:T(128)}, u32[]{:S(2)}) copy-start(s32[8]{0:T(128)} %fusion.33.place_ref) | copy-start | bytes 100
  28.8 30.0 %copy-start.9 = (s32[2,64]{1,0:T(2,128)S(1)}, s32[2,64]{1,0:T(2,128)}, u32[]{:S(2)}) copy-start(s32[2,64]{1,0:T(2,128)} %counts_ref.11) | copy-start | bytes 1540
  29.6 37.8 %copy-start.2 = (bf16[128,1024]{1,0:T(8,128)(2,1)}, bf16[128,1024]{1,0:T(8,128)(2,1)S(1)}, u32[]{:S(2)}) copy-start(bf16[128,1024]{1,0:T(8,128)(2,1)S(1)} %fusion.4.q_own) | copy-start | bytes 786436
  52.1 6.6 %collective-permute-start.2 = (bf16[32,32,1024]{2,1,0:T(8,128)(2,1)S(1)}, bf16[32,32,1024]{2,1,0:T(8,128)(2,1)S(1)}, u32[]{:S(2)}, u32[]{:S(2)}) collective-permute-start(bf16[32,32,1024]{2,1,0:T(8,128)(2,1)S(1)} %all-to-all-done.arrived_ref), channel_id=1, source_target_pairs={{0,1},{1,0},{2,3},{3,2},{4,5},{5,4},{6,7},{7,6},{8,9},{9,8},{10,11... | collective-permute-start | bytes 6291464 | tf_op jit(solution)/shard_map/ppermute | solution.py:631
  54.0 12.3 %collective-permute-start = (bf16[128,1024]{1,0:T(8,128)(2,1)S(1)}, bf16[128,1024]{1,0:T(8,128)(2,1)S(1)}, u32[]{:S(2)}, u32[]{:S(2)}) collective-permute-start(bf16[128,1024]{1,0:T(8,128)(2,1)S(1)} %fusion.4.q_own), channel_id=1, source_target_pairs={{0,64},{64,0},{1,65},{65,1},{2,66},{66,2},{3,67},{67,3},{4,68},{68... | collective-permute-start | bytes 786440 | tf_op jit(solution)/shard_map/ppermute | solution.py:626
  54.7 12.7 %collective-permute-start.1 = (bf16[128,1024]{1,0:T(8,128)(2,1)S(1)}, bf16[128,1024]{1,0:T(8,128)(2,1)S(1)}, u32[]{:S(2)}, u32[]{:S(2)}) collective-permute-start(bf16[128,1024]{1,0:T(8,128)(2,1)S(1)} %convolution_convert_fusion.dc_own), channel_id=1, source_target_pairs={{0,64},{64,0},{1,65},{65,1},{2,66},{66,2},{3,67},{67,3},{4,68},{68... | collective-permute-start | bytes 786440 | tf_op jit(solution)/shard_map/ppermute | solution.py:627
  58.8 36.0 %copy-start.5 = (s32[8]{0:T(128)}, s32[8]{0:T(128)S(1)}, u32[]{:S(2)}) copy-start(s32[8]{0:T(128)S(1)} %touched.1.place_ref) | copy-start | bytes 100
  72.5 4.1 %collective-permute-start.3 = (f32[3,8,512]{2,1,0:T(8,128)S(1)}, f32[3,8,512]{2,1,0:T(8,128)S(1)}, u32[]{:S(2)}, u32[]{:S(2)}) collective-permute-start(f32[3,8,512]{2,1,0:T(8,128)S(1)} %attention_stats.1.stats_ref), channel_id=1, source_target_pairs={{0,64},{64,0},{1,65},{65,1},{2,66},{66,2},{3,67},{67,3},{4,68},{68... | collective-permute-start | bytes 147464 | tf_op jit(solution)/shard_map/ppermute | solution.py:635
  89.8 4.9 %copy-start.6 = (bf16[640,1024]{1,0:T(8,128)(2,1)}, bf16[640,1024]{1,0:T(8,128)(2,1)S(1)}, u32[]{:S(2)}) copy-start(bf16[640,1024]{1,0:T(8,128)(2,1)S(1)} %get-tuple-element.43) | copy-start | bytes 3932164
  93.5 12.2 %collective-permute-start.7 = (bf16[4,256,1024]{2,1,0:T(8,128)(2,1)}, bf16[4,256,1024]{2,1,0:T(8,128)(2,1)}, u32[]{:S(2)}, u32[]{:S(2)}) collective-permute-start(bf16[4,256,1024]{2,1,0:T(8,128)(2,1)} %given_term.1), channel_id=1, source_target_pairs={{0,1},{1,0},{2,3},{3,2},{4,5},{5,4},{6,7},{7,6},{8,9},{9,8},{10,11... | collective-permute-start | bytes 6291464 | tf_op jit(solution)/shard_map/ppermute | solution.py:646
  94.7 6.0 %collective-permute-start.4 = (bf16[20,32,1024]{2,1,0:T(8,128)(2,1)S(1)}, bf16[20,32,1024]{2,1,0:T(8,128)(2,1)}, u32[]{:S(2)}, u32[]{:S(2)}) collective-permute-start(bf16[20,32,1024]{2,1,0:T(8,128)(2,1)S(1)} %bitcast.59), channel_id=1, source_target_pairs={{0,1},{1,0},{2,3},{3,2},{4,5},{5,4},{6,7},{7,6},{8,9},{9,8},{10,11... | collective-permute-start | bytes 3932168 | tf_op jit(solution)/shard_map/ppermute | solution.py:644
  104.8 20.4 %collective-permute-start.6 = (bf16[128,1024]{1,0:T(8,128)(2,1)}, bf16[128,1024]{1,0:T(8,128)(2,1)}, u32[]{:S(2)}, u32[]{:S(2)}) collective-permute-start(bf16[128,1024]{1,0:T(8,128)(2,1)} %get-tuple-element.53), channel_id=1, source_target_pairs={{0,64},{64,0},{1,65},{65,1},{2,66},{66,2},{3,67},{67,3},{4,68},{68... | collective-permute-start | bytes 786440 | tf_op jit(solution)/shard_map/ppermute | solution.py:659
  107.7 6.8 %collective-permute-start.8 = (bf16[128,1024]{1,0:T(8,128)(2,1)S(1)}, bf16[128,1024]{1,0:T(8,128)(2,1)S(1)}, u32[]{:S(2)}, u32[]{:S(2)}) collective-permute-start(bf16[128,1024]{1,0:T(8,128)(2,1)S(1)} %get-tuple-element.66), channel_id=1, source_target_pairs={{0,8},{1,3},{2,10},{3,5},{4,12},{5,7},{6,14},{7,1},{8,16},{9,11},{... | collective-permute-start | bytes 786440 | tf_op jit(solution)/shard_map/ppermute | solution.py:467
  108.9 6.5 %collective-permute-start.10 = (bf16[128,1024]{1,0:T(8,128)(2,1)S(1)}, bf16[128,1024]{1,0:T(8,128)(2,1)S(1)}, u32[]{:S(2)}, u32[]{:S(2)}) collective-permute-start(bf16[128,1024]{1,0:T(8,128)(2,1)S(1)} %get-tuple-element.67), channel_id=1, source_target_pairs={{0,24},{1,7},{2,26},{3,1},{4,28},{5,3},{6,30},{7,5},{8,0},{9,15},{... | collective-permute-start | bytes 786440 | tf_op jit(solution)/shard_map/ppermute | solution.py:467
  115.4 13.8 %collective-permute-start.9 = (bf16[256,1024]{1,0:T(8,128)(2,1)}, bf16[256,1024]{1,0:T(8,128)(2,1)}, u32[]{:S(2)}, u32[]{:S(2)}) collective-permute-start(bf16[256,1024]{1,0:T(8,128)(2,1)} %pad_maximum_fusion), channel_id=1, source_target_pairs={{0,8},{1,3},{2,10},{3,5},{4,12},{5,7},{6,14},{7,1},{8,16},{9,11},{... | collective-permute-start | bytes 1572872 | tf_op jit(solution)/shard_map/ppermute | solution.py:467
  115.5 9.2 %copy-start.8 = (bf16[128,1024]{1,0:T(8,128)(2,1)S(1)}, bf16[128,1024]{1,0:T(8,128)(2,1)}, u32[]{:S(2)}) copy-start(bf16[128,1024]{1,0:T(8,128)(2,1)} %copy-done.7) | copy-start | bytes 786436
  116.3 12.9 %collective-permute-start.11 = (bf16[256,1024]{1,0:T(8,128)(2,1)}, bf16[256,1024]{1,0:T(8,128)(2,1)}, u32[]{:S(2)}, u32[]{:S(2)}) collective-permute-start(bf16[256,1024]{1,0:T(8,128)(2,1)} %pad_maximum_fusion.1), channel_id=1, source_target_pairs={{0,24},{1,7},{2,26},{3,1},{4,28},{5,3},{6,30},{7,5},{8,0},{9,15},{... | collective-permute-start | bytes 1572872 | tf_op jit(solution)/shard_map/ppermute | solution.py:467
  119.0 47.2 %all-to-all-start.1 = ((bf16[32,32,1024]{2,1,0:T(8,128)(2,1)}), bf16[32,32,1024]{2,1,0:T(8,128)(2,1)}, u32[]{:S(2)}, u32[]{:S(2)}) async-start(bf16[32,32,1024]{2,1,0:T(8,128)(2,1)} %pack_gradients.1), calls=%async_computation.1 | async-start | bytes 4194304 | tf_op jit(solution)/shard_map/all_to_all | solution.py:652
  124.7 39.3 %collective-permute-start.5 = (bf16[128,1024]{1,0:T(8,128)(2,1)S(1)}, bf16[128,1024]{1,0:T(8,128)(2,1)S(1)}, u32[]{:S(2)}, u32[]{:S(2)}) collective-permute-start(bf16[128,1024]{1,0:T(8,128)(2,1)S(1)} %copy-done.8), channel_id=1, source_target_pairs={{0,64},{64,0},{1,65},{65,1},{2,66},{66,2},{3,67},{67,3},{4,68},{68... | collective-permute-start | bytes 786440 | tf_op jit(solution)/shard_map/ppermute | solution.py:655
  129.2 30.2 %copy-start.13 = (bf16[1,1,128,2048]{3,2,1,0:T(8,128)(2,1)S(1)}, bf16[1,1,128,2048]{3,2,1,0:T(8,128)(2,1)}, u32[]{:S(2)}) copy-start(bf16[1,1,128,2048]{3,2,1,0:T(8,128)(2,1)} %param.19) | copy-start | bytes 1572868
  129.2 30.2 %copy-start.15 = (bf16[1,1,128,2048]{3,2,1,0:T(8,128)(2,1)S(1)}, bf16[1,1,128,2048]{3,2,1,0:T(8,128)(2,1)}, u32[]{:S(2)}) copy-start(bf16[1,1,128,2048]{3,2,1,0:T(8,128)(2,1)} %param.25) | copy-start | bytes 1572868
  131.0 33.0 %copy-start.11 = (bf16[1024,2048]{1,0:T(8,128)(2,1)S(1)}, bf16[1024,2048]{1,0:T(8,128)(2,1)}, u32[]{:S(2)}) copy-start(bf16[1024,2048]{1,0:T(8,128)(2,1)} %param.24) | copy-start | bytes 12582916
  131.1 21.2 %collective-permute-start.12 = (bf16[64,1024]{1,0:T(8,128)(2,1)S(1)}, bf16[64,1024]{1,0:T(8,128)(2,1)S(1)}, u32[]{:S(2)}, u32[]{:S(2)}) collective-permute-start(bf16[64,1024]{1,0:T(8,128)(2,1)S(1)} %get-tuple-element.63), channel_id=1, source_target_pairs={{0,2},{1,9},{2,4},{3,11},{4,6},{5,13},{6,0},{7,15},{8,10},{9,17},{... | collective-permute-start | bytes 393224 | tf_op jit(solution)/shard_map/ppermute | solution.py:467
  132.3 22.1 %collective-permute-start.13 = (bf16[64,1024]{1,0:T(8,128)(2,1)S(1)}, bf16[64,1024]{1,0:T(8,128)(2,1)S(1)}, u32[]{:S(2)}, u32[]{:S(2)}) collective-permute-start(bf16[64,1024]{1,0:T(8,128)(2,1)S(1)} %get-tuple-element.65), channel_id=1, source_target_pairs={{0,4},{1,17},{2,6},{3,19},{4,0},{5,21},{6,2},{7,23},{8,12},{9,25},... | collective-permute-start | bytes 393224 | tf_op jit(solution)/shard_map/ppermute | solution.py:467
  134.7 19.7 %collective-permute-start.14 = (bf16[64,1024]{1,0:T(8,128)(2,1)S(1)}, bf16[64,1024]{1,0:T(8,128)(2,1)S(1)}, u32[]{:S(2)}, u32[]{:S(2)}) collective-permute-start(bf16[64,1024]{1,0:T(8,128)(2,1)S(1)} %get-tuple-element.64), channel_id=1, source_target_pairs={{0,6},{1,25},{2,0},{3,27},{4,2},{5,29},{6,4},{7,31},{8,14},{9,1},{... | collective-permute-start | bytes 393224 | tf_op jit(solution)/shard_map/ppermute | solution.py:467
  154.5 6.1 %collective-permute-start.15 = (bf16[16,1024]{1,0:T(8,128)(2,1)S(1)}, bf16[16,1024]{1,0:T(8,128)(2,1)S(1)}, u32[]{:S(2)}, u32[]{:S(2)}) collective-permute-start(bf16[16,1024]{1,0:T(8,128)(2,1)S(1)} %get-tuple-element.68), channel_id=1, source_target_pairs={{0,64},{1,65},{2,66},{3,67},{4,68},{5,69},{6,70},{7,71},{8,72},{9,... | collective-permute-start | bytes 98312 | tf_op jit(solution)/shard_map/ppermute | solution.py:467
  154.9 5.7 %collective-permute-start.16 = (bf16[16,1024]{1,0:T(8,128)(2,1)S(1)}, bf16[16,1024]{1,0:T(8,128)(2,1)S(1)}, u32[]{:S(2)}, u32[]{:S(2)}) collective-permute-start(bf16[16,1024]{1,0:T(8,128)(2,1)S(1)} %get-tuple-element.70), channel_id=1, source_target_pairs={{0,32},{1,33},{2,34},{3,35},{4,36},{5,37},{6,38},{7,39},{8,40},{9,... | collective-permute-start | bytes 98312 | tf_op jit(solution)/shard_map/ppermute | solution.py:467
  158.6 3.2 %collective-permute-start.17 = (bf16[16,1024]{1,0:T(8,128)(2,1)S(1)}, bf16[16,1024]{1,0:T(8,128)(2,1)S(1)}, u32[]{:S(2)}, u32[]{:S(2)}) collective-permute-start(bf16[16,1024]{1,0:T(8,128)(2,1)S(1)} %get-tuple-element.69), channel_id=1, source_target_pairs={{0,96},{1,97},{2,98},{3,99},{4,100},{5,101},{6,102},{7,103},{8,104... | collective-permute-start | bytes 98312 | tf_op jit(solution)/shard_map/ppermute | solution.py:467
  161.8 3.8 %collective-permute-start.18 = (f32[8,1024]{1,0:T(8,128)S(1)}, f32[8,1024]{1,0:T(8,128)S(1)}, u32[]{:S(2)}, u32[]{:S(2)}) collective-permute-start(f32[8,1024]{1,0:T(8,128)S(1)} %get-tuple-element.72), channel_id=1, source_target_pairs={{0,1},{1,0},{2,3},{3,2},{4,5},{5,4},{6,7},{7,6},{8,9},{9,8},{10,11... | collective-permute-start | bytes 98312 | tf_op jit(solution)/shard_map/ppermute | solution.py:670
  (6 other events, 19.1 us)

commit v3 on v2

--- a/solution.py
+++ b/solution.py
@@ -471,22 +471,66 @@
     return value.astype(jnp.float32)
 
 
-def summed_terms(kept, got):
-    total = [wider(kept[r]) + wider(got[r]) for r in range(RINGS)]
+def far_kernel(kept_ref, got_ref, ahead_ref, behind_ref):
     half = PART // 2
-    ahead = shifted(total[2][:half], 1, 0, 0)
-    behind = shifted(total[2][half:], RINGS - 1, 0, 0)
-    nearer = jnp.concatenate([total[1][:half] + wider(ahead), total[1][half:]], axis=0)
-    farther = jnp.concatenate([total[3][:half], total[3][half:] + wider(behind)], axis=0)
-    whole = (
-        total[0]
-        + wider(shifted(nearer, 1, 0, 0))
-        + wider(shifted(farther, RINGS - 1, 0, 0))
-    )
-    total = whole.reshape(RINGS, -1, INNER)
-    sent = [wider(shifted(total[r], 0, r, 0)) for r in range(1, RINGS)]
-    total = (total[0] + sent[0] + sent[1] + sent[2]).reshape(RINGS, -1, INNER)
-    return [total[0]] + [shifted(total[r], 0, 0, r) for r in range(1, RINGS)]
+    for rows, out_ref in ((pl.ds(0, half), ahead_ref), (pl.ds(half, half), behind_ref)):
+        total = wider(kept_ref[2, rows, :]) + wider(got_ref[2, rows, :])
+        out_ref[...] = total.astype(jnp.bfloat16)
+
+
+def near_kernel(kept_ref, got_ref, ahead_ref, behind_ref, nearer_ref, farther_ref):
+    half = PART // 2
+    low, high = pl.ds(0, half), pl.ds(half, half)
+    for step, out_ref, more_ref, there in (
+        (1, nearer_ref, ahead_ref, low),
+        (3, farther_ref, behind_ref, high),
+    ):
+        for rows in (low, high):
+            total = wider(kept_ref[step, rows, :]) + wider(got_ref[step, rows, :])
+            if rows is there:
+                total += wider(more_ref[...])
+            out_ref[rows, :] = total.astype(jnp.bfloat16)
+
+
+def own_kernel(kept_ref, got_ref, one_ref, other_ref, own_ref, *out_refs):
+    size = PART // RINGS
+    for step in range(RINGS):
+        rows = pl.ds(step * size, size)
+        total = wider(kept_ref[0, rows, :]) + wider(got_ref[0, rows, :])
+        total += wider(one_ref[rows, :]) + wider(other_ref[rows, :])
+        if step:
+            out_refs[step - 1][...] = total.astype(jnp.bfloat16)
+        else:
+            own_ref[...] = total
+
+
+def sums(kernel, shapes, *operands):
+    return pl.pallas_call(
+        kernel,
+        out_shape=tuple(jax.ShapeDtypeStruct((rows, INNER), kind) for rows, kind in shapes),
+        in_specs=[vmem()] * len(operands),
+        out_specs=(vmem(),) * len(shapes),
+        compiler_params=limit(16),
+        cost_estimate=pl.CostEstimate(flops=10**9, bytes_accessed=10**6, transcendentals=0),
+    )(*operands)
+
+
+def summed_terms(kept, got, *done):
+    narrow = jnp.bfloat16
+    ahead, behind = sums(far_kernel, [(PART // 2, narrow)] * 2, kept, got)
+    ahead = shifted(ahead, 1, 0, 0)
+    behind = shifted(behind, RINGS - 1, 0, 0)
+    nearer, farther = sums(near_kernel, [(PART, narrow)] * 2, kept, got, ahead, behind)
+    sides = [shifted(nearer, 1, 0, 0), shifted(farther, RINGS - 1, 0, 0)]
+    size = PART // RINGS
+    total = sums(
+        own_kernel, [(size, jnp.float32)] + [(size, narrow)] * (RINGS - 1), kept, got, *sides
+    )
+    sent = [shifted(total[r], 0, r, 0) for r in range(1, RINGS)]
+    own, *done = lax.optimization_barrier((total[0], *done))
+    sent = [wider(value) for value in sent]
+    total = (own + sent[0] + sent[1] + sent[2]).reshape(RINGS, -1, INNER)
+    return [total[0]] + [shifted(total[r], 0, 0, r) for r in range(1, RINGS)] + done
 
 
 def heads_apart(product):
@@ -515,7 +559,7 @@
 ):
     live = counts_ref[place_ref[0], place_ref[1]] * QUERIES
 
-    @pl.loop(0, PAIRS)
+    @pl.loop(0, PAIRS, unroll=2)
     def _(pair):
         at = columns(pair)
         keys, values = kv_ref[:, at], kv_ref[:, columns(pair, INNER)]
@@ -646,7 +690,6 @@
     got = lax.ppermute(given, CORE, SWAP)
     d_sum, given = lax.optimization_barrier((d_sum, given))
     kept = gradient_term(place, turned_kept, d_sum, False)
-    d_beside, kept = lax.optimization_barrier((d_beside, kept))
     packed = pack_gradients(place, window_counts, d_memory, d_beside)
     packed, context_other, dq_other = lax.optimization_barrier((packed, context_other, dq_other))
     returned = lax.all_to_all(packed, CHIP, split_axis=0, concat_axis=0, tiled=True)
@@ -663,7 +706,7 @@
     )
     caption_grad = caption_grad.astype(jnp.bfloat16)
 
-    own, *sent = summed_terms(kept, got)
+    own, *sent, decoded, caption_grad = summed_terms(kept, got, decoded, caption_grad)
     total = (own + wider(sent[0]) + wider(sent[1]) + wider(sent[2])).reshape(2, -1, INNER)
     stays = lax.dynamic_index_in_dim(total, core, 0, keepdims=False)
     leaves = lax.dynamic_index_in_dim(total, 1 - core, 0, keepdims=False)

time: 171 us -> 185 us (1.082)
  waiting for transfers between devices: 50.8 us -> 59.3 us
  local copies, waits for them, and re-layouts: 3.43 us -> 11.2 us
  other arithmetic: 8.24 us -> 2.64 us
  starting transfers between devices: 41.3 us -> 44.9 us
    unnamed x34 -> x54, local copies, waits for them, and re-layouts: 3.28 us -> 11.2 us
    ppermute x10, waiting for transfers between devices: 23.5 us -> 29.3 us  [shifted(): return lax.ppermute(value.astype(jnp.bfloat16), SECTION_DEV, moved(shifts))]
    ppermute x1, starting transfers between devices: 2.25 us -> 5.04 us  [local(): comes = lax.ppermute(leaves, CORE, SWAP)]
    ppermute x1, waiting for transfers between devices: 3.57 us -> 5.9 us  [local(): d_beside = lax.ppermute(d_memory, CORE, SWAP)]
    add x1 -> x0, other arithmetic: 1.99 us -> none  [summed_terms(): total = [wider(kept[r]) + wider(got[r]) for r in range(RINGS)]]
    another operation x4 -> x1, other arithmetic: 2.01 us -> 0.06 us
  transfers between devices with their start and end apart: 21 -> 21, of which waited for: 7 -> 10; matrix products, arithmetic and copies ran while one was open for 11% -> 7% of each run, Pallas kernels for 10% -> 10%
where the time goes in v3:
time: 185 us
  waiting for transfers between devices  59.3 us (32%)
  Pallas kernels  54 us (29%)
  starting transfers between devices  44.9 us (24%)
  local copies, waits for them, and re-layouts  11.2 us (6%)
  matrix products  10.4 us (6%)
  other arithmetic  2.64 us (1%)
  between operations  2 us (1%)
    ppermute x10, waiting for transfers between devices, shifted(): return lax.ppermute(value.astype(jnp.bfloat16), SECTION_DEV, moved(shifts))  29.3 us
    all_to_all x1, waiting for transfers between devices, local(): lax.all_to_all(sent, CHIP, split_axis=0, concat_axis=0, tiled=True)  22 us
    ppermute x10, starting transfers between devices, shifted(): return lax.ppermute(value.astype(jnp.bfloat16), SECTION_DEV, moved(shifts))  14.4 us
    pallas_call x1, Pallas kernels, attention_grads(): pl.pallas_call(grads_kernel, out_shape=(wide, narrow, wide, narrow, jax.S...  12.1 us
    pallas_call x1, Pallas kernels, compress_windows(): pl.pallas_call(compress_kernel, out_shape=jax.ShapeDtypeStruct((chips, QU...  11.5 us
    all_to_all x1, starting transfers between devices, local(): lax.all_to_all(sent, CHIP, split_axis=0, concat_axis=0, tiled=True)  11.3 us
    unnamed x54, local copies, waits for them, and re-layouts  11.2 us
    all_to_all x1, starting transfers between devices, local(): lax.all_to_all(packed, CHIP, split_axis=0, concat_axis=0, tiled=True)  6.97 us
  transfers between devices with their start and end apart: 21, of which 10 were waited for; matrix products, arithmetic and copies ran while one was open for 7% of the time, Pallas kernels for 10%

profile of v3, /device:TPU:1, one launch (start us, length us, event | category | flops | bytes accessed | tf_op | source)
XLA Modules:
  0.0 184.6 jit_solution(2388839714923325098)
XLA Ops:
  1.2 11.5 %compress_windows.1 = bf16[32,32,1024]{2,1,0:T(8,128)(2,1)} custom-call(s32[8]{0:T(128)} %fusion.22.place_ref, s32[2,64]{1,0:T(2,128)} %counts_ref.11, bf16[32,1024]{1,0:T(8,128)(2,1)} %queries_ref.1, f32[1,1024]{1,0:T(1,128)} %bitcast.37, bf16[512,1024]{1,0:T(8,128)(2,1)} %bitcast.36, bf16[1024,2048]{1,0:T(8,128)(2,1)} %weight_hbm.1, bf16[1024,1024]{1,0:T(8,128)(2,1)} %out_hbm.1), custom_call_target="tpu_custom_call" | custom-call | flops 6000000000 | bytes 9000000 | tf_op jit(solution)/shard_map/compress_windows/pallas_call | solution.py:172
  12.7 11.3 %all-to-all-start = ((bf16[32,32,1024]{2,1,0:T(8,128)(2,1)}), bf16[32,32,1024]{2,1,0:T(8,128)(2,1)S(1)}, u32[]{:S(2)}, u32[]{:S(2)}) async-start(bf16[32,32,1024]{2,1,0:T(8,128)(2,1)} %compress_windows.1), calls=%async_computation | async-start | bytes 4194304 | tf_op jit(solution)/shard_map/all_to_all | solution.py:657
  25.1 4.3 %convolution_convert_fusion.dc_own = bf16[128,1024]{1,0:T(8,128)(2,1)S(1)} fusion(bf16[1024,2048]{1,0:T(8,128)(2,1)} %param.24, bf16[1,1,128,2048]{3,2,1,0:T(8,128)(2,1)} %param.25, pred[128]{0:T(512)(128)(4,1)S(1)} %iota_compare_fusion), kind=kOutput, calls=%fused_computation.8 | convolution fusion | flops 537264128 | bytes 4980864 | tf_op jit(solution)/shard_map/dot_general | solution.py:667
  30.2 22.0 %all-to-all-done.arrived_ref = bf16[32,32,1024]{2,1,0:T(8,128)(2,1)S(1)} async-done(((bf16[32,32,1024]{2,1,0:T(8,128)(2,1)}), bf16[32,32,1024]{2,1,0:T(8,128)(2,1)S(1)}, u32[]{:S(2)}, u32[]{:S(2)}) %all-to-all-start) | async-done | bytes 2097184 | tf_op jit(solution)/shard_map/all_to_all | solution.py:657
  52.2 1.8 collective-permute-start.2
  55.5 2.2 %copy-done.3 = bf16[1024,2048]{1,0:T(8,128)(2,1)S(1)} copy-done((bf16[1024,2048]{1,0:T(8,128)(2,1)S(1)}, bf16[1024,2048]{1,0:T(8,128)(2,1)}, u32[]{:S(2)}) %copy-start.3) | copy-done | bytes 4194328
  59.8 6.4 %project_memory.1 = (bf16[640,1024]{1,0:T(8,128)(2,1)S(1)}, bf16[640,2048]{1,0:T(8,128)(2,1)S(1)}) custom-call(s32[8]{0:T(128)S(1)} %touched.1.place_ref, s32[2,64]{1,0:T(2,128)S(1)} %copy-done.14, bf16[32,32,1024]{2,1,0:T(8,128)(2,1)S(1)} %all-to-all-done.arrived_ref, bf16[32,32,1024]{2,1,0:T(8,128)(2,1)S(1)} %collective-permute-done.2.beside_ref, ...), custom_call_target="tpu_custom_call" | custom-call | flops 5000000000 | bytes 10000000 | tf_op jit(solution)/shard_map/project_memory/pallas_call | solution.py:270
  66.2 1.2 collective-permute-done.1.dc_other
  67.5 5.1 %attention_stats.1.stats_ref = f32[3,8,512]{2,1,0:T(8,128)S(1)} custom-call(s32[8]{0:T(128)S(1)} %touched.1.place_ref, s32[2,64]{1,0:T(2,128)S(1)} %copy-done.14, bf16[128,1024]{1,0:T(8,128)(2,1)S(1)} %fusion.3.q_own, bf16[128,1024]{1,0:T(8,128)(2,1)S(1)} %collective-permute-done.q_other, bf16[128,1024]{1,0:T(8,128)(2,1)S(1)} %convolution_convert_fusion.dc_own, ...), custom_call_target="tpu_custom_call" | custom-call | flops 5000000000 | bytes 4000000 | tf_op jit(solution)/shard_map/attention_stats/pallas_call | solution.py:306
  73.6 3.1 %turned_memory.1 = (bf16[1024,640]{1,0:T(8,128)(2,1)S(1)}, bf16[1024,640]{1,0:T(8,128)(2,1)S(1)}) custom-call(s32[8]{0:T(128)S(1)} %touched.1.place_ref, bf16[640,1024]{1,0:T(8,128)(2,1)S(1)} %get-tuple-element.46.half_ref), custom_call_target="tpu_custom_call" | custom-call | flops 2000000000 | bytes 4000000 | tf_op jit(solution)/shard_map/turned_memory/pallas_call | solution.py:419
  77.9 12.1 %attention_grads.1 = (f32[128,1024]{1,0:T(8,128)S(1)}, bf16[128,1024]{1,0:T(8,128)(2,1)S(1)}, f32[128,1024]{1,0:T(8,128)S(1)}, bf16[128,1024]{1,0:T(8,128)(2,1)S...) custom-call(s32[8]{0:T(128)S(1)} %touched.1.place_ref, s32[2,64]{1,0:T(2,128)S(1)} %copy-done.14, ...), custom_call_target="tpu_custom_call" | custom-call | flops 12000000000 | bytes 10000000 | tf_op jit(solution)/shard_map/attention_grads/pallas_call | solution.py:606
  90.7 3.7 %given_term.1 = bf16[4,256,1024]{2,1,0:T(8,128)(2,1)} custom-call(s32[8]{0:T(128)S(1)} %touched.1.place_ref, bf16[1024,640]{1,0:T(8,128)(2,1)S(1)} %get-tuple-element.53.turned_ref, bf16[2,640,1024]{2,1,0:T(8,128)(2,1)S(1)} %get-tuple-element.54.sum_ref), custom_call_target="tpu_custom_call" | custom-call | flops 3000000000 | bytes 5000000 | tf_op jit(solution)/shard_map/given_term/pallas_call | solution.py:442
  95.7 5.9 %collective-permute-done.9.near_hbm = bf16[20,32,1024]{2,1,0:T(8,128)(2,1)} collective-permute-done((bf16[20,32,1024]{2,1,0:T(8,128)(2,1)S(1)}, bf16[20,32,1024]{2,1,0:T(8,128)(2,1)}, u32[]{:S(2)}, u32[]{:S(2)}) %collective-permute-start.9) | collective-permute-done | bytes 1310752 | tf_op jit(solution)/shard_map/ppermute | solution.py:688
  101.6 4.1 %pack_gradients.1 = bf16[32,32,1024]{2,1,0:T(8,128)(2,1)} custom-call(s32[8]{0:T(128)} %copy-done.8, s32[2,64]{1,0:T(2,128)} %counts_ref.11, bf16[20,32,1024]{2,1,0:T(8,128)(2,1)} %bitcast.33, bf16[20,32,1024]{2,1,0:T(8,128)(2,1)} %collective-permute-done.9.near_hbm), custom_call_target="tpu_custom_call" | custom-call | flops 2000000000 | bytes 4000000 | tf_op jit(solution)/shard_map/pack_gradients/pallas_call | solution.py:344
  106.6 1.7 copy-done.16
  108.4 1.3 copy-done.18
  109.7 2.3 %kept_term.1.kept_ref = bf16[4,256,1024]{2,1,0:T(8,128)(2,1)S(1)} custom-call(s32[8]{0:T(128)S(1)} %copy-done.9, bf16[1024,640]{1,0:T(8,128)(2,1)S(1)} %copy-done.18, bf16[2,640,1024]{2,1,0:T(8,128)(2,1)S(1)} %copy-done.16), custom_call_target="tpu_custom_call" | custom-call | flops 3000000000 | bytes 5000000 | tf_op jit(solution)/shard_map/kept_term/pallas_call | solution.py:442
  112.1 1.4 copy-done
  114.1 7.0 %all-to-all-start.1 = ((bf16[32,32,1024]{2,1,0:T(8,128)(2,1)}), bf16[32,32,1024]{2,1,0:T(8,128)(2,1)}, u32[]{:S(2)}, u32[]{:S(2)}) async-start(bf16[32,32,1024]{2,1,0:T(8,128)(2,1)} %pack_gradients.1), calls=%async_computation.1 | async-start | bytes 4194304 | tf_op jit(solution)/shard_map/all_to_all | solution.py:695
  121.1 1.6 copy-done.1
  122.8 1.2 collective-permute-start.5
  124.1 1.5 collective-permute-start.6
  125.6 2.8 %fusion.11 = (f32[128]{0:T(128)S(1)}, f32[128,2048]{1,0:T(8,128)S(1)}) fusion(bf16[1,1,128,2048]{3,2,1,0:T(8,128)(2,1)} %param.19, f32[2048]{0:T(1024)S(1)} %copy-done.26, bf16[2048,1024]{1,0:T(8,128)(2,1)S(1)} %copy-done.20, f32[128,1024]{1,0:T(8,128)S(1)} %get-tuple-element.65, bf16[128,1024]{1,0:T(8,128)(2,1)} %collective-permute-done.11), kind=kOutput, calls=%fused_computation.18 | convolution fusion | flops 538312576 | bytes 6562304 | tf_op jit(solution)/shard_map/dot_general | solution.py:703
  128.5 21.8 %collective-permute-done.5.ahead_ref = bf16[128,1024]{1,0:T(8,128)(2,1)S(1)} collective-permute-done((bf16[128,1024]{1,0:T(8,128)(2,1)S(1)}, bf16[128,1024]{1,0:T(8,128)(2,1)S(1)}, u32[]{:S(2)}, u32[]{:S(2)}) %collective-permute-start.5) | collective-permute-done | bytes 262176 | tf_op jit(solution)/shard_map/ppermute | solution.py:467
  150.6 2.7 %collective-permute-start.8 = (bf16[256,1024]{1,0:T(8,128)(2,1)S(1)}, bf16[256,1024]{1,0:T(8,128)(2,1)S(1)}, u32[]{:S(2)}, u32[]{:S(2)}) collective-permute-start(bf16[256,1024]{1,0:T(8,128)(2,1)S(1)} %get-tuple-element.58), channel_id=1, source_target_pairs={{0,24},{1,7},{2,26},{3,1},{4,28},{5,3},{6,30},{7,5},{8,0},{9,15},{... | collective-permute-start | bytes 1572872 | tf_op jit(solution)/shard_map/ppermute | solution.py:467
  154.5 5.7 %collective-permute-done.7.one_ref = bf16[256,1024]{1,0:T(8,128)(2,1)S(1)} collective-permute-done((bf16[256,1024]{1,0:T(8,128)(2,1)S(1)}, bf16[256,1024]{1,0:T(8,128)(2,1)S(1)}, u32[]{:S(2)}, u32[]{:S(2)}) %collective-permute-start.7) | collective-permute-done | bytes 524320 | tf_op jit(solution)/shard_map/ppermute | solution.py:467
  160.9 3.1 %collective-permute-start.13 = (bf16[64,1024]{1,0:T(8,128)(2,1)S(1)}, bf16[64,1024]{1,0:T(8,128)(2,1)S(1)}, u32[]{:S(2)}, u32[]{:S(2)}) collective-permute-start(bf16[64,1024]{1,0:T(8,128)(2,1)S(1)} %get-tuple-element.72), channel_id=1, source_target_pairs={{0,4},{1,17},{2,6},{3,19},{4,0},{5,21},{6,2},{7,23},{8,12},{9,25},... | collective-permute-start | bytes 393224 | tf_op jit(solution)/shard_map/ppermute | solution.py:467
  164.9 2.5 %fusion = bf16[128,2048]{1,0:T(8,128)(2,1)} fusion(bf16[1024,2048]{1,0:T(8,128)(2,1)S(1)} %copy-done.21, bf16[1,1,128,2048]{3,2,1,0:T(8,128)(2,1)S(1)} %copy-done.24, f32[128,1024]{1,0:T(8,128)S(1)} %get-tuple-element.60, bf16[128,1024]{1,0:T(8,128)(2,1)} %collective-permute-done.10), kind=kOutput, calls=%fused_computation.2 | convolution fusion | flops 538050560 | bytes 6029312 | tf_op jit(solution)/shard_map/dot_general | solution.py:699
  168.2 3.0 %collective-permute-start.16 = (bf16[16,1024]{1,0:T(8,128)(2,1)S(1)}, bf16[16,1024]{1,0:T(8,128)(2,1)S(1)}, u32[]{:S(2)}, u32[]{:S(2)}) collective-permute-start(bf16[16,1024]{1,0:T(8,128)(2,1)S(1)} %get-tuple-element.78), channel_id=1, source_target_pairs={{0,32},{1,33},{2,34},{3,35},{4,36},{5,37},{6,38},{7,39},{8,40},{9,... | collective-permute-start | bytes 98312 | tf_op jit(solution)/shard_map/ppermute | solution.py:467
  171.2 1.2 collective-permute-start.17
  174.0 5.0 %collective-permute-start.18 = (f32[8,1024]{1,0:T(8,128)S(1)}, f32[8,1024]{1,0:T(8,128)S(1)}, u32[]{:S(2)}, u32[]{:S(2)}) collective-permute-start(f32[8,1024]{1,0:T(8,128)S(1)} %get-tuple-element.80), channel_id=1, source_target_pairs={{0,1},{1,0},{2,3},{3,2},{4,5},{5,4},{6,7},{7,6},{8,9},{9,8},{10,11... | collective-permute-start | bytes 98312 | tf_op jit(solution)/shard_map/ppermute | solution.py:713
  180.5 3.9 %unpack_gradients.1 = bf16[16,32,1024]{2,1,0:T(8,128)(2,1)} custom-call(s32[8]{0:T(128)} %copy-done.8, s32[2,64]{1,0:T(2,128)} %counts_ref.11, bf16[32,32,1024]{2,1,0:T(8,128)(2,1)} %all-to-all-done.1.returned_hbm), custom_call_target="tpu_custom_call" | custom-call | flops 2000000000 | bytes 2000000 | tf_op jit(solution)/shard_map/unpack_gradients/pallas_call | solution.py:379
  (92 shorter events, 18.0 us)
Async XLA Ops:
  12.7 12.2 %copy-start.22 = (bf16[1,1,128,2048]{3,2,1,0:T(8,128)(2,1)S(1)}, bf16[1,1,128,2048]{3,2,1,0:T(8,128)(2,1)}, u32[]{:S(2)}) copy-start(bf16[1,1,128,2048]{3,2,1,0:T(8,128)(2,1)} %param.19) | copy-start | bytes 1572868
  12.7 16.7 %copy-start.26 = (f32[2048]{0:T(1024)S(1)}, f32[2048]{0:T(1024)}, u32[]{:S(2)}) copy-start(f32[2048]{0:T(1024)} %param.21) | copy-start | bytes 24580
  12.7 39.5 %all-to-all-start = ((bf16[32,32,1024]{2,1,0:T(8,128)(2,1)}), bf16[32,32,1024]{2,1,0:T(8,128)(2,1)S(1)}, u32[]{:S(2)}, u32[]{:S(2)}) async-start(bf16[32,32,1024]{2,1,0:T(8,128)(2,1)} %compress_windows.1), calls=%async_computation | async-start | bytes 4194304 | tf_op jit(solution)/shard_map/all_to_all | solution.py:657
  25.1 30.4 %copy-start.7 = (s32[8]{0:T(128)S(1)}, s32[8]{0:T(128)}, u32[]{:S(2)}) copy-start(s32[8]{0:T(128)} %fusion.22.place_ref) | copy-start | bytes 100
  29.4 29.4 %copy-start.14 = (s32[2,64]{1,0:T(2,128)S(1)}, s32[2,64]{1,0:T(2,128)}, u32[]{:S(2)}) copy-start(s32[2,64]{1,0:T(2,128)} %counts_ref.11) | copy-start | bytes 1540
  30.2 37.3 %copy-start.5 = (bf16[128,1024]{1,0:T(8,128)(2,1)}, bf16[128,1024]{1,0:T(8,128)(2,1)S(1)}, u32[]{:S(2)}) copy-start(bf16[128,1024]{1,0:T(8,128)(2,1)S(1)} %fusion.3.q_own) | copy-start | bytes 786436
  52.2 6.6 %collective-permute-start.2 = (bf16[32,32,1024]{2,1,0:T(8,128)(2,1)S(1)}, bf16[32,32,1024]{2,1,0:T(8,128)(2,1)S(1)}, u32[]{:S(2)}, u32[]{:S(2)}) collective-permute-start(bf16[32,32,1024]{2,1,0:T(8,128)(2,1)S(1)} %all-to-all-done.arrived_ref), channel_id=1, source_target_pairs={{0,1},{1,0},{2,3},{3,2},{4,5},{5,4},{6,7},{7,6},{8,9},{9,8},{10,11... | collective-permute-start | bytes 6291464 | tf_op jit(solution)/shard_map/ppermute | solution.py:675
  54.0 12.2 %collective-permute-start = (bf16[128,1024]{1,0:T(8,128)(2,1)S(1)}, bf16[128,1024]{1,0:T(8,128)(2,1)S(1)}, u32[]{:S(2)}, u32[]{:S(2)}) collective-permute-start(bf16[128,1024]{1,0:T(8,128)(2,1)S(1)} %fusion.3.q_own), channel_id=1, source_target_pairs={{0,64},{64,0},{1,65},{65,1},{2,66},{66,2},{3,67},{67,3},{4,68},{68... | collective-permute-start | bytes 786440 | tf_op jit(solution)/shard_map/ppermute | solution.py:670
  54.7 12.7 %collective-permute-start.1 = (bf16[128,1024]{1,0:T(8,128)(2,1)S(1)}, bf16[128,1024]{1,0:T(8,128)(2,1)S(1)}, u32[]{:S(2)}, u32[]{:S(2)}) collective-permute-start(bf16[128,1024]{1,0:T(8,128)(2,1)S(1)} %convolution_convert_fusion.dc_own), channel_id=1, source_target_pairs={{0,64},{64,0},{1,65},{65,1},{2,66},{66,2},{3,67},{67,3},{4,68},{68... | collective-permute-start | bytes 786440 | tf_op jit(solution)/shard_map/ppermute | solution.py:671
  58.8 31.9 %copy-start.8 = (s32[8]{0:T(128)}, s32[8]{0:T(128)S(1)}, u32[]{:S(2)}) copy-start(s32[8]{0:T(128)S(1)} %touched.1.place_ref) | copy-start | bytes 100
  72.6 5.3 %collective-permute-start.3 = (f32[3,8,512]{2,1,0:T(8,128)S(1)}, f32[3,8,512]{2,1,0:T(8,128)S(1)}, u32[]{:S(2)}, u32[]{:S(2)}) collective-permute-start(f32[3,8,512]{2,1,0:T(8,128)S(1)} %attention_stats.1.stats_ref), channel_id=1, source_target_pairs={{0,64},{64,0},{1,65},{65,1},{2,66},{66,2},{3,67},{67,3},{4,68},{68... | collective-permute-start | bytes 147464 | tf_op jit(solution)/shard_map/ppermute | solution.py:679
  94.4 12.3 %copy-start.9 = (s32[8]{0:T(128)S(1)}, s32[8]{0:T(128)}, u32[]{:S(2)}) copy-start(s32[8]{0:T(128)} %copy-done.8) | copy-start | bytes 100
  94.4 26.7 %collective-permute-start.4 = (bf16[4,256,1024]{2,1,0:T(8,128)(2,1)}, bf16[4,256,1024]{2,1,0:T(8,128)(2,1)S(1)}, u32[]{:S(2)}, u32[]{:S(2)}) collective-permute-start(bf16[4,256,1024]{2,1,0:T(8,128)(2,1)} %given_term.1), channel_id=1, source_target_pairs={{0,1},{1,0},{2,3},{3,2},{4,5},{5,4},{6,7},{7,6},{8,9},{9,8},{10,11... | collective-permute-start | bytes 6291464 | tf_op jit(solution)/shard_map/ppermute | solution.py:690
  95.6 6.0 %collective-permute-start.9 = (bf16[20,32,1024]{2,1,0:T(8,128)(2,1)S(1)}, bf16[20,32,1024]{2,1,0:T(8,128)(2,1)}, u32[]{:S(2)}, u32[]{:S(2)}) collective-permute-start(bf16[20,32,1024]{2,1,0:T(8,128)(2,1)S(1)} %bitcast.32), channel_id=1, source_target_pairs={{0,1},{1,0},{2,3},{3,2},{4,5},{5,4},{6,7},{7,6},{8,9},{9,8},{10,11... | collective-permute-start | bytes 3932168 | tf_op jit(solution)/shard_map/ppermute | solution.py:688
  105.8 19.8 %collective-permute-start.11 = (bf16[128,1024]{1,0:T(8,128)(2,1)}, bf16[128,1024]{1,0:T(8,128)(2,1)}, u32[]{:S(2)}, u32[]{:S(2)}) collective-permute-start(bf16[128,1024]{1,0:T(8,128)(2,1)} %copy-done.13), channel_id=1, source_target_pairs={{0,64},{64,0},{1,65},{65,1},{2,66},{66,2},{3,67},{67,3},{4,68},{68... | collective-permute-start | bytes 786440 | tf_op jit(solution)/shard_map/ppermute | solution.py:702
  113.5 51.4 %collective-permute-start.10 = (bf16[128,1024]{1,0:T(8,128)(2,1)S(1)}, bf16[128,1024]{1,0:T(8,128)(2,1)}, u32[]{:S(2)}, u32[]{:S(2)}) collective-permute-start(bf16[128,1024]{1,0:T(8,128)(2,1)S(1)} %copy-done.12), channel_id=1, source_target_pairs={{0,64},{64,0},{1,65},{65,1},{2,66},{66,2},{3,67},{67,3},{4,68},{68... | collective-permute-start | bytes 786440 | tf_op jit(solution)/shard_map/ppermute | solution.py:698
  114.1 66.4 %all-to-all-start.1 = ((bf16[32,32,1024]{2,1,0:T(8,128)(2,1)}), bf16[32,32,1024]{2,1,0:T(8,128)(2,1)}, u32[]{:S(2)}, u32[]{:S(2)}) async-start(bf16[32,32,1024]{2,1,0:T(8,128)(2,1)} %pack_gradients.1), calls=%async_computation.1 | async-start | bytes 4194304 | tf_op jit(solution)/shard_map/all_to_all | solution.py:695
  122.8 27.4 %copy-start.2 = (bf16[4,256,1024]{2,1,0:T(8,128)(2,1)S(1)}, bf16[4,256,1024]{2,1,0:T(8,128)(2,1)}, u32[]{:S(2)}) copy-start(bf16[4,256,1024]{2,1,0:T(8,128)(2,1)} %copy-done) | copy-start | bytes 6291460
  122.8 27.4 %collective-permute-start.5 = (bf16[128,1024]{1,0:T(8,128)(2,1)S(1)}, bf16[128,1024]{1,0:T(8,128)(2,1)S(1)}, u32[]{:S(2)}, u32[]{:S(2)}) collective-permute-start(bf16[128,1024]{1,0:T(8,128)(2,1)S(1)} %get-tuple-element.55), channel_id=1, source_target_pairs={{0,8},{1,3},{2,10},{3,5},{4,12},{5,7},{6,14},{7,1},{8,16},{9,11},{... | collective-permute-start | bytes 786440 | tf_op jit(solution)/shard_map/ppermute | solution.py:467
  124.1 26.2 %collective-permute-start.6 = (bf16[128,1024]{1,0:T(8,128)(2,1)S(1)}, bf16[128,1024]{1,0:T(8,128)(2,1)S(1)}, u32[]{:S(2)}, u32[]{:S(2)}) collective-permute-start(bf16[128,1024]{1,0:T(8,128)(2,1)S(1)} %get-tuple-element.56), channel_id=1, source_target_pairs={{0,24},{1,7},{2,26},{3,1},{4,28},{5,3},{6,30},{7,5},{8,0},{9,15},{... | collective-permute-start | bytes 786440 | tf_op jit(solution)/shard_map/ppermute | solution.py:467
  125.6 27.7 %copy-start.24 = (bf16[1,1,128,2048]{3,2,1,0:T(8,128)(2,1)S(1)}, bf16[1,1,128,2048]{3,2,1,0:T(8,128)(2,1)}, u32[]{:S(2)}) copy-start(bf16[1,1,128,2048]{3,2,1,0:T(8,128)(2,1)} %param.19) | copy-start | bytes 1572868
  125.6 27.7 %copy-start.25 = (bf16[1,1,128,2048]{3,2,1,0:T(8,128)(2,1)S(1)}, bf16[1,1,128,2048]{3,2,1,0:T(8,128)(2,1)}, u32[]{:S(2)}) copy-start(bf16[1,1,128,2048]{3,2,1,0:T(8,128)(2,1)} %param.25) | copy-start | bytes 1572868
  150.6 14.3 %copy-start.21 = (bf16[1024,2048]{1,0:T(8,128)(2,1)S(1)}, bf16[1024,2048]{1,0:T(8,128)(2,1)}, u32[]{:S(2)}) copy-start(bf16[1024,2048]{1,0:T(8,128)(2,1)} %param.24) | copy-start | bytes 12582916
  150.6 9.6 %collective-permute-start.7 = (bf16[256,1024]{1,0:T(8,128)(2,1)S(1)}, bf16[256,1024]{1,0:T(8,128)(2,1)S(1)}, u32[]{:S(2)}, u32[]{:S(2)}) collective-permute-start(bf16[256,1024]{1,0:T(8,128)(2,1)S(1)} %get-tuple-element.57), channel_id=1, source_target_pairs={{0,8},{1,3},{2,10},{3,5},{4,12},{5,7},{6,14},{7,1},{8,16},{9,11},{... | collective-permute-start | bytes 1572872 | tf_op jit(solution)/shard_map/ppermute | solution.py:467
  150.6 9.5 %collective-permute-start.8 = (bf16[256,1024]{1,0:T(8,128)(2,1)S(1)}, bf16[256,1024]{1,0:T(8,128)(2,1)S(1)}, u32[]{:S(2)}, u32[]{:S(2)}) collective-permute-start(bf16[256,1024]{1,0:T(8,128)(2,1)S(1)} %get-tuple-element.58), channel_id=1, source_target_pairs={{0,24},{1,7},{2,26},{3,1},{4,28},{5,3},{6,30},{7,5},{8,0},{9,15},{... | collective-permute-start | bytes 1572872 | tf_op jit(solution)/shard_map/ppermute | solution.py:467
  160.4 7.0 %collective-permute-start.12 = (bf16[64,1024]{1,0:T(8,128)(2,1)S(1)}, bf16[64,1024]{1,0:T(8,128)(2,1)S(1)}, u32[]{:S(2)}, u32[]{:S(2)}) collective-permute-start(bf16[64,1024]{1,0:T(8,128)(2,1)S(1)} %get-tuple-element.71), channel_id=1, source_target_pairs={{0,2},{1,9},{2,4},{3,11},{4,6},{5,13},{6,0},{7,15},{8,10},{9,17},{... | collective-permute-start | bytes 393224 | tf_op jit(solution)/shard_map/ppermute | solution.py:467
  160.9 6.9 %collective-permute-start.13 = (bf16[64,1024]{1,0:T(8,128)(2,1)S(1)}, bf16[64,1024]{1,0:T(8,128)(2,1)S(1)}, u32[]{:S(2)}, u32[]{:S(2)}) collective-permute-start(bf16[64,1024]{1,0:T(8,128)(2,1)S(1)} %get-tuple-element.72), channel_id=1, source_target_pairs={{0,4},{1,17},{2,6},{3,19},{4,0},{5,21},{6,2},{7,23},{8,12},{9,25},... | collective-permute-start | bytes 393224 | tf_op jit(solution)/shard_map/ppermute | solution.py:467
  164.0 3.8 %collective-permute-start.14 = (bf16[64,1024]{1,0:T(8,128)(2,1)S(1)}, bf16[64,1024]{1,0:T(8,128)(2,1)S(1)}, u32[]{:S(2)}, u32[]{:S(2)}) collective-permute-start(bf16[64,1024]{1,0:T(8,128)(2,1)S(1)} %get-tuple-element.73), channel_id=1, source_target_pairs={{0,6},{1,25},{2,0},{3,27},{4,2},{5,29},{6,4},{7,31},{8,14},{9,1},{... | collective-permute-start | bytes 393224 | tf_op jit(solution)/shard_map/ppermute | solution.py:467
  167.9 4.5 %collective-permute-start.15 = (bf16[16,1024]{1,0:T(8,128)(2,1)S(1)}, bf16[16,1024]{1,0:T(8,128)(2,1)S(1)}, u32[]{:S(2)}, u32[]{:S(2)}) collective-permute-start(bf16[16,1024]{1,0:T(8,128)(2,1)S(1)} %get-tuple-element.76), channel_id=1, source_target_pairs={{0,64},{1,65},{2,66},{3,67},{4,68},{5,69},{6,70},{7,71},{8,72},{9,... | collective-permute-start | bytes 98312 | tf_op jit(solution)/shard_map/ppermute | solution.py:467
  168.2 4.6 %collective-permute-start.16 = (bf16[16,1024]{1,0:T(8,128)(2,1)S(1)}, bf16[16,1024]{1,0:T(8,128)(2,1)S(1)}, u32[]{:S(2)}, u32[]{:S(2)}) collective-permute-start(bf16[16,1024]{1,0:T(8,128)(2,1)S(1)} %get-tuple-element.78), channel_id=1, source_target_pairs={{0,32},{1,33},{2,34},{3,35},{4,36},{5,37},{6,38},{7,39},{8,40},{9,... | collective-permute-start | bytes 98312 | tf_op jit(solution)/shard_map/ppermute | solution.py:467
  171.2 2.8 %collective-permute-start.17 = (bf16[16,1024]{1,0:T(8,128)(2,1)S(1)}, bf16[16,1024]{1,0:T(8,128)(2,1)S(1)}, u32[]{:S(2)}, u32[]{:S(2)}) collective-permute-start(bf16[16,1024]{1,0:T(8,128)(2,1)S(1)} %get-tuple-element.77), channel_id=1, source_target_pairs={{0,96},{1,97},{2,98},{3,99},{4,100},{5,101},{6,102},{7,103},{8,104... | collective-permute-start | bytes 98312 | tf_op jit(solution)/shard_map/ppermute | solution.py:467
  174.0 5.9 %collective-permute-start.18 = (f32[8,1024]{1,0:T(8,128)S(1)}, f32[8,1024]{1,0:T(8,128)S(1)}, u32[]{:S(2)}, u32[]{:S(2)}) collective-permute-start(f32[8,1024]{1,0:T(8,128)S(1)} %get-tuple-element.80), channel_id=1, source_target_pairs={{0,1},{1,0},{2,3},{3,2},{4,5},{5,4},{6,7},{7,6},{8,9},{9,8},{10,11... | collective-permute-start | bytes 98312 | tf_op jit(solution)/shard_map/ppermute | solution.py:713
  (16 other events, 51.2 us)

commit v4 on v3

--- a/solution.py
+++ b/solution.py
@@ -123,7 +123,7 @@
     same = row // FRAMES == column // (2 * QUERIES)
     low = lax.broadcasted_iota(jnp.int32, (QUERIES, 128), 1) < HEAD_DIM
 
-    @pl.loop(0, PAIRS, unroll=2)
+    @pl.loop(0, PAIRS, unroll=4)
     def _(pair):
         at = columns(pair)
         queries = queries_ref[:, at]
@@ -224,9 +224,7 @@
     )(place, memory_kv)
 
 
-def project_kernel(
-    place_ref, counts_ref, arrived_ref, beside_ref, weight_ref, half_ref, kv_ref, sems
-):
+def gather_kernel(place_ref, counts_ref, arrived_ref, beside_ref, half_ref, sems):
     section, video_id = place_ref[0], place_ref[1]
     videos = counts_ref.shape[1]
     core = video_id % 2
@@ -262,26 +260,39 @@
         def _():
             pltpu.make_async_copy(arrived_ref.at[0], block(p), sems.at[p]).wait()
 
+
+def gathered_memory(place, counts, arrived, beside):
+    return pl.pallas_call(
+        gather_kernel,
+        out_shape=jax.ShapeDtypeStruct((ROWS, QDIM), jnp.bfloat16),
+        in_specs=[smem(), smem(), anywhere(), anywhere()],
+        out_specs=vmem(),
+        scratch_shapes=[pltpu.SemaphoreType.DMA((MOST_WIN,))],
+        compiler_params=limit(16),
+        cost_estimate=pl.CostEstimate(
+            flops=3 * 10**9, bytes_accessed=4 * 10**6, transcendentals=0
+        ),
+        name="gathered_memory",
+    )(place, counts, arrived, beside)
+
+
+def project_kernel(half_ref, weight_ref, kv_ref):
     for cut in CUTS:
         kv_ref[:, cut] = dot(half_ref[...], weight_ref[:, cut]).astype(jnp.bfloat16)
 
 
-def project_memory(place, counts, arrived, beside, memory_kv):
+def project_memory(half, memory_kv):
     return pl.pallas_call(
         project_kernel,
-        out_shape=(
-            jax.ShapeDtypeStruct((ROWS, QDIM), jnp.bfloat16),
-            jax.ShapeDtypeStruct((ROWS, 2 * INNER), jnp.bfloat16),
-        ),
-        in_specs=[smem(), smem(), anywhere(), anywhere(), vmem()],
-        out_specs=(vmem(), vmem()),
-        scratch_shapes=[pltpu.SemaphoreType.DMA((MOST_WIN,))],
+        out_shape=jax.ShapeDtypeStruct((ROWS, 2 * INNER), jnp.bfloat16),
+        in_specs=[vmem(), vmem()],
+        out_specs=vmem(),
         compiler_params=limit(16),
         cost_estimate=pl.CostEstimate(
-            flops=5 * 10**9, bytes_accessed=10**7, transcendentals=0
+            flops=3 * 10**9, bytes_accessed=8 * 10**6, transcendentals=0
         ),
         name="project_memory",
-    )(place, counts, arrived, beside, memory_kv)
+    )(half, memory_kv)
 
 
 def stats_kernel(
@@ -289,7 +300,7 @@
 ):
     live = counts_ref[place_ref[0], place_ref[1]] * QUERIES
 
-    @pl.loop(0, PAIRS, unroll=2)
+    @pl.loop(0, PAIRS, unroll=4)
     def _(pair):
         at = columns(pair)
         keys, values = kv_ref[:, at], kv_ref[:, columns(pair, INNER)]
@@ -350,6 +361,7 @@
         cost_estimate=pl.CostEstimate(
             flops=2 * 10**9, bytes_accessed=4 * 10**6, transcendentals=0
         ),
+        compiler_params=limit(24),
         name="pack_gradients",
     )(place, counts, own, near)
 
@@ -674,7 +686,8 @@
     place = touched(place, memory_kv)
     beside = lax.ppermute(arrived, CORE, SWAP)
     tokens = (query, query_other, d_context, d_context_other)
-    half, key_value = project_memory(place, window_counts, arrived, beside, memory_kv)
+    half = gathered_memory(place, window_counts, arrived, beside)
+    key_value = project_memory(half, memory_kv)
     stats = attention_stats(place, window_counts, tokens, key_value)
     peer = lax.ppermute(stats, "section", SWAP)
     half, stats = lax.optimization_barrier((half, stats))

time: 185 us -> 178 us (0.962)
  local copies, waits for them, and re-layouts: 11.2 us -> 5.27 us
  waiting for transfers between devices: 59.3 us -> 61.5 us
    unnamed x54 -> x40, local copies, waits for them, and re-layouts: 11.2 us -> 5.25 us
    pallas_call x1 -> x2, Pallas kernels: 6.38 us -> 6.37 us  [the longest x1 3.5 us: gathered_memory(): pl.pallas_call(gather_kernel, out_shape=jax.ShapeDtypeStruct((ROWS, QDIM)...]
  transfers between devices with their start and end apart: 21 -> 21, of which waited for: 10 -> 10; matrix products, arithmetic and copies ran while one was open for 7% -> 6% of each run, Pallas kernels for 10% -> 10%
where the time goes in v4:
time: 178 us
  waiting for transfers between devices  61.5 us (35%)
  Pallas kernels  52.4 us (29%)
  starting transfers between devices  44.8 us (25%)
  matrix products  9.32 us (5%)
  local copies, waits for them, and re-layouts  5.27 us (3%)
  other arithmetic  2.64 us (1%)
  between operations  2.03 us (1%)
    ppermute x10, waiting for transfers between devices, shifted(): return lax.ppermute(value.astype(jnp.bfloat16), SECTION_DEV, moved(shifts))  30.4 us
    all_to_all x1, waiting for transfers between devices, local(): lax.all_to_all(sent, CHIP, split_axis=0, concat_axis=0, tiled=True)  22.1 us
    ppermute x10, starting transfers between devices, shifted(): return lax.ppermute(value.astype(jnp.bfloat16), SECTION_DEV, moved(shifts))  14.4 us
    pallas_call x1, Pallas kernels, attention_grads(): pl.pallas_call(grads_kernel, out_shape=(wide, narrow, wide, narrow, jax.S...  12.4 us
    all_to_all x1, starting transfers between devices, local(): lax.all_to_all(sent, CHIP, split_axis=0, concat_axis=0, tiled=True)  11.3 us
    pallas_call x1, Pallas kernels, compress_windows(): pl.pallas_call(compress_kernel, out_shape=jax.ShapeDtypeStruct((chips, QU...  10.5 us
    all_to_all x1, starting transfers between devices, local(): lax.all_to_all(packed, CHIP, split_axis=0, concat_axis=0, tiled=True)  6.97 us
    pallas_call x2, Pallas kernels, gradient_term(): pl.pallas_call(functools.partial(term_kernel, sibling), out_shape=jax.Sha...  6.11 us
  transfers between devices with their start and end apart: 21, of which 10 were waited for; matrix products, arithmetic and copies ran while one was open for 6% of the time, Pallas kernels for 10%

profile of v4, /device:TPU:1, one launch (start us, length us, event | category | flops | bytes accessed | tf_op | source)
XLA Modules:
  0.0 177.9 jit_solution(16119175813161769829)
XLA Ops:
  1.2 10.5 %compress_windows.1 = bf16[32,32,1024]{2,1,0:T(8,128)(2,1)} custom-call(s32[8]{0:T(128)} %fusion.22.place_ref, s32[2,64]{1,0:T(2,128)} %counts_ref.11, bf16[32,1024]{1,0:T(8,128)(2,1)} %queries_ref.1, f32[1,1024]{1,0:T(1,128)} %bitcast.37, bf16[512,1024]{1,0:T(8,128)(2,1)} %bitcast.36, bf16[1024,2048]{1,0:T(8,128)(2,1)} %weight_hbm.1, bf16[1024,1024]{1,0:T(8,128)(2,1)} %out_hbm.1), custom_call_target="tpu_custom_call" | custom-call | flops 6000000000 | bytes 9000000 | tf_op jit(solution)/shard_map/compress_windows/pallas_call | solution.py:172
  11.7 11.3 %all-to-all-start = ((bf16[32,32,1024]{2,1,0:T(8,128)(2,1)}), bf16[32,32,1024]{2,1,0:T(8,128)(2,1)S(1)}, u32[]{:S(2)}, u32[]{:S(2)}) async-start(bf16[32,32,1024]{2,1,0:T(8,128)(2,1)} %compress_windows.1), calls=%async_computation | async-start | bytes 4194304 | tf_op jit(solution)/shard_map/all_to_all | solution.py:669
  24.1 4.1 %convolution_convert_fusion.dc_own = bf16[128,1024]{1,0:T(8,128)(2,1)S(1)} fusion(bf16[1024,2048]{1,0:T(8,128)(2,1)} %param.24, bf16[1,1,128,2048]{3,2,1,0:T(8,128)(2,1)S(1)} %copy-done.17, pred[128]{0:T(512)(128)(4,1)S(1)} %iota_compare_fusion), kind=kOutput, calls=%fused_computation.8 | convolution fusion | flops 537264128 | bytes 4980864 | tf_op jit(solution)/shard_map/dot_general | solution.py:679
  29.1 22.1 %all-to-all-done.arrived_ref = bf16[32,32,1024]{2,1,0:T(8,128)(2,1)S(1)} async-done(((bf16[32,32,1024]{2,1,0:T(8,128)(2,1)}), bf16[32,32,1024]{2,1,0:T(8,128)(2,1)S(1)}, u32[]{:S(2)}, u32[]{:S(2)}) %all-to-all-start) | async-done | bytes 2097184 | tf_op jit(solution)/shard_map/all_to_all | solution.py:669
  51.2 1.8 %collective-permute-start.2 = (bf16[32,32,1024]{2,1,0:T(8,128)(2,1)S(1)}, bf16[32,32,1024]{2,1,0:T(8,128)(2,1)S(1)}, u32[]{:S(2)}, u32[]{:S(2)}) collective-permute-start(bf16[32,32,1024]{2,1,0:T(8,128)(2,1)S(1)} %all-to-all-done.arrived_ref), channel_id=1, source_target_pairs={{0,1},{1,0},{2,3},{3,2},{4,5},{5,4},{6,7},{7,6},{8,9},{9,8},{10,11... | collective-permute-start | bytes 6291464 | tf_op jit(solution)/shard_map/ppermute | solution.py:687
  54.5 2.2 %copy-done.3 = bf16[1024,2048]{1,0:T(8,128)(2,1)S(1)} copy-done((bf16[1024,2048]{1,0:T(8,128)(2,1)S(1)}, bf16[1024,2048]{1,0:T(8,128)(2,1)}, u32[]{:S(2)}) %copy-start.3) | copy-done | bytes 4194328
  57.9 3.5 %gathered_memory.1.half_ref = bf16[640,1024]{1,0:T(8,128)(2,1)S(1)} custom-call(s32[8]{0:T(128)S(1)} %touched.1.place_ref, s32[2,64]{1,0:T(2,128)S(1)} %copy-done.10, bf16[32,32,1024]{2,1,0:T(8,128)(2,1)S(1)} %all-to-all-done.arrived_ref, bf16[32,32,1024]{2,1,0:T(8,128)(2,1)S(1)} %collective-permute-done.2.beside_ref), custom_call_target="tpu_custom_call" | custom-call | flops 3000000000 | bytes 4000000 | tf_op jit(solution)/shard_map/gathered_memory/pallas_call | solution.py:265
  61.4 2.9 %project_memory.1.kv_ref = bf16[640,2048]{1,0:T(8,128)(2,1)S(1)} custom-call(bf16[640,1024]{1,0:T(8,128)(2,1)S(1)} %gathered_memory.1.half_ref, bf16[1024,2048]{1,0:T(8,128)(2,1)S(1)} %copy-done.4), custom_call_target="tpu_custom_call" | custom-call | flops 3000000000 | bytes 8000000 | tf_op jit(solution)/shard_map/project_memory/pallas_call | solution.py:285
  64.3 2.2 %collective-permute-done.1.dc_other = bf16[128,1024]{1,0:T(8,128)(2,1)S(1)} collective-permute-done((bf16[128,1024]{1,0:T(8,128)(2,1)S(1)}, bf16[128,1024]{1,0:T(8,128)(2,1)S(1)}, u32[]{:S(2)}, u32[]{:S(2)}) %collective-permute-start.1) | collective-permute-done | bytes 262176 | tf_op jit(solution)/shard_map/ppermute | solution.py:683
  66.5 4.7 %attention_stats.1.stats_ref = f32[3,8,512]{2,1,0:T(8,128)S(1)} custom-call(s32[8]{0:T(128)S(1)} %touched.1.place_ref, s32[2,64]{1,0:T(2,128)S(1)} %copy-done.10, bf16[128,1024]{1,0:T(8,128)(2,1)S(1)} %fusion.3.q_own, bf16[128,1024]{1,0:T(8,128)(2,1)S(1)} %collective-permute-done.q_other, bf16[128,1024]{1,0:T(8,128)(2,1)S(1)} %convolution_convert_fusion.dc_own, ...), custom_call_target="tpu_custom_call" | custom-call | flops 5000000000 | bytes 4000000 | tf_op jit(solution)/shard_map/attention_stats/pallas_call | solution.py:317
  72.3 3.1 %turned_memory.1 = (bf16[1024,640]{1,0:T(8,128)(2,1)S(1)}, bf16[1024,640]{1,0:T(8,128)(2,1)S(1)}) custom-call(s32[8]{0:T(128)S(1)} %touched.1.place_ref, bf16[640,1024]{1,0:T(8,128)(2,1)S(1)} %gathered_memory.1.half_ref), custom_call_target="tpu_custom_call" | custom-call | flops 2000000000 | bytes 4000000 | tf_op jit(solution)/shard_map/turned_memory/pallas_call | solution.py:431
  75.4 12.4 %attention_grads.1 = (f32[128,1024]{1,0:T(8,128)S(1)}, bf16[128,1024]{1,0:T(8,128)(2,1)}, f32[128,1024]{1,0:T(8,128)S(1)}, bf16[128,1024]{1,0:T(8,128)(2,1)}, bf...) custom-call(s32[8]{0:T(128)S(1)} %touched.1.place_ref, s32[2,64]{1,0:T(2,128)S(1)} %copy-done.10, ...), custom_call_target="tpu_custom_call" | custom-call | flops 12000000000 | bytes 10000000 | tf_op jit(solution)/shard_map/attention_grads/pallas_call | solution.py:618
  87.8 3.8 %given_term.1 = bf16[4,256,1024]{2,1,0:T(8,128)(2,1)} custom-call(s32[8]{0:T(128)S(1)} %touched.1.place_ref, bf16[1024,640]{1,0:T(8,128)(2,1)S(1)} %get-tuple-element.49.turned_ref, bf16[2,640,1024]{2,1,0:T(8,128)(2,1)S(1)} %get-tuple-element.50.sum_ref), custom_call_target="tpu_custom_call" | custom-call | flops 3000000000 | bytes 5000000 | tf_op jit(solution)/shard_map/given_term/pallas_call | solution.py:454
  92.7 5.9 %collective-permute-done.9.near_hbm = bf16[20,32,1024]{2,1,0:T(8,128)(2,1)S(1)} collective-permute-done((bf16[20,32,1024]{2,1,0:T(8,128)(2,1)S(1)}, bf16[20,32,1024]{2,1,0:T(8,128)(2,1)S(1)}, u32[]{:S(2)}, u32[]{:S(2)}) %collective-permute-start.9) | collective-permute-done | bytes 1310752 | tf_op jit(solution)/shard_map/ppermute | solution.py:701
  98.6 3.5 %pack_gradients.1 = bf16[32,32,1024]{2,1,0:T(8,128)(2,1)S(1)} custom-call(s32[8]{0:T(128)S(1)} %touched.1.place_ref, s32[2,64]{1,0:T(2,128)S(1)} %copy-done.10, bf16[20,32,1024]{2,1,0:T(8,128)(2,1)S(1)} %bitcast.33, bf16[20,32,1024]{2,1,0:T(8,128)(2,1)S(1)} %collective-permute-done.9.near_hbm), custom_call_target="tpu_custom_call" | custom-call | flops 2000000000 | bytes 4000000 | tf_op jit(solution)/shard_map/pack_gradients/pallas_call | solution.py:355
  103.1 2.3 %kept_term.1.kept_ref = bf16[4,256,1024]{2,1,0:T(8,128)(2,1)S(1)} custom-call(s32[8]{0:T(128)S(1)} %touched.1.place_ref, bf16[1024,640]{1,0:T(8,128)(2,1)S(1)} %get-tuple-element.45.turned_ref, bf16[2,640,1024]{2,1,0:T(8,128)(2,1)S(1)} %get-tuple-element.50.sum_ref), custom_call_target="tpu_custom_call" | custom-call | flops 3000000000 | bytes 5000000 | tf_op jit(solution)/shard_map/kept_term/pallas_call | solution.py:454
  105.5 1.4 copy-done
  107.4 7.0 %all-to-all-start.1 = ((bf16[32,32,1024]{2,1,0:T(8,128)(2,1)}), bf16[32,32,1024]{2,1,0:T(8,128)(2,1)}, u32[]{:S(2)}, u32[]{:S(2)}) async-start(bf16[32,32,1024]{2,1,0:T(8,128)(2,1)} %copy-done.5), calls=%async_computation.1 | async-start | bytes 4194304 | tf_op jit(solution)/shard_map/all_to_all | solution.py:708
  114.4 1.6 copy-done.1
  116.1 1.2 collective-permute-start.5
  117.3 1.5 collective-permute-start.6
  118.8 2.8 %fusion.11 = (f32[128]{0:T(128)S(1)}, f32[128,2048]{1,0:T(8,128)S(1)}) fusion(bf16[1,1,128,2048]{3,2,1,0:T(8,128)(2,1)} %param.19, f32[2048]{0:T(1024)S(1)} %copy-done.19, bf16[2048,1024]{1,0:T(8,128)(2,1)S(1)} %copy-done.12, f32[128,1024]{1,0:T(8,128)S(1)} %get-tuple-element.61, bf16[128,1024]{1,0:T(8,128)(2,1)} %collective-permute-done.11), kind=kOutput, calls=%fused_computation.18 | convolution fusion | flops 538312576 | bytes 6562304 | tf_op jit(solution)/shard_map/dot_general | solution.py:716
  121.7 21.8 %collective-permute-done.5.ahead_ref = bf16[128,1024]{1,0:T(8,128)(2,1)S(1)} collective-permute-done((bf16[128,1024]{1,0:T(8,128)(2,1)S(1)}, bf16[128,1024]{1,0:T(8,128)(2,1)S(1)}, u32[]{:S(2)}, u32[]{:S(2)}) %collective-permute-start.5) | collective-permute-done | bytes 262176 | tf_op jit(solution)/shard_map/ppermute | solution.py:479
  143.9 2.7 %collective-permute-start.8 = (bf16[256,1024]{1,0:T(8,128)(2,1)S(1)}, bf16[256,1024]{1,0:T(8,128)(2,1)S(1)}, u32[]{:S(2)}, u32[]{:S(2)}) collective-permute-start(bf16[256,1024]{1,0:T(8,128)(2,1)S(1)} %get-tuple-element.54), channel_id=1, source_target_pairs={{0,24},{1,7},{2,26},{3,1},{4,28},{5,3},{6,30},{7,5},{8,0},{9,15},{... | collective-permute-start | bytes 1572872 | tf_op jit(solution)/shard_map/ppermute | solution.py:479
  146.5 1.2 fusion.9
  147.7 5.7 %collective-permute-done.7.one_ref = bf16[256,1024]{1,0:T(8,128)(2,1)S(1)} collective-permute-done((bf16[256,1024]{1,0:T(8,128)(2,1)S(1)}, bf16[256,1024]{1,0:T(8,128)(2,1)S(1)}, u32[]{:S(2)}, u32[]{:S(2)}) %collective-permute-start.7) | collective-permute-done | bytes 524320 | tf_op jit(solution)/shard_map/ppermute | solution.py:479
  154.1 3.1 %collective-permute-start.13 = (bf16[64,1024]{1,0:T(8,128)(2,1)S(1)}, bf16[64,1024]{1,0:T(8,128)(2,1)S(1)}, u32[]{:S(2)}, u32[]{:S(2)}) collective-permute-start(bf16[64,1024]{1,0:T(8,128)(2,1)S(1)} %get-tuple-element.68), channel_id=1, source_target_pairs={{0,4},{1,17},{2,6},{3,19},{4,0},{5,21},{6,2},{7,23},{8,12},{9,25},... | collective-permute-start | bytes 393224 | tf_op jit(solution)/shard_map/ppermute | solution.py:479
  158.1 1.6 fusion
  159.7 1.3 collective-permute-done.13
  161.5 3.0 %collective-permute-start.16 = (bf16[16,1024]{1,0:T(8,128)(2,1)S(1)}, bf16[16,1024]{1,0:T(8,128)(2,1)S(1)}, u32[]{:S(2)}, u32[]{:S(2)}) collective-permute-start(bf16[16,1024]{1,0:T(8,128)(2,1)S(1)} %get-tuple-element.74), channel_id=1, source_target_pairs={{0,32},{1,33},{2,34},{3,35},{4,36},{5,37},{6,38},{7,39},{8,40},{9,... | collective-permute-start | bytes 98312 | tf_op jit(solution)/shard_map/ppermute | solution.py:479
  167.3 5.0 %collective-permute-start.18 = (f32[8,1024]{1,0:T(8,128)S(1)}, f32[8,1024]{1,0:T(8,128)S(1)}, u32[]{:S(2)}, u32[]{:S(2)}) collective-permute-start(f32[8,1024]{1,0:T(8,128)S(1)} %get-tuple-element.76), channel_id=1, source_target_pairs={{0,1},{1,0},{2,3},{3,2},{4,5},{5,4},{6,7},{7,6},{8,9},{9,8},{10,11... | collective-permute-start | bytes 98312 | tf_op jit(solution)/shard_map/ppermute | solution.py:726
  173.9 3.9 %unpack_gradients.1 = bf16[16,32,1024]{2,1,0:T(8,128)(2,1)} custom-call(s32[8]{0:T(128)} %copy-done.9, s32[2,64]{1,0:T(2,128)} %counts_ref.11, bf16[32,32,1024]{2,1,0:T(8,128)(2,1)} %all-to-all-done.1.returned_hbm), custom_call_target="tpu_custom_call" | custom-call | flops 2000000000 | bytes 2000000 | tf_op jit(solution)/shard_map/unpack_gradients/pallas_call | solution.py:391
  (79 shorter events, 14.8 us)
Async XLA Ops:
  11.7 12.2 %copy-start.14 = (bf16[1,1,128,2048]{3,2,1,0:T(8,128)(2,1)S(1)}, bf16[1,1,128,2048]{3,2,1,0:T(8,128)(2,1)}, u32[]{:S(2)}) copy-start(bf16[1,1,128,2048]{3,2,1,0:T(8,128)(2,1)} %param.19) | copy-start | bytes 1572868
  11.7 12.4 %copy-start.17 = (bf16[1,1,128,2048]{3,2,1,0:T(8,128)(2,1)S(1)}, bf16[1,1,128,2048]{3,2,1,0:T(8,128)(2,1)}, u32[]{:S(2)}) copy-start(bf16[1,1,128,2048]{3,2,1,0:T(8,128)(2,1)} %param.25) | copy-start | bytes 1572868
  11.7 16.5 %copy-start.19 = (f32[2048]{0:T(1024)S(1)}, f32[2048]{0:T(1024)}, u32[]{:S(2)}) copy-start(f32[2048]{0:T(1024)} %param.21) | copy-start | bytes 24580
  11.7 39.5 %all-to-all-start = ((bf16[32,32,1024]{2,1,0:T(8,128)(2,1)}), bf16[32,32,1024]{2,1,0:T(8,128)(2,1)S(1)}, u32[]{:S(2)}, u32[]{:S(2)}) async-start(bf16[32,32,1024]{2,1,0:T(8,128)(2,1)} %compress_windows.1), calls=%async_computation | async-start | bytes 4194304 | tf_op jit(solution)/shard_map/all_to_all | solution.py:669
  24.1 30.4 %copy-start.8 = (s32[8]{0:T(128)S(1)}, s32[8]{0:T(128)}, u32[]{:S(2)}) copy-start(s32[8]{0:T(128)} %fusion.22.place_ref) | copy-start | bytes 100
  28.3 29.6 %copy-start.10 = (s32[2,64]{1,0:T(2,128)S(1)}, s32[2,64]{1,0:T(2,128)}, u32[]{:S(2)}) copy-start(s32[2,64]{1,0:T(2,128)} %counts_ref.11) | copy-start | bytes 1540
  29.1 37.4 %copy-start.6 = (bf16[128,1024]{1,0:T(8,128)(2,1)}, bf16[128,1024]{1,0:T(8,128)(2,1)S(1)}, u32[]{:S(2)}) copy-start(bf16[128,1024]{1,0:T(8,128)(2,1)S(1)} %fusion.3.q_own) | copy-start | bytes 786436
  51.2 6.7 %collective-permute-start.2 = (bf16[32,32,1024]{2,1,0:T(8,128)(2,1)S(1)}, bf16[32,32,1024]{2,1,0:T(8,128)(2,1)S(1)}, u32[]{:S(2)}, u32[]{:S(2)}) collective-permute-start(bf16[32,32,1024]{2,1,0:T(8,128)(2,1)S(1)} %all-to-all-done.arrived_ref), channel_id=1, source_target_pairs={{0,1},{1,0},{2,3},{3,2},{4,5},{5,4},{6,7},{7,6},{8,9},{9,8},{10,11... | collective-permute-start | bytes 6291464 | tf_op jit(solution)/shard_map/ppermute | solution.py:687
  53.0 11.2 %collective-permute-start = (bf16[128,1024]{1,0:T(8,128)(2,1)S(1)}, bf16[128,1024]{1,0:T(8,128)(2,1)S(1)}, u32[]{:S(2)}, u32[]{:S(2)}) collective-permute-start(bf16[128,1024]{1,0:T(8,128)(2,1)S(1)} %fusion.3.q_own), channel_id=1, source_target_pairs={{0,64},{64,0},{1,65},{65,1},{2,66},{66,2},{3,67},{67,3},{4,68},{68... | collective-permute-start | bytes 786440 | tf_op jit(solution)/shard_map/ppermute | solution.py:682
  53.8 12.7 %collective-permute-start.1 = (bf16[128,1024]{1,0:T(8,128)(2,1)S(1)}, bf16[128,1024]{1,0:T(8,128)(2,1)S(1)}, u32[]{:S(2)}, u32[]{:S(2)}) collective-permute-start(bf16[128,1024]{1,0:T(8,128)(2,1)S(1)} %convolution_convert_fusion.dc_own), channel_id=1, source_target_pairs={{0,64},{64,0},{1,65},{65,1},{2,66},{66,2},{3,67},{67,3},{4,68},{68... | collective-permute-start | bytes 786440 | tf_op jit(solution)/shard_map/ppermute | solution.py:683
  57.8 45.3 %copy-start.9 = (s32[8]{0:T(128)}, s32[8]{0:T(128)S(1)}, u32[]{:S(2)}) copy-start(s32[8]{0:T(128)S(1)} %touched.1.place_ref) | copy-start | bytes 100
  71.3 4.1 %collective-permute-start.3 = (f32[3,8,512]{2,1,0:T(8,128)S(1)}, f32[3,8,512]{2,1,0:T(8,128)S(1)}, u32[]{:S(2)}, u32[]{:S(2)}) collective-permute-start(f32[3,8,512]{2,1,0:T(8,128)S(1)} %attention_stats.1.stats_ref), channel_id=1, source_target_pairs={{0,64},{64,0},{1,65},{65,1},{2,66},{66,2},{3,67},{67,3},{4,68},{68... | collective-permute-start | bytes 147464 | tf_op jit(solution)/shard_map/ppermute | solution.py:692
  91.6 22.8 %collective-permute-start.4 = (bf16[4,256,1024]{2,1,0:T(8,128)(2,1)}, bf16[4,256,1024]{2,1,0:T(8,128)(2,1)S(1)}, u32[]{:S(2)}, u32[]{:S(2)}) collective-permute-start(bf16[4,256,1024]{2,1,0:T(8,128)(2,1)} %given_term.1), channel_id=1, source_target_pairs={{0,1},{1,0},{2,3},{3,2},{4,5},{5,4},{6,7},{7,6},{8,9},{9,8},{10,11... | collective-permute-start | bytes 6291464 | tf_op jit(solution)/shard_map/ppermute | solution.py:703
  92.7 5.9 %collective-permute-start.9 = (bf16[20,32,1024]{2,1,0:T(8,128)(2,1)S(1)}, bf16[20,32,1024]{2,1,0:T(8,128)(2,1)S(1)}, u32[]{:S(2)}, u32[]{:S(2)}) collective-permute-start(bf16[20,32,1024]{2,1,0:T(8,128)(2,1)S(1)} %bitcast.32), channel_id=1, source_target_pairs={{0,1},{1,0},{2,3},{3,2},{4,5},{5,4},{6,7},{7,6},{8,9},{9,8},{10,11... | collective-permute-start | bytes 3932168 | tf_op jit(solution)/shard_map/ppermute | solution.py:701
  102.1 16.8 %collective-permute-start.11 = (bf16[128,1024]{1,0:T(8,128)(2,1)}, bf16[128,1024]{1,0:T(8,128)(2,1)}, u32[]{:S(2)}, u32[]{:S(2)}) collective-permute-start(bf16[128,1024]{1,0:T(8,128)(2,1)} %get-tuple-element.62), channel_id=1, source_target_pairs={{0,64},{64,0},{1,65},{65,1},{2,66},{66,2},{3,67},{67,3},{4,68},{68... | collective-permute-start | bytes 786440 | tf_op jit(solution)/shard_map/ppermute | solution.py:715
  106.9 51.2 %collective-permute-start.10 = (bf16[128,1024]{1,0:T(8,128)(2,1)}, bf16[128,1024]{1,0:T(8,128)(2,1)S(1)}, u32[]{:S(2)}, u32[]{:S(2)}) collective-permute-start(bf16[128,1024]{1,0:T(8,128)(2,1)} %get-tuple-element.60), channel_id=1, source_target_pairs={{0,64},{64,0},{1,65},{65,1},{2,66},{66,2},{3,67},{67,3},{4,68},{68... | collective-permute-start | bytes 786440 | tf_op jit(solution)/shard_map/ppermute | solution.py:711
  107.4 66.5 %all-to-all-start.1 = ((bf16[32,32,1024]{2,1,0:T(8,128)(2,1)}), bf16[32,32,1024]{2,1,0:T(8,128)(2,1)}, u32[]{:S(2)}, u32[]{:S(2)}) async-start(bf16[32,32,1024]{2,1,0:T(8,128)(2,1)} %copy-done.5), calls=%async_computation.1 | async-start | bytes 4194304 | tf_op jit(solution)/shard_map/all_to_all | solution.py:708
  116.1 27.4 %copy-start.2 = (bf16[4,256,1024]{2,1,0:T(8,128)(2,1)S(1)}, bf16[4,256,1024]{2,1,0:T(8,128)(2,1)}, u32[]{:S(2)}) copy-start(bf16[4,256,1024]{2,1,0:T(8,128)(2,1)} %copy-done) | copy-start | bytes 6291460
  116.1 27.4 %collective-permute-start.5 = (bf16[128,1024]{1,0:T(8,128)(2,1)S(1)}, bf16[128,1024]{1,0:T(8,128)(2,1)S(1)}, u32[]{:S(2)}, u32[]{:S(2)}) collective-permute-start(bf16[128,1024]{1,0:T(8,128)(2,1)S(1)} %get-tuple-element.51), channel_id=1, source_target_pairs={{0,8},{1,3},{2,10},{3,5},{4,12},{5,7},{6,14},{7,1},{8,16},{9,11},{... | collective-permute-start | bytes 786440 | tf_op jit(solution)/shard_map/ppermute | solution.py:479
  117.3 26.2 %collective-permute-start.6 = (bf16[128,1024]{1,0:T(8,128)(2,1)S(1)}, bf16[128,1024]{1,0:T(8,128)(2,1)S(1)}, u32[]{:S(2)}, u32[]{:S(2)}) collective-permute-start(bf16[128,1024]{1,0:T(8,128)(2,1)S(1)} %get-tuple-element.52), channel_id=1, source_target_pairs={{0,24},{1,7},{2,26},{3,1},{4,28},{5,3},{6,30},{7,5},{8,0},{9,15},{... | collective-permute-start | bytes 786440 | tf_op jit(solution)/shard_map/ppermute | solution.py:479
  118.8 27.7 %copy-start.16 = (bf16[1,1,128,2048]{3,2,1,0:T(8,128)(2,1)S(1)}, bf16[1,1,128,2048]{3,2,1,0:T(8,128)(2,1)}, u32[]{:S(2)}) copy-start(bf16[1,1,128,2048]{3,2,1,0:T(8,128)(2,1)} %param.19) | copy-start | bytes 1572868
  118.8 27.7 %copy-start.18 = (bf16[1,1,128,2048]{3,2,1,0:T(8,128)(2,1)S(1)}, bf16[1,1,128,2048]{3,2,1,0:T(8,128)(2,1)}, u32[]{:S(2)}) copy-start(bf16[1,1,128,2048]{3,2,1,0:T(8,128)(2,1)} %param.25) | copy-start | bytes 1572868
  143.8 14.3 %copy-start.13 = (bf16[1024,2048]{1,0:T(8,128)(2,1)S(1)}, bf16[1024,2048]{1,0:T(8,128)(2,1)}, u32[]{:S(2)}) copy-start(bf16[1024,2048]{1,0:T(8,128)(2,1)} %param.24) | copy-start | bytes 12582916
  143.8 9.6 %collective-permute-start.7 = (bf16[256,1024]{1,0:T(8,128)(2,1)S(1)}, bf16[256,1024]{1,0:T(8,128)(2,1)S(1)}, u32[]{:S(2)}, u32[]{:S(2)}) collective-permute-start(bf16[256,1024]{1,0:T(8,128)(2,1)S(1)} %get-tuple-element.53), channel_id=1, source_target_pairs={{0,8},{1,3},{2,10},{3,5},{4,12},{5,7},{6,14},{7,1},{8,16},{9,11},{... | collective-permute-start | bytes 1572872 | tf_op jit(solution)/shard_map/ppermute | solution.py:479
  143.9 9.5 %collective-permute-start.8 = (bf16[256,1024]{1,0:T(8,128)(2,1)S(1)}, bf16[256,1024]{1,0:T(8,128)(2,1)S(1)}, u32[]{:S(2)}, u32[]{:S(2)}) collective-permute-start(bf16[256,1024]{1,0:T(8,128)(2,1)S(1)} %get-tuple-element.54), channel_id=1, source_target_pairs={{0,24},{1,7},{2,26},{3,1},{4,28},{5,3},{6,30},{7,5},{8,0},{9,15},{... | collective-permute-start | bytes 1572872 | tf_op jit(solution)/shard_map/ppermute | solution.py:479
  153.7 6.1 %collective-permute-start.12 = (bf16[64,1024]{1,0:T(8,128)(2,1)S(1)}, bf16[64,1024]{1,0:T(8,128)(2,1)S(1)}, u32[]{:S(2)}, u32[]{:S(2)}) collective-permute-start(bf16[64,1024]{1,0:T(8,128)(2,1)S(1)} %get-tuple-element.67), channel_id=1, source_target_pairs={{0,2},{1,9},{2,4},{3,11},{4,6},{5,13},{6,0},{7,15},{8,10},{9,17},{... | collective-permute-start | bytes 393224 | tf_op jit(solution)/shard_map/ppermute | solution.py:479
  154.1 6.9 %collective-permute-start.13 = (bf16[64,1024]{1,0:T(8,128)(2,1)S(1)}, bf16[64,1024]{1,0:T(8,128)(2,1)S(1)}, u32[]{:S(2)}, u32[]{:S(2)}) collective-permute-start(bf16[64,1024]{1,0:T(8,128)(2,1)S(1)} %get-tuple-element.68), channel_id=1, source_target_pairs={{0,4},{1,17},{2,6},{3,19},{4,0},{5,21},{6,2},{7,23},{8,12},{9,25},... | collective-permute-start | bytes 393224 | tf_op jit(solution)/shard_map/ppermute | solution.py:479
  157.2 3.8 %collective-permute-start.14 = (bf16[64,1024]{1,0:T(8,128)(2,1)S(1)}, bf16[64,1024]{1,0:T(8,128)(2,1)S(1)}, u32[]{:S(2)}, u32[]{:S(2)}) collective-permute-start(bf16[64,1024]{1,0:T(8,128)(2,1)S(1)} %get-tuple-element.69), channel_id=1, source_target_pairs={{0,6},{1,25},{2,0},{3,27},{4,2},{5,29},{6,4},{7,31},{8,14},{9,1},{... | collective-permute-start | bytes 393224 | tf_op jit(solution)/shard_map/ppermute | solution.py:479
  161.1 4.5 %collective-permute-start.15 = (bf16[16,1024]{1,0:T(8,128)(2,1)S(1)}, bf16[16,1024]{1,0:T(8,128)(2,1)S(1)}, u32[]{:S(2)}, u32[]{:S(2)}) collective-permute-start(bf16[16,1024]{1,0:T(8,128)(2,1)S(1)} %get-tuple-element.72), channel_id=1, source_target_pairs={{0,64},{1,65},{2,66},{3,67},{4,68},{5,69},{6,70},{7,71},{8,72},{9,... | collective-permute-start | bytes 98312 | tf_op jit(solution)/shard_map/ppermute | solution.py:479
  161.5 4.6 %collective-permute-start.16 = (bf16[16,1024]{1,0:T(8,128)(2,1)S(1)}, bf16[16,1024]{1,0:T(8,128)(2,1)S(1)}, u32[]{:S(2)}, u32[]{:S(2)}) collective-permute-start(bf16[16,1024]{1,0:T(8,128)(2,1)S(1)} %get-tuple-element.74), channel_id=1, source_target_pairs={{0,32},{1,33},{2,34},{3,35},{4,36},{5,37},{6,38},{7,39},{8,40},{9,... | collective-permute-start | bytes 98312 | tf_op jit(solution)/shard_map/ppermute | solution.py:479
  164.5 2.8 %collective-permute-start.17 = (bf16[16,1024]{1,0:T(8,128)(2,1)S(1)}, bf16[16,1024]{1,0:T(8,128)(2,1)S(1)}, u32[]{:S(2)}, u32[]{:S(2)}) collective-permute-start(bf16[16,1024]{1,0:T(8,128)(2,1)S(1)} %get-tuple-element.73), channel_id=1, source_target_pairs={{0,96},{1,97},{2,98},{3,99},{4,100},{5,101},{6,102},{7,103},{8,104... | collective-permute-start | bytes 98312 | tf_op jit(solution)/shard_map/ppermute | solution.py:479
  167.3 5.9 %collective-permute-start.18 = (f32[8,1024]{1,0:T(8,128)S(1)}, f32[8,1024]{1,0:T(8,128)S(1)}, u32[]{:S(2)}, u32[]{:S(2)}) collective-permute-start(f32[8,1024]{1,0:T(8,128)S(1)} %get-tuple-element.76), channel_id=1, source_target_pairs={{0,1},{1,0},{2,3},{3,2},{4,5},{5,4},{6,7},{7,6},{8,9},{9,8},{10,11... | collective-permute-start | bytes 98312 | tf_op jit(solution)/shard_map/ppermute | solution.py:726
  (9 other events, 29.5 us)
